TPU v7x, 256 devices: a whole 4x4x8 slice. The times are simulated.
256 devices in a mesh: group: 32 (over x, z), member: 8 (over y, core).
Axes of the slice: x: 4, y: 4, z: 8, core: 2. Of those that a mesh axis runs over, the one named last changes fastest.
Arguments:
- particles: float32 [8, 524288], P(None, ('group', 'member')), may hold values from 0 to 20, as said below
- new_slot: int32 [4096], P(('group', 'member')), may hold values from 0 to 4095, as said below
- neighbours: int32 [4096, 6], P(('group', 'member')), may hold values from 0 to 23, as said below
- ghosts: int32 [256, 2], P(('group', 'member')), may hold values from 0 to 4, as said below
Outputs:
- energy: float32 [524288], P(('group', 'member'))
- density: float32 [524288], P(('group', 'member'))
Inputs may be any that keep to these rules, and one draw needn't show every extreme that they name: A permutation of 0 to 4095. Tile t goes to segment new_slot[t] // 16, where segment number = group index * 8 + member index; a tile keeps its member index. Every segment receives 16 tiles, no segment sends more than 2 tiles to one segment, and some segment sends exactly 2 tiles to one segment. `ghosts`: row d holds the number of tiles that segment d takes from the end of segment d - 1 and from the start of segment d + 1. Both are at least 1 except the first segment's left count and the last segment's right count, which are 0; some segment takes exactly 4 tiles from its left neighbour. `neighbours`: for moved tile s of segment d, entries count along the extended range: the last ghosts[d, 0] tiles of segment d - 1, then the 16 tiles of segment d, then the first ghosts[d, 1] tiles of segment d + 1; every entry lies inside that range, entry 0 is the tile itself, and entries may repeat. `particles`: Rows: positions within 0 to 1, masses within 0.5 / 768 to 2 / 768, smoothing lengths within 0.3 to 0.5, initial energies within 0.5 to 4, opacities within 0.05 to 20, heating within 0 to 1.
All inputs are finite; a program needn't handle non-finite values.
Results may differ from a plain program's by a relative error of at most 0.00014.
Values sent between devices are 32-bit elements; how exact they have to be, the bound alone decides.
No kernel may reach another device: no remote copies, remote signals or barrier semaphores. Data moves between devices by JAX's collectives and lax.ppermute only.
A program may use at most 64 MiB of HBM per device.

v0:
```python
import math

import jax
import jax.numpy as jnp
from jax import lax
from jax.sharding import PartitionSpec as P

TILE = 128
GMAX = 4
SWEEPS = 3


KERNEL_NORM = 21.0 / (16.0 * math.pi)
TIME_STEP = 0.05


def shifted(value, axis, steps):
    count = lax.axis_size(axis)
    first, last = (max(0, -steps), min(count, count - steps))
    return lax.ppermute(value, axis, [(source, source + steps) for source in range(first, last)])


def geometry(own_fields, near_fields):
    offsets = near_fields[0:3, :, :, None, :] - own_fields[0:3, :, None, :, None]
    distance = jnp.sqrt(jnp.sum(offsets * offsets, axis=0))
    return (offsets, distance)


def pair_forces(own_fields, near_fields, distance):
    mean_smooth = 0.5 * (own_fields[4][:, None, :, None] + near_fields[4][:, :, None, :])
    falloff = jax.nn.relu(1.0 - 0.5 * distance / mean_smooth)
    return 5.0 * KERNEL_NORM * falloff**3 / mean_smooth**5


def density_kernel(own_items, near_items):
    own_fields = own_items[0]
    near_fields = near_items[0]
    offsets, distance = geometry(own_fields, near_fields)
    smooth = own_fields[4][:, None, :, None]
    scaled = distance / smooth
    falloff = jax.nn.relu(1.0 - 0.5 * scaled)
    weight = KERNEL_NORM * falloff**4 * (2.0 * scaled + 1.0) / smooth**3
    return jnp.sum(near_fields[3][:, :, None, :] * weight, axis=(1, 3))


def limiter_kernel(own_items, near_items):
    own_fields, own_density, own_energy = own_items
    near_fields, near_density, near_energy = near_items
    offsets, distance = geometry(own_fields, near_fields)
    forces = pair_forces(own_fields, near_fields, distance)
    volume = near_fields[3] / near_density[0]
    change = near_energy[0][:, :, None, :] - own_energy[0][:, None, :, None]
    scaled = volume[:, :, None, :] * forces * change
    gradient = jnp.sum(scaled[None] * offsets, axis=(2, 4))
    stream_ratio = jnp.sqrt(jnp.sum(gradient * gradient, axis=0)) / (
        own_fields[6] * own_density[0] * own_energy[0]
    )
    limiter = (2.0 + stream_ratio) / (6.0 + 3.0 * stream_ratio + stream_ratio * stream_ratio)
    return limiter / (own_fields[6] * own_density[0])


def jacobi_kernel(own_items, near_items):
    own_fields, own_density, own_diffusion = own_items
    near_fields, near_density, near_diffusion, near_energy = near_items
    offsets, distance = geometry(own_fields, near_fields)
    forces = pair_forces(own_fields, near_fields, distance)
    coupling = (
        near_fields[3][:, :, None, :]
        * (own_diffusion[0][:, None, :, None] + near_diffusion[0][:, :, None, :])
        * forces
    )
    coupling = coupling / (own_density[0][:, None, :, None] * near_density[0][:, :, None, :])
    rate_sum = jnp.sum(coupling, axis=(1, 3))
    inflow = jnp.sum(coupling * near_energy[0][:, :, None, :], axis=(1, 3))
    return (own_fields[5] + TIME_STEP * own_fields[7] + TIME_STEP * inflow) / (
        1.0 + TIME_STEP * rate_sum
    )


def tile_blocks(kernel, own_items, ext_items, near_index):
    per_block = 4
    block_count = near_index.shape[0] // per_block

    def one_block(block_id):
        first_tile = block_id * per_block
        own_part = tuple(
            (lax.dynamic_slice_in_dim(values, first_tile, per_block, 1) for values in own_items)
        )
        near_rows = lax.dynamic_slice_in_dim(near_index, first_tile, per_block, 0)
        near_part = tuple((jnp.take(values, near_rows, axis=1) for values in ext_items))
        return kernel(own_part, near_part)

    blocks = lax.map(one_block, jnp.arange(block_count, dtype=jnp.int32))
    return blocks.reshape(1, near_index.shape[0], blocks.shape[-1])


def with_ghosts(values, depth_tiles):
    tail_rows = values[:, values.shape[1] - depth_tiles :]
    head_rows = values[:, :depth_tiles]
    from_left = shifted(tail_rows, ("group", "member"), 1)
    from_right = shifted(head_rows, ("group", "member"), -1)
    return jnp.concatenate([from_left, values, from_right], axis=1)


def local(particles, new_slot, neighbours, ghosts):
    tile_count = new_slot.shape[0]
    local_tiles = particles.reshape(8, tile_count, TILE)
    groups = lax.axis_size("group")
    members = lax.axis_size("member")
    capacity = max(2, (2 * tile_count + groups - 1) // groups)
    target = new_slot // (tile_count * members)
    in_group = (target[:, None] == jnp.arange(groups, dtype=jnp.int32)[None, :]).astype(jnp.int32)
    order_in = jnp.sum(jnp.cumsum(in_group, axis=0) * in_group, axis=1) - 1
    bucket = target * capacity + order_in
    placement = bucket[:, None] == jnp.arange(groups * capacity, dtype=jnp.int32)[None, :]
    outgoing = jnp.einsum(
        "ts,kti->ski", placement.astype(jnp.float32), local_tiles, precision=lax.Precision.HIGHEST
    )
    slot_label = new_slot % tile_count + 1
    out_slots = jnp.sum(placement.astype(jnp.int32) * slot_label[:, None], axis=0)
    received, got_slots = (
        lax.all_to_all(outgoing, "group", split_axis=0, concat_axis=0, tiled=True),
        lax.all_to_all(out_slots, "group", split_axis=0, concat_axis=0, tiled=True),
    )
    choose = (got_slots[:, None] - 1 == jnp.arange(tile_count, dtype=jnp.int32)[None, :]).astype(
        jnp.float32
    )
    arranged = jnp.einsum("st,ski->kti", choose, received, precision=lax.Precision.HIGHEST)
    left_count = ghosts[0, 0]
    near_index = neighbours + (GMAX - left_count)
    statics = with_ghosts(arranged[0:6], GMAX)
    density = tile_blocks(density_kernel, (arranged,), (statics,), near_index)
    density_ext = with_ghosts(density, GMAX)
    energy = arranged[5:6]
    energy_ext = statics[5:6]
    for sweep_step in range(SWEEPS):
        if sweep_step > 0:
            energy_ext = with_ghosts(energy, GMAX)
        diffusion = tile_blocks(
            limiter_kernel,
            (arranged, density, energy),
            (statics, density_ext, energy_ext),
            near_index,
        )
        diffusion_ext = with_ghosts(diffusion, GMAX)
        energy = tile_blocks(
            jacobi_kernel,
            (arranged, density, diffusion),
            (statics, density_ext, diffusion_ext, energy_ext),
            near_index,
        )
    return (energy.reshape(-1), density.reshape(-1))


def solution(mesh):
    in_specs = (
        P(None, ("group", "member")),
        P(("group", "member")),
        P(("group", "member"), None),
        P(("group", "member"), None),
    )
    out_specs = (P(("group", "member")), P(("group", "member")))
    return jax.shard_map(local, mesh=mesh, in_specs=in_specs, out_specs=out_specs, check_vma=False)
```

profile of v0, /device:TPU:2, one launch (start us, length us, event | category | flops | bytes accessed | tf_op | source)
XLA Modules:
  0.0 284.3 jit_solution(9606929900134054529)
XLA Ops:
  2.4 11.6 %all-to-all-start.1 = ((s32[32,2,1]{1,2,0:T(1,128)}), s32[32,2,1]{1,2,0:T(1,128)S(1)}, u32[]{:S(2)}, u32[]{:S(2)}) async-start(s32[32,2,1]{1,2,0:T(1,128)} %bitcast.89), calls=%async_computation.1 | async-start | bytes 32768 | tf_op jit(solution)/shard_map/all_to_all | solution.py:123
  15.3 7.4 %all-to-all-done.1 = s32[32,2,1]{1,2,0:T(1,128)S(1)} async-done(((s32[32,2,1]{1,2,0:T(1,128)}), s32[32,2,1]{1,2,0:T(1,128)S(1)}, u32[]{:S(2)}, u32[]{:S(2)}) %all-to-all-start.1) | async-done | bytes 288 | tf_op jit(solution)/shard_map/all_to_all | solution.py:123
  22.7 5.0 %all-to-all-start = ((f32[64,8,128]{2,1,0:T(8,128)}), f32[64,8,128]{2,1,0:T(8,128)S(1)}, u32[]{:S(2)}, u32[]{:S(2)}) async-start(f32[64,8,128]{2,1,0:T(8,128)} %copy.49), calls=%async_computation | async-start | bytes 524288 | tf_op jit(solution)/shard_map/all_to_all | solution.py:122
  29.3 8.6 %all-to-all-done = f32[64,8,128]{2,1,0:T(8,128)S(1)} async-done(((f32[64,8,128]{2,1,0:T(8,128)}), f32[64,8,128]{2,1,0:T(8,128)S(1)}, u32[]{:S(2)}, u32[]{:S(2)}) %all-to-all-start) | async-done | bytes 262176 | tf_op jit(solution)/shard_map/all_to_all | solution.py:122
  40.0 7.9 %collective-permute-start.1 = (f32[6,4,128]{2,1,0:T(4,128)S(1)}, f32[6,4,128]{2,1,0:T(4,128)S(1)}, u32[]{:S(2)}, u32[]{:S(2)}) collective-permute-start(f32[6,4,128]{2,1,0:T(4,128)S(1)} %get-tuple-element.783), channel_id=1, source_target_pairs={{1,0},{2,1},{3,2},{4,3},{5,4},{6,5},{7,6},{8,7},{9,8},{10,9},{11,1... | collective-permute-start | bytes 36872 | tf_op jit(solution)/shard_map/ppermute | solution.py:20
  49.4 15.3 %while.70 = (s32[]{:T(128)}, f32[4,4,128]{2,1,0:T(4,128)S(1)}, s32[4]{0:T(128)S(1)}, s32[16,6]{1,0:T(8,128)S(1)}, f32[6,24,128]{2,0,1:T(8,128)S(1)}, /*index=5*/...) while((s32[]{:T(128)}, f32[4,4,128]{2,1,0:T(4,128)S(1)}, ...), condition=%wide.region_6.8_spmd, body=%wide.region_3.7_spmd.sunk | while | flops 8277655 | bytes 3627839 | solution.py:93
  64.7 1.9 collective-permute-start.2
  66.6 7.9 %collective-permute-start.3 = (f32[1,4,128]{2,1,0:T(4,128)S(1)}, f32[1,4,128]{2,1,0:T(4,128)S(1)}, u32[]{:S(2)}, u32[]{:S(2)}) collective-permute-start(f32[1,4,128]{2,1,0:T(4,128)S(1)} %get-tuple-element.795), channel_id=1, source_target_pairs={{1,0},{2,1},{3,2},{4,3},{5,4},{6,5},{7,6},{8,7},{9,8},{10,9},{11,1... | collective-permute-start | bytes 6152 | tf_op jit(solution)/shard_map/ppermute | solution.py:20
  75.8 24.6 %while.71 = (s32[]{:T(128)}, f32[4,4,128]{2,1,0:T(4,128)S(1)}, s32[4]{0:T(128)S(1)}, s32[16,6]{1,0:T(8,128)S(1)}, f32[6,24,128]{2,0,1:T(8,128)S(1)}, /*index=5*/...) while((s32[]{:T(128)}, f32[4,4,128]{2,1,0:T(4,128)S(1)}, ...), condition=%wide.region_11.14_spmd, body=%wide.region_7.13_spmd.sunk | while | flops 13011096 | bytes 7021651 | solution.py:93
  102.4 7.9 %collective-permute-start.5 = (f32[1,4,128]{2,1,0:T(4,128)S(1)}, f32[1,4,128]{2,1,0:T(4,128)S(1)}, u32[]{:S(2)}, u32[]{:S(2)}) collective-permute-start(f32[1,4,128]{2,1,0:T(4,128)S(1)} %get-tuple-element.793), channel_id=1, source_target_pairs={{1,0},{2,1},{3,2},{4,3},{5,4},{6,5},{7,6},{8,7},{9,8},{10,9},{11,1... | collective-permute-start | bytes 6152 | tf_op jit(solution)/shard_map/ppermute | solution.py:20
  111.6 26.1 %while.72 = (s32[]{:T(128)}, f32[4,4,128]{2,1,0:T(4,128)S(1)}, s32[4]{0:T(128)S(1)}, f32[8,16,128]{2,1,0:T(8,128)S(1)}, s32[16,6]{1,0:T(8,128)S(1)}, /*index=5*/...) while((s32[]{:T(128)}, f32[4,4,128]{2,1,0:T(4,128)S(1)}, ...), condition=%wide.region_16.19_spmd, body=%wide.region_12.18_spmd.sunk | while | flops 11434649 | bytes 3939543 | solution.py:93
  116.0 2.0 multiply_reduce_fusion.26
  122.6 2.0 multiply_reduce_fusion.26
  129.1 2.0 multiply_reduce_fusion.26
  135.6 2.0 multiply_reduce_fusion.26
  137.7 1.9 collective-permute-start.6
  139.6 8.0 %collective-permute-start.7 = (f32[1,4,128]{2,1,0:T(4,128)S(1)}, f32[1,4,128]{2,1,0:T(4,128)S(1)}, u32[]{:S(2)}, u32[]{:S(2)}) collective-permute-start(f32[1,4,128]{2,1,0:T(4,128)S(1)} %get-tuple-element.791), channel_id=1, source_target_pairs={{1,0},{2,1},{3,2},{4,3},{5,4},{6,5},{7,6},{8,7},{9,8},{10,9},{11,1... | collective-permute-start | bytes 6152 | tf_op jit(solution)/shard_map/ppermute | solution.py:20
  148.8 24.6 %while.73 = (s32[]{:T(128)}, f32[4,4,128]{2,1,0:T(4,128)S(1)}, s32[4]{0:T(128)S(1)}, s32[16,6]{1,0:T(8,128)S(1)}, f32[6,24,128]{2,0,1:T(8,128)S(1)}, /*index=5*/...) while((s32[]{:T(128)}, f32[4,4,128]{2,1,0:T(4,128)S(1)}, ...), condition=%wide.region_21.24_spmd, body=%wide.region_17.23_spmd.sunk | while | flops 13011096 | bytes 7021651 | solution.py:93
  175.4 7.9 %collective-permute-start.9 = (f32[1,4,128]{2,1,0:T(4,128)S(1)}, f32[1,4,128]{2,1,0:T(4,128)S(1)}, u32[]{:S(2)}, u32[]{:S(2)}) collective-permute-start(f32[1,4,128]{2,1,0:T(4,128)S(1)} %get-tuple-element.789), channel_id=1, source_target_pairs={{1,0},{2,1},{3,2},{4,3},{5,4},{6,5},{7,6},{8,7},{9,8},{10,9},{11,1... | collective-permute-start | bytes 6152 | tf_op jit(solution)/shard_map/ppermute | solution.py:20
  184.5 26.1 %while.74 = (s32[]{:T(128)}, f32[4,4,128]{2,1,0:T(4,128)S(1)}, s32[4]{0:T(128)S(1)}, f32[8,16,128]{2,1,0:T(8,128)S(1)}, s32[16,6]{1,0:T(8,128)S(1)}, /*index=5*/...) while((s32[]{:T(128)}, f32[4,4,128]{2,1,0:T(4,128)S(1)}, ...), condition=%wide.region_26.29_spmd, body=%wide.region_22.28_spmd.sunk | while | flops 11434649 | bytes 3939543 | solution.py:93
  189.0 2.0 multiply_reduce_fusion.29
  195.5 2.0 multiply_reduce_fusion.29
  202.1 2.0 multiply_reduce_fusion.29
  208.6 2.0 multiply_reduce_fusion.29
  212.6 7.9 %collective-permute-start.11 = (f32[1,4,128]{2,1,0:T(4,128)S(1)}, f32[1,4,128]{2,1,0:T(4,128)S(1)}, u32[]{:S(2)}, u32[]{:S(2)}) collective-permute-start(f32[1,4,128]{2,1,0:T(4,128)S(1)} %get-tuple-element.787), channel_id=1, source_target_pairs={{1,0},{2,1},{3,2},{4,3},{5,4},{6,5},{7,6},{8,7},{9,8},{10,9},{11,1... | collective-permute-start | bytes 6152 | tf_op jit(solution)/shard_map/ppermute | solution.py:20
  221.8 24.6 %while.75 = (s32[]{:T(128)}, f32[4,4,128]{2,1,0:T(4,128)S(1)}, s32[4]{0:T(128)S(1)}, s32[16,6]{1,0:T(8,128)S(1)}, f32[6,24,128]{2,0,1:T(8,128)S(1)}, /*index=5*/...) while((s32[]{:T(128)}, f32[4,4,128]{2,1,0:T(4,128)S(1)}, ...), condition=%wide.region_31.34_spmd, body=%wide.region_27.33_spmd.sunk | while | flops 13011096 | bytes 7021651 | solution.py:93
  248.4 8.1 %collective-permute-start.13 = (f32[1,4,128]{2,1,0:T(4,128)S(1)}, f32[1,4,128]{2,1,0:T(4,128)S(1)}, u32[]{:S(2)}, u32[]{:S(2)}) collective-permute-start(f32[1,4,128]{2,1,0:T(4,128)S(1)} %get-tuple-element.785), channel_id=1, source_target_pairs={{1,0},{2,1},{3,2},{4,3},{5,4},{6,5},{7,6},{8,7},{9,8},{10,9},{11,1... | collective-permute-start | bytes 6152 | tf_op jit(solution)/shard_map/ppermute | solution.py:20
  257.5 26.1 %while.76 = (s32[]{:T(128)}, f32[4,4,128]{2,1,0:T(4,128)S(1)}, s32[4]{0:T(128)S(1)}, f32[8,16,128]{2,1,0:T(8,128)S(1)}, s32[16,6]{1,0:T(8,128)S(1)}, /*index=5*/...) while((s32[]{:T(128)}, f32[4,4,128]{2,1,0:T(4,128)S(1)}, ...), condition=%wide.region_36.39_spmd, body=%wide.region_32.38_spmd.sunk | while | flops 11434649 | bytes 3939543 | solution.py:93
  262.0 2.0 multiply_reduce_fusion.32
  268.5 2.0 multiply_reduce_fusion.32
  275.1 2.0 multiply_reduce_fusion.32
  281.6 2.0 multiply_reduce_fusion.32
  (579 shorter events, 145.7 us)
Async XLA Ops:
  0.6 13.4 %copy-start = (f32[8,2048]{1,0:T(8,128)S(1)}, f32[8,2048]{1,0:T(8,128)}, u32[]{:S(2)}) copy-start(f32[8,2048]{1,0:T(8,128)} %param.22) | copy-start | bytes 196612
  2.4 20.3 %all-to-all-start.1 = ((s32[32,2,1]{1,2,0:T(1,128)}), s32[32,2,1]{1,2,0:T(1,128)S(1)}, u32[]{:S(2)}, u32[]{:S(2)}) async-start(s32[32,2,1]{1,2,0:T(1,128)} %bitcast.89), calls=%async_computation.1 | async-start | bytes 32768 | tf_op jit(solution)/shard_map/all_to_all | solution.py:123
  22.7 15.1 %all-to-all-start = ((f32[64,8,128]{2,1,0:T(8,128)}), f32[64,8,128]{2,1,0:T(8,128)S(1)}, u32[]{:S(2)}, u32[]{:S(2)}) async-start(f32[64,8,128]{2,1,0:T(8,128)} %copy.49), calls=%async_computation | async-start | bytes 524288 | tf_op jit(solution)/shard_map/all_to_all | solution.py:122
  38.1 9.8 %collective-permute-start = (f32[6,4,128]{2,1,0:T(4,128)S(1)}, f32[6,4,128]{2,1,0:T(4,128)S(1)}, u32[]{:S(2)}, u32[]{:S(2)}) collective-permute-start(f32[6,4,128]{2,1,0:T(4,128)S(1)} %get-tuple-element.782), channel_id=1, source_target_pairs={{0,1},{1,2},{2,3},{3,4},{4,5},{5,6},{6,7},{7,8},{8,9},{9,10},{10,1... | collective-permute-start | bytes 36872 | tf_op jit(solution)/shard_map/ppermute | solution.py:20
  40.0 9.3 %collective-permute-start.1 = (f32[6,4,128]{2,1,0:T(4,128)S(1)}, f32[6,4,128]{2,1,0:T(4,128)S(1)}, u32[]{:S(2)}, u32[]{:S(2)}) collective-permute-start(f32[6,4,128]{2,1,0:T(4,128)S(1)} %get-tuple-element.783), channel_id=1, source_target_pairs={{1,0},{2,1},{3,2},{4,3},{5,4},{6,5},{7,6},{8,7},{9,8},{10,9},{11,1... | collective-permute-start | bytes 36872 | tf_op jit(solution)/shard_map/ppermute | solution.py:20
  64.7 9.8 %collective-permute-start.2 = (f32[1,4,128]{2,1,0:T(4,128)S(1)}, f32[1,4,128]{2,1,0:T(4,128)S(1)}, u32[]{:S(2)}, u32[]{:S(2)}) collective-permute-start(f32[1,4,128]{2,1,0:T(4,128)S(1)} %get-tuple-element.794), channel_id=1, source_target_pairs={{0,1},{1,2},{2,3},{3,4},{4,5},{5,6},{6,7},{7,8},{8,9},{9,10},{10,1... | collective-permute-start | bytes 6152 | tf_op jit(solution)/shard_map/ppermute | solution.py:20
  66.6 9.2 %collective-permute-start.3 = (f32[1,4,128]{2,1,0:T(4,128)S(1)}, f32[1,4,128]{2,1,0:T(4,128)S(1)}, u32[]{:S(2)}, u32[]{:S(2)}) collective-permute-start(f32[1,4,128]{2,1,0:T(4,128)S(1)} %get-tuple-element.795), channel_id=1, source_target_pairs={{1,0},{2,1},{3,2},{4,3},{5,4},{6,5},{7,6},{8,7},{9,8},{10,9},{11,1... | collective-permute-start | bytes 6152 | tf_op jit(solution)/shard_map/ppermute | solution.py:20
  100.5 9.8 %collective-permute-start.4 = (f32[1,4,128]{2,1,0:T(4,128)S(1)}, f32[1,4,128]{2,1,0:T(4,128)S(1)}, u32[]{:S(2)}, u32[]{:S(2)}) collective-permute-start(f32[1,4,128]{2,1,0:T(4,128)S(1)} %get-tuple-element.792), channel_id=1, source_target_pairs={{0,1},{1,2},{2,3},{3,4},{4,5},{5,6},{6,7},{7,8},{8,9},{9,10},{10,1... | collective-permute-start | bytes 6152 | tf_op jit(solution)/shard_map/ppermute | solution.py:20
  102.4 9.2 %collective-permute-start.5 = (f32[1,4,128]{2,1,0:T(4,128)S(1)}, f32[1,4,128]{2,1,0:T(4,128)S(1)}, u32[]{:S(2)}, u32[]{:S(2)}) collective-permute-start(f32[1,4,128]{2,1,0:T(4,128)S(1)} %get-tuple-element.793), channel_id=1, source_target_pairs={{1,0},{2,1},{3,2},{4,3},{5,4},{6,5},{7,6},{8,7},{9,8},{10,9},{11,1... | collective-permute-start | bytes 6152 | tf_op jit(solution)/shard_map/ppermute | solution.py:20
  137.7 10.0 %collective-permute-start.6 = (f32[1,4,128]{2,1,0:T(4,128)S(1)}, f32[1,4,128]{2,1,0:T(4,128)S(1)}, u32[]{:S(2)}, u32[]{:S(2)}) collective-permute-start(f32[1,4,128]{2,1,0:T(4,128)S(1)} %get-tuple-element.790), channel_id=1, source_target_pairs={{0,1},{1,2},{2,3},{3,4},{4,5},{5,6},{6,7},{7,8},{8,9},{9,10},{10,1... | collective-permute-start | bytes 6152 | tf_op jit(solution)/shard_map/ppermute | solution.py:20
  139.6 9.2 %collective-permute-start.7 = (f32[1,4,128]{2,1,0:T(4,128)S(1)}, f32[1,4,128]{2,1,0:T(4,128)S(1)}, u32[]{:S(2)}, u32[]{:S(2)}) collective-permute-start(f32[1,4,128]{2,1,0:T(4,128)S(1)} %get-tuple-element.791), channel_id=1, source_target_pairs={{1,0},{2,1},{3,2},{4,3},{5,4},{6,5},{7,6},{8,7},{9,8},{10,9},{11,1... | collective-permute-start | bytes 6152 | tf_op jit(solution)/shard_map/ppermute | solution.py:20
  173.4 9.8 %collective-permute-start.8 = (f32[1,4,128]{2,1,0:T(4,128)S(1)}, f32[1,4,128]{2,1,0:T(4,128)S(1)}, u32[]{:S(2)}, u32[]{:S(2)}) collective-permute-start(f32[1,4,128]{2,1,0:T(4,128)S(1)} %get-tuple-element.788), channel_id=1, source_target_pairs={{0,1},{1,2},{2,3},{3,4},{4,5},{5,6},{6,7},{7,8},{8,9},{9,10},{10,1... | collective-permute-start | bytes 6152 | tf_op jit(solution)/shard_map/ppermute | solution.py:20
  175.4 9.2 %collective-permute-start.9 = (f32[1,4,128]{2,1,0:T(4,128)S(1)}, f32[1,4,128]{2,1,0:T(4,128)S(1)}, u32[]{:S(2)}, u32[]{:S(2)}) collective-permute-start(f32[1,4,128]{2,1,0:T(4,128)S(1)} %get-tuple-element.789), channel_id=1, source_target_pairs={{1,0},{2,1},{3,2},{4,3},{5,4},{6,5},{7,6},{8,7},{9,8},{10,9},{11,1... | collective-permute-start | bytes 6152 | tf_op jit(solution)/shard_map/ppermute | solution.py:20
  210.7 9.8 %collective-permute-start.10 = (f32[1,4,128]{2,1,0:T(4,128)S(1)}, f32[1,4,128]{2,1,0:T(4,128)S(1)}, u32[]{:S(2)}, u32[]{:S(2)}) collective-permute-start(f32[1,4,128]{2,1,0:T(4,128)S(1)} %get-tuple-element.786), channel_id=1, source_target_pairs={{0,1},{1,2},{2,3},{3,4},{4,5},{5,6},{6,7},{7,8},{8,9},{9,10},{10,1... | collective-permute-start | bytes 6152 | tf_op jit(solution)/shard_map/ppermute | solution.py:20
  212.6 9.2 %collective-permute-start.11 = (f32[1,4,128]{2,1,0:T(4,128)S(1)}, f32[1,4,128]{2,1,0:T(4,128)S(1)}, u32[]{:S(2)}, u32[]{:S(2)}) collective-permute-start(f32[1,4,128]{2,1,0:T(4,128)S(1)} %get-tuple-element.787), channel_id=1, source_target_pairs={{1,0},{2,1},{3,2},{4,3},{5,4},{6,5},{7,6},{8,7},{9,8},{10,9},{11,1... | collective-permute-start | bytes 6152 | tf_op jit(solution)/shard_map/ppermute | solution.py:20
  246.4 10.0 %collective-permute-start.12 = (f32[1,4,128]{2,1,0:T(4,128)S(1)}, f32[1,4,128]{2,1,0:T(4,128)S(1)}, u32[]{:S(2)}, u32[]{:S(2)}) collective-permute-start(f32[1,4,128]{2,1,0:T(4,128)S(1)} %get-tuple-element.784), channel_id=1, source_target_pairs={{0,1},{1,2},{2,3},{3,4},{4,5},{5,6},{6,7},{7,8},{8,9},{9,10},{10,1... | collective-permute-start | bytes 6152 | tf_op jit(solution)/shard_map/ppermute | solution.py:20
  248.4 9.2 %collective-permute-start.13 = (f32[1,4,128]{2,1,0:T(4,128)S(1)}, f32[1,4,128]{2,1,0:T(4,128)S(1)}, u32[]{:S(2)}, u32[]{:S(2)}) collective-permute-start(f32[1,4,128]{2,1,0:T(4,128)S(1)} %get-tuple-element.785), channel_id=1, source_target_pairs={{1,0},{2,1},{3,2},{4,3},{5,4},{6,5},{7,6},{8,7},{9,8},{10,9},{11,1... | collective-permute-start | bytes 6152 | tf_op jit(solution)/shard_map/ppermute | solution.py:20
  283.6 0.6 copy-start.1
  283.7 0.6 copy-start.2
where the time goes:
time: 285 us; the launch traced here: 284 us
  starting transfers between devices  85.5 us (30%)
  other arithmetic  78 us (27%)
  local copies, waits for them, and re-layouts  73.3 us (26%)
  waiting for transfers between devices  24.6 us (9%)
  loops' own time  20.6 us (7%)
    ppermute x14, starting transfers between devices, shifted(): lax.ppermute(value, axis, [(source, source + steps) for source in range(f...  68.9 us
    gather x148, local copies, waits for them, and re-layouts, one_block(): jnp.take(values, near_rows, axis=1)  50.6 us
    reduce_sum x12, other arithmetic, jacobi_kernel(): inflow = jnp.sum(coupling * near_energy[0][:, :, None, :], axis=(1, 3))  24.3 us
    another operation x7, loops' own time, tile_blocks(): blocks = lax.map(one_block, jnp.arange(block_count, dtype=jnp.int32))  20.6 us
    mul x12, other arithmetic, limiter_kernel(): scaled = volume[:, :, None, :] * forces * change  17.4 us
    dynamic_slice x28, local copies, waits for them, and re-layouts, tile_blocks(): blocks = lax.map(one_block, jnp.arange(block_count, dtype=jnp.int32))  16.4 us
    reduce_sum x28, other arithmetic, geometry(): distance = jnp.sqrt(jnp.sum(offsets * offsets, axis=0))  15.4 us
    all_to_all x1, starting transfers between devices, local(): lax.all_to_all(out_slots, 'group', split_axis=0, concat_axis=0, tiled=True)  11.6 us
  transfers between devices with their start and end apart: 16, of which 9 were waited for; matrix products, arithmetic and copies ran while one was open for 1% of the time, Pallas kernels for 0%

commit v1 on v0

v1 whole, which is shorter than its diff:
```python
import math

import jax
import jax.numpy as jnp
from jax import lax
from jax.experimental import pallas as pl
from jax.experimental.pallas import tpu as pltpu
from jax.sharding import PartitionSpec as P

TILE = 128
GMAX = 4
SWEEPS = 3
NB = 6
TD = 16
EXT = TD + 2 * GMAX
ROWS = 24
CHUNK = 32
KERNEL_NORM = 21.0 / (16.0 * math.pi)
TIME_STEP = 0.05
F32 = jnp.float32
BF16 = jnp.bfloat16
VMEM = pltpu.MemorySpace.VMEM
SMEM = pltpu.MemorySpace.SMEM
AXES = ("group", "member")


def call(body, outs, scratch, name, *args):
    specs = [
        pl.BlockSpec(memory_space=SMEM if a.dtype == jnp.int32 else VMEM) for a in args
    ]
    return pl.pallas_call(
        body,
        out_shape=[jax.ShapeDtypeStruct(shape, dtype) for shape, dtype in outs],
        in_specs=specs,
        out_specs=[pl.BlockSpec(memory_space=VMEM) for _ in outs],
        scratch_shapes=scratch,
        name=name,
        compiler_params=pltpu.CompilerParams(vmem_limit_bytes=40 * 1024 * 1024),
    )(*args)


def pack_body(slot, part, out, count):
    groups = out.shape[0]
    for g in range(groups):
        count[g] = 0
        out[g, 0:16] = jnp.zeros((16, TILE), F32)
        out[g, 16:24] = jnp.full((8, TILE), -1.0, F32)
    for t in range(TD):
        s = slot[t]
        g = s // (TD * 8)
        n = count[g]
        count[g] = n + 1
        out[g, pl.ds(pl.multiple_of(n * 8, 8), 8), :] = part[:, t * TILE : (t + 1) * TILE]
        out[g, pl.ds(16 + n, 1), :] = jnp.full((1, TILE), (s % TD).astype(F32))


def split3(x):
    hi = x.astype(BF16).astype(F32)
    rest = x - hi
    mid = rest.astype(BF16).astype(F32)
    return hi, mid, rest - mid


def send_parts(odd, values, first, second):
    n = values.shape[-2]
    tail = values[..., n - GMAX :, :]
    head = values[..., :GMAX, :]
    first[...] = jnp.where(odd, tail, head)
    second[...] = jnp.where(odd, head, tail)


def extend(odd, values, first, second):
    left = jnp.where(odd, second, first)
    right = jnp.where(odd, first, second)
    return jnp.concatenate([values, left, right], axis=-2)


def unpack_body(par, got, arranged, first, second):
    groups = got.shape[0] // ROWS
    odd = par[0] == 1
    lane = lax.broadcasted_iota(jnp.int32, (groups, TILE), 1).astype(F32)
    marks = [
        jnp.where(got[pl.ds(16 + n, groups, stride=ROWS), :] == lane, 1.0, 0.0) for n in range(2)
    ]
    marks.append(jnp.zeros((TILE - 2 * groups, TILE), F32))
    choose = jnp.concatenate(marks, axis=0).T[:TD, : 2 * groups].astype(BF16)
    for r in range(8):
        tiles = jnp.concatenate(
            [got[pl.ds(n * 8 + r, groups, stride=ROWS), :] for n in range(2)], axis=0
        )
        moved = sum(
            jnp.dot(choose, piece.astype(BF16), preferred_element_type=F32)
            for piece in split3(tiles)
        )
        arranged[r] = moved
    send_parts(odd, arranged[0:6], first, second)


def place_of(entry, left):
    j = entry - left
    return jnp.where(j < 0, j + TD + GMAX, jnp.where(j < TD, j, j + GMAX))


def pairs_body(par, near, ghosts, arranged, first, second, dens, ext, fh, fl, out1, out2, cols):
    odd = par[0] == 1
    left = ghosts[0, 0]
    ext[...] = extend(odd, arranged[0:6], first[...], second[...])
    for f in range(5):
        turned = ext[f].T
        for t in range(EXT):
            cols[f, t] = jnp.broadcast_to(turned[:, t : t + 1], (TILE, TILE))

    def tile(s, carry):
        own = [arranged[f, pl.ds(s, 1), :] for f in range(5)]
        x_i, y_i, z_i, _, h_i = [jnp.broadcast_to(v, (CHUNK, TILE)) for v in own]
        half = 0.5 / h_i
        total = jnp.zeros((CHUNK, TILE), F32)
        for n in range(NB):
            t = place_of(near[s, n], left)
            for c in range(TILE // CHUNK):
                rows = pl.ds(c * CHUNK, CHUNK)
                dx = cols[0, t, rows, :] - x_i
                dy = cols[1, t, rows, :] - y_i
                dz = cols[2, t, rows, :] - z_i
                r2 = dx * dx + dy * dy + dz * dz
                r = r2 * lax.rsqrt(jnp.maximum(r2, 1e-30))
                u = jnp.maximum(1.0 - r * half, 0.0)
                u2 = u * u
                total = total + (cols[3, t, rows, :] * (5.0 - 4.0 * u)) * (u2 * u2)
                reach = cols[4, t, rows, :] + h_i
                w = jnp.maximum(reach - r, 0.0)
                p2 = reach * reach
                p4 = p2 * p2
                force = (w * w * w) / (p4 * p4)
                high = force.astype(BF16)
                at = pl.ds(n * TILE + c * CHUNK, CHUNK)
                fh[s, at, :] = high
                fl[s, at, :] = (force - high.astype(F32)).astype(BF16)
        dens[pl.ds(s, 1), :] = jnp.sum(total, axis=0, keepdims=True)
        return carry

    lax.fori_loop(0, TD, tile, 0)
    h = arranged[4]
    density = KERNEL_NORM * dens[...] / (h * h * h)
    dens[...] = density
    send_parts(odd, density, out1, out2)


def weigh(near, left, fh, fl, vectors, staged, operand, result):
    count = len(vectors)
    used = 3 * count
    height = staged.shape[0] // EXT
    pieces = [split3(v) for v in vectors]
    for k in range(3):
        for q in range(count):
            staged[pl.ds(k * count + q, EXT, stride=height), :] = pieces[q][k]
    for q in range(used, height):
        staged[pl.ds(q, EXT, stride=height), :] = jnp.zeros((EXT, TILE), F32)
    for t in range(EXT):
        operand[t] = staged[t * height : (t + 1) * height, :].astype(BF16)
    for s in range(TD):
        row = jnp.concatenate([operand[place_of(near[s, n], left)] for n in range(NB)], axis=1)
        got = jnp.dot(row, fh[s], preferred_element_type=F32)
        got = got + jnp.dot(row, fl[s], preferred_element_type=F32)
        result[s * height : (s + 1) * height, :] = got
    sums = []
    for q in range(count):
        sums.append(
            sum(result[pl.ds(k * count + q, TD, stride=height), :] for k in (2, 1, 0))
        )
    return sums


def limiter_body(begin, *refs):
    if begin:
        (par, near, ghosts, arranged, ext, fh, fl, dens, d1, d2) = refs[:10]
        (diff, out1, out2, sums, fixed, dens_ext, staged, operand, result) = refs[10:]
        odd = par[0] == 1
        rho = extend(odd, dens[...], d1[...], d2[...])
        dens_ext[...] = rho
        e = ext[5]
    else:
        (par, near, ghosts, arranged, ext, fh, fl, dens_ext, fixed, energy, e1, e2) = refs[:12]
        (diff, out1, out2, sums, ext_energy, staged, operand, result) = refs[12:]
        odd = par[0] == 1
        rho = dens_ext[...]
        e = extend(odd, energy[...], e1[...], e2[...])
        ext_energy[...] = e
    left = ghosts[0, 0]
    v = (160.0 * KERNEL_NORM) * ext[3] / rho
    x = [ext[f] - 0.5 for f in range(3)]
    ve = v * e
    vectors = [ve] + [ve * x[f] for f in range(3)]
    if begin:
        vectors = vectors + [v] + [v * x[f] for f in range(3)]
    got = weigh(near, left, fh, fl, vectors, staged, operand, result)
    if begin:
        for q in range(4):
            fixed[q] = got[4 + q]
    base = [fixed[q] for q in range(4)]
    e_i = e[:TD]
    square = jnp.zeros((TD, TILE), F32)
    for f in range(3):
        x_i = x[f][:TD]
        grad = (got[1 + f] - x_i * got[0]) - e_i * (base[1 + f] - x_i * base[0])
        square = square + grad * grad
    thick = arranged[6] * rho[:TD]
    ratio = jnp.sqrt(square) / (thick * e_i)
    value = (2.0 + ratio) / ((6.0 + 3.0 * ratio + ratio * ratio) * thick)
    diff[...] = value
    sums[0] = base[0]
    sums[1] = got[0]
    send_parts(odd, value, out1, out2)


def jacobi_body(last, par, near, ghosts, arranged, ext, fh, fl, dens_ext, e_ext, sums, diff, d1, d2, *refs):
    if last:
        new, staged, operand, result = refs
    else:
        new, out1, out2, staged, operand, result = refs
    odd = par[0] == 1
    left = ghosts[0, 0]
    spread = extend(odd, diff[...], d1[...], d2[...])
    rho = dens_ext[...]
    vd = ((160.0 * KERNEL_NORM) * ext[3] / rho) * spread
    got = weigh(near, left, fh, fl, [vd, vd * e_ext[...]], staged, operand, result)
    own = spread[:TD]
    scale = TIME_STEP / rho[:TD]
    rate = scale * (own * sums[0] + got[0])
    inflow = scale * (own * sums[1] + got[1])
    value = (arranged[5] + TIME_STEP * arranged[7] + inflow) / (1.0 + rate)
    new[...] = value
    if not last:
        send_parts(odd, value, out1, out2)


def workspace(height):
    return [
        pltpu.VMEM((EXT * height, TILE), F32),
        pltpu.VMEM((EXT, height, TILE), BF16),
        pltpu.VMEM((TD * height, TILE), F32),
    ]


def swap(first, second):
    count = lax.axis_size("group") * lax.axis_size("member")
    odd = [(s, s + 1) for s in range(1, count - 1, 2)]
    even = [(s, s + 1) for s in range(0, count - 1, 2)]
    got = []
    for value, pairs in ((first, odd), (second, even)):
        got.append(lax.ppermute(value, AXES, pairs + [(b, a) for a, b in pairs]))
    return got


def local(particles, new_slot, neighbours, ghosts):
    groups = lax.axis_size("group")
    par = (lax.axis_index("member") % 2).astype(jnp.int32).reshape(1)
    (outgoing,) = call(
        pack_body,
        [((groups, ROWS, TILE), F32)],
        [pltpu.SMEM((groups,), jnp.int32)],
        "pack",
        new_slot,
        particles,
    )
    received = lax.all_to_all(outgoing, "group", split_axis=0, concat_axis=0, tiled=True)
    edge = ((GMAX, TILE), F32)
    own = ((TD, TILE), F32)
    wide = ((EXT, TILE), F32)
    arranged, s1, s2 = call(
        unpack_body,
        [((8, TD, TILE), F32), ((6, GMAX, TILE), F32), ((6, GMAX, TILE), F32)],
        [],
        "unpack",
        par,
        received.reshape(groups * ROWS, TILE),
    )
    table = (par, neighbours, ghosts)
    s1, s2 = swap(s1, s2)
    density, ext, fh, fl, r1, r2 = call(
        pairs_body,
        [
            own,
            ((6, EXT, TILE), F32),
            ((TD, NB * TILE, TILE), BF16),
            ((TD, NB * TILE, TILE), BF16),
            edge,
            edge,
        ],
        [pltpu.VMEM((5, EXT, TILE, TILE), F32)],
        "pairs",
        *table,
        arranged,
        s1,
        s2,
    )
    r1, r2 = swap(r1, r2)
    shared = (*table, arranged, ext, fh, fl)
    for step in range(SWEEPS):
        if step == 0:
            diff, d1, d2, sums, fixed, dens_ext = call(
                lambda *refs: limiter_body(True, *refs),
                [own, edge, edge, ((2, TD, TILE), F32), ((4, TD, TILE), F32), wide],
                workspace(32),
                "limiter_first",
                *shared,
                density,
                r1,
                r2,
            )
            e_ext = ext[5]
        else:
            diff, d1, d2, sums, e_ext = call(
                lambda *refs: limiter_body(False, *refs),
                [own, edge, edge, ((2, TD, TILE), F32), wide],
                workspace(16),
                "limiter",
                *shared,
                dens_ext,
                fixed,
                energy,
                e1,
                e2,
            )
        d1, d2 = swap(d1, d2)
        last = step == SWEEPS - 1
        results = call(
            lambda *refs: jacobi_body(last, *refs),
            [own] if last else [own, edge, edge],
            workspace(16),
            "jacobi",
            *shared,
            dens_ext,
            e_ext,
            sums,
            diff,
            d1,
            d2,
        )
        if last:
            energy = results[0]
        else:
            energy, e1, e2 = results
            e1, e2 = swap(e1, e2)
    return (energy.reshape(-1), density.reshape(-1))


def solution(mesh):
    in_specs = (
        P(None, ("group", "member")),
        P(("group", "member")),
        P(("group", "member"), None),
        P(("group", "member"), None),
    )
    out_specs = (P(("group", "member")), P(("group", "member")))
    return jax.shard_map(local, mesh=mesh, in_specs=in_specs, out_specs=out_specs, check_vma=False)
```

time: 285 us -> 118 us (0.41)
  other arithmetic: 78 us -> 0 us
  local copies, waits for them, and re-layouts: 73.3 us -> 4.27 us
  starting transfers between devices: 85.5 us -> 35.9 us
  waiting for transfers between devices: 24.6 us -> 52.1 us
  Pallas kernels: 0 us -> 24.1 us
  loops' own time: 20.6 us -> 0 us
    reduce_sum x70 -> x0, other arithmetic: 54.1 us -> none  [the longest x12 24.3 us: jacobi_kernel(): inflow = jnp.sum(coupling * near_energy[0][:, :, None, :], axis=(1, 3))]
    gather x148 -> x0, local copies, waits for them, and re-layouts: 50.6 us -> none  [one_block(): jnp.take(values, near_rows, axis=1)]
    ppermute x14, starting transfers between devices: 68.9 us -> 24.3 us  [swap(): got.append(lax.ppermute(value, AXES, pairs + [(b, a) for a, b in pairs]))]
    ppermute x14, waiting for transfers between devices: 8.6 us -> 38.8 us  [swap(): got.append(lax.ppermute(value, AXES, pairs + [(b, a) for a, b in pairs]))]
    pallas_call x0 -> x9, Pallas kernels: none -> 24.1 us  [call(): pl.pallas_call(body, out_shape=[jax.ShapeDtypeStruct(shape, dtype) for sh...]
    another operation x7 -> x0, loops' own time: 20.6 us -> none  [tile_blocks(): blocks = lax.map(one_block, jnp.arange(block_count, dtype=jnp.int32))]
    mul x24 -> x0, other arithmetic: 18.3 us -> none  [the longest x12 17.4 us: limiter_kernel(): scaled = volume[:, :, None, :] * forces * change]
    dynamic_slice x28 -> x0, local copies, waits for them, and re-layouts: 16.4 us -> none  [tile_blocks(): blocks = lax.map(one_block, jnp.arange(block_count, dtype=jnp.int32))]
  transfers between devices with their start and end apart: 16 -> 15, of which waited for: 9 -> 8; matrix products, arithmetic and copies ran while one was open for 1% -> 1% of each run, Pallas kernels for 0% -> 0%
where the time goes in v1:
time: 118 us; the launch traced here: 117 us
  waiting for transfers between devices  52.1 us (44%)
  starting transfers between devices  35.9 us (30%)
  Pallas kernels  24.1 us (20%)
  local copies, waits for them, and re-layouts  4.27 us (4%)
    ppermute x14, waiting for transfers between devices, swap(): got.append(lax.ppermute(value, AXES, pairs + [(b, a) for a, b in pairs]))  38.8 us
    ppermute x14, starting transfers between devices, swap(): got.append(lax.ppermute(value, AXES, pairs + [(b, a) for a, b in pairs]))  24.3 us
    pallas_call x9, Pallas kernels, call(): pl.pallas_call(body, out_shape=[jax.ShapeDtypeStruct(shape, dtype) for sh...  24.1 us
    all_to_all x1, waiting for transfers between devices, local(): lax.all_to_all(outgoing, 'group', split_axis=0, concat_axis=0, tiled=True)  13.2 us
    all_to_all x1, starting transfers between devices, local(): lax.all_to_all(outgoing, 'group', split_axis=0, concat_axis=0, tiled=True)  11.6 us
    unnamed x13, local copies, waits for them, and re-layouts  4.26 us
  transfers between devices with their start and end apart: 15, of which 8 were waited for; matrix products, arithmetic and copies ran while one was open for 1% of the time, Pallas kernels for 0%

profile of v1, /device:TPU:2, one launch (start us, length us, event | category | flops | bytes accessed | tf_op | source)
XLA Modules:
  0.0 117.1 jit_solution(8707619833559473803)
XLA Ops:
  0.6 0.8 copy-done
  1.5 0.7 copy-done.5
  2.1 1.5 %pack.1 = f32[32,24,128]{2,1,0:T(8,128)} custom-call(s32[16]{0:T(128)S(1)} %copy-done.5, f32[8,2048]{1,0:T(8,128)S(1)} %copy-done), custom_call_target="tpu_custom_call" | custom-call | tf_op jit(solution)/shard_map/pack/pallas_call | solution.py:31
  3.6 11.6 %all-to-all-start = ((f32[32,24,128]{2,1,0:T(8,128)}), f32[32,24,128]{2,1,0:T(8,128)S(1)}, u32[]{:S(2)}, u32[]{:S(2)}) async-start(f32[32,24,128]{2,1,0:T(8,128)} %pack.1), calls=%async_computation | async-start | bytes 786432 | tf_op jit(solution)/shard_map/all_to_all | solution.py:266
  15.2 13.2 %all-to-all-done = f32[32,24,128]{2,1,0:T(8,128)S(1)} async-done(((f32[32,24,128]{2,1,0:T(8,128)}), f32[32,24,128]{2,1,0:T(8,128)S(1)}, u32[]{:S(2)}, u32[]{:S(2)}) %all-to-all-start) | async-done | bytes 393248 | tf_op jit(solution)/shard_map/all_to_all | solution.py:266
  28.5 0.3 unpack.1
  28.8 3.3 %collective-permute-start = (f32[6,4,128]{2,1,0:T(4,128)S(1)}, f32[6,4,128]{2,1,0:T(4,128)S(1)}, u32[]{:S(2)}, u32[]{:S(2)}) collective-permute-start(f32[6,4,128]{2,1,0:T(4,128)S(1)} %get-tuple-element.34), channel_id=1, source_target_pairs={{1,2},{3,4},{5,6},{7,8},{9,10},{11,12},{13,14},{15,16},{17,18},{19... | collective-permute-start | bytes 36872 | tf_op jit(solution)/shard_map/ppermute | solution.py:251
  32.1 0.4 collective-permute-start.1
  32.5 0.8 copy.12.near.refs_1_
  33.2 4.8 %collective-permute-done.first = f32[6,4,128]{2,1,0:T(4,128)S(1)} collective-permute-done((f32[6,4,128]{2,1,0:T(4,128)S(1)}, f32[6,4,128]{2,1,0:T(4,128)S(1)}, u32[]{:S(2)}, u32[]{:S(2)}) %collective-permute-start) | collective-permute-done | bytes 12320 | tf_op jit(solution)/shard_map/ppermute | solution.py:251
  38.0 0.7 copy-done.1
  38.6 10.9 %pairs.1 = (f32[16,128]{1,0:T(8,128)}, f32[6,24,128]{2,1,0:T(8,128)S(1)}, bf16[16,768,128]{2,1,0:T(8,128)(2,1)S(1)}, bf16[16,768,128]{2,1,0:T(8,128)(2,1)S(1)}, ...) custom-call(s32[1]{0:T(128)} %bitcast.par.refs_0_, s32[16,6]{1,0:T(8,128)S(1)} %copy.12.near.refs_1_, s32[1,2]{1,0:T(1,128)S(1)} %copy-done.1, ...), custom_call_target="tpu_custom_call" | custom-call | tf_op jit(solution)/shard_map/pairs/pallas_call | solution.py:31
  49.5 3.3 %collective-permute-start.2 = (f32[4,128]{1,0:T(4,128)S(1)}, f32[4,128]{1,0:T(4,128)S(1)}, u32[]{:S(2)}, u32[]{:S(2)}) collective-permute-start(f32[4,128]{1,0:T(4,128)S(1)} %get-tuple-element.40), channel_id=1, source_target_pairs={{1,2},{3,4},{5,6},{7,8},{9,10},{11,12},{13,14},{15,16},{17,18},{19... | collective-permute-start | bytes 6152 | tf_op jit(solution)/shard_map/ppermute | solution.py:251
  52.9 5.7 %collective-permute-done.2.refs_8_ = f32[4,128]{1,0:T(4,128)S(1)} collective-permute-done((f32[4,128]{1,0:T(4,128)S(1)}, f32[4,128]{1,0:T(4,128)S(1)}, u32[]{:S(2)}, u32[]{:S(2)}) %collective-permute-start.2) | collective-permute-done | bytes 2080 | tf_op jit(solution)/shard_map/ppermute | solution.py:251
  58.6 0.7 copy-done.2
  59.3 0.7 copy-done.4
  60.0 2.2 %limiter_first.1 = (f32[16,128]{1,0:T(8,128)S(1)}, f32[4,128]{1,0:T(4,128)S(1)}, f32[4,128]{1,0:T(4,128)S(1)}, f32[2,16,128]{2,1,0:T(8,128)S(1)}, f32[4,16,128]{2,1,0:T(8,128)S(1)}, /*index=5*/f32[24,128]{1,0:T(8,128)S(1)}) custom-call(s32[1]{0:T(128)} %bitcast.par.refs_0_, s32[16,6]{1,0:T(8,128)S(1)} %copy.12.near.refs_1_, s32[1,2]{1,0:T(1,128)S(1)} %copy-done.2, ...), custom_call_target="tpu_custom_call" | custom-call | tf_op jit(solution)/shard_map/limiter_first/pallas_call | solution.py:31
  62.2 3.3 %collective-permute-start.4 = (f32[4,128]{1,0:T(4,128)S(1)}, f32[4,128]{1,0:T(4,128)S(1)}, u32[]{:S(2)}, u32[]{:S(2)}) collective-permute-start(f32[4,128]{1,0:T(4,128)S(1)} %get-tuple-element.46), channel_id=1, source_target_pairs={{1,2},{3,4},{5,6},{7,8},{9,10},{11,12},{13,14},{15,16},{17,18},{19... | collective-permute-start | bytes 6152 | tf_op jit(solution)/shard_map/ppermute | solution.py:251
  65.6 5.7 %collective-permute-done.4.refs_11_ = f32[4,128]{1,0:T(4,128)S(1)} collective-permute-done((f32[4,128]{1,0:T(4,128)S(1)}, f32[4,128]{1,0:T(4,128)S(1)}, u32[]{:S(2)}, u32[]{:S(2)}) %collective-permute-start.4) | collective-permute-done | bytes 2080 | tf_op jit(solution)/shard_map/ppermute | solution.py:251
  71.3 1.7 %jacobi.3 = (f32[16,128]{1,0:T(8,128)S(1)}, f32[4,128]{1,0:T(4,128)S(1)}, f32[4,128]{1,0:T(4,128)S(1)}) custom-call(s32[1]{0:T(128)} %bitcast.par.refs_0_, s32[16,6]{1,0:T(8,128)S(1)} %copy.12.near.refs_1_, s32[1,2]{1,0:T(1,128)S(1)} %copy-done.3, f32[8,16,128]{2,1,0:T(8,128)S(1)} %get-tuple-element.33.arranged.refs_3_, ...), custom_call_target="tpu_custom_call" | custom-call | tf_op jit(solution)/shard_map/jacobi/pallas_call | solution.py:31
  73.0 3.3 %collective-permute-start.6 = (f32[4,128]{1,0:T(4,128)S(1)}, f32[4,128]{1,0:T(4,128)S(1)}, u32[]{:S(2)}, u32[]{:S(2)}) collective-permute-start(f32[4,128]{1,0:T(4,128)S(1)} %get-tuple-element.49), channel_id=1, source_target_pairs={{1,2},{3,4},{5,6},{7,8},{9,10},{11,12},{13,14},{15,16},{17,18},{19... | collective-permute-start | bytes 6152 | tf_op jit(solution)/shard_map/ppermute | solution.py:251
  76.4 5.7 %collective-permute-done.6.refs_10_ = f32[4,128]{1,0:T(4,128)S(1)} collective-permute-done((f32[4,128]{1,0:T(4,128)S(1)}, f32[4,128]{1,0:T(4,128)S(1)}, u32[]{:S(2)}, u32[]{:S(2)}) %collective-permute-start.6) | collective-permute-done | bytes 2080 | tf_op jit(solution)/shard_map/ppermute | solution.py:251
  82.2 1.8 %limiter.2 = (f32[16,128]{1,0:T(8,128)S(1)}, f32[4,128]{1,0:T(4,128)S(1)}, f32[4,128]{1,0:T(4,128)S(1)}, f32[2,16,128]{2,1,0:T(8,128)S(1)}, f32[24,128]{1,0:T(8,128)S(1)}) custom-call(s32[1]{0:T(128)} %bitcast.par.refs_0_, s32[16,6]{1,0:T(8,128)S(1)} %copy.12.near.refs_1_, s32[1,2]{1,0:T(1,128)S(1)} %copy-done.3, ...), custom_call_target="tpu_custom_call" | custom-call | tf_op jit(solution)/shard_map/limiter/pallas_call | solution.py:31
  83.9 3.3 %collective-permute-start.8 = (f32[4,128]{1,0:T(4,128)S(1)}, f32[4,128]{1,0:T(4,128)S(1)}, u32[]{:S(2)}, u32[]{:S(2)}) collective-permute-start(f32[4,128]{1,0:T(4,128)S(1)} %get-tuple-element.54), channel_id=1, source_target_pairs={{1,2},{3,4},{5,6},{7,8},{9,10},{11,12},{13,14},{15,16},{17,18},{19... | collective-permute-start | bytes 6152 | tf_op jit(solution)/shard_map/ppermute | solution.py:251
  87.3 5.7 %collective-permute-done.8.refs_11_ = f32[4,128]{1,0:T(4,128)S(1)} collective-permute-done((f32[4,128]{1,0:T(4,128)S(1)}, f32[4,128]{1,0:T(4,128)S(1)}, u32[]{:S(2)}, u32[]{:S(2)}) %collective-permute-start.8) | collective-permute-done | bytes 2080 | tf_op jit(solution)/shard_map/ppermute | solution.py:251
  93.1 1.7 %jacobi.4 = (f32[16,128]{1,0:T(8,128)S(1)}, f32[4,128]{1,0:T(4,128)S(1)}, f32[4,128]{1,0:T(4,128)S(1)}) custom-call(s32[1]{0:T(128)} %bitcast.par.refs_0_, s32[16,6]{1,0:T(8,128)S(1)} %copy.12.near.refs_1_, s32[1,2]{1,0:T(1,128)S(1)} %copy-done.3, f32[8,16,128]{2,1,0:T(8,128)S(1)} %get-tuple-element.33.arranged.refs_3_, ...), custom_call_target="tpu_custom_call" | custom-call | tf_op jit(solution)/shard_map/jacobi/pallas_call | solution.py:31
  94.8 3.3 %collective-permute-start.10 = (f32[4,128]{1,0:T(4,128)S(1)}, f32[4,128]{1,0:T(4,128)S(1)}, u32[]{:S(2)}, u32[]{:S(2)}) collective-permute-start(f32[4,128]{1,0:T(4,128)S(1)} %get-tuple-element.57), channel_id=1, source_target_pairs={{1,2},{3,4},{5,6},{7,8},{9,10},{11,12},{13,14},{15,16},{17,18},{19... | collective-permute-start | bytes 6152 | tf_op jit(solution)/shard_map/ppermute | solution.py:251
  98.4 5.5 %collective-permute-done.10.refs_10_ = f32[4,128]{1,0:T(4,128)S(1)} collective-permute-done((f32[4,128]{1,0:T(4,128)S(1)}, f32[4,128]{1,0:T(4,128)S(1)}, u32[]{:S(2)}, u32[]{:S(2)}) %collective-permute-start.10) | collective-permute-done | bytes 2080 | tf_op jit(solution)/shard_map/ppermute | solution.py:251
  103.9 1.8 %limiter.3 = (f32[16,128]{1,0:T(8,128)S(1)}, f32[4,128]{1,0:T(4,128)S(1)}, f32[4,128]{1,0:T(4,128)S(1)}, f32[2,16,128]{2,1,0:T(8,128)S(1)}, f32[24,128]{1,0:T(8,128)S(1)}) custom-call(s32[1]{0:T(128)} %bitcast.par.refs_0_, s32[16,6]{1,0:T(8,128)S(1)} %copy.12.near.refs_1_, s32[1,2]{1,0:T(1,128)S(1)} %copy-done.3, ...), custom_call_target="tpu_custom_call" | custom-call | tf_op jit(solution)/shard_map/limiter/pallas_call | solution.py:31
  105.7 3.3 %collective-permute-start.12 = (f32[4,128]{1,0:T(4,128)S(1)}, f32[4,128]{1,0:T(4,128)S(1)}, u32[]{:S(2)}, u32[]{:S(2)}) collective-permute-start(f32[4,128]{1,0:T(4,128)S(1)} %get-tuple-element.62), channel_id=1, source_target_pairs={{1,2},{3,4},{5,6},{7,8},{9,10},{11,12},{13,14},{15,16},{17,18},{19... | collective-permute-start | bytes 6152 | tf_op jit(solution)/shard_map/ppermute | solution.py:251
  109.1 5.7 %collective-permute-done.12.refs_11_ = f32[4,128]{1,0:T(4,128)S(1)} collective-permute-done((f32[4,128]{1,0:T(4,128)S(1)}, f32[4,128]{1,0:T(4,128)S(1)}, u32[]{:S(2)}, u32[]{:S(2)}) %collective-permute-start.12) | collective-permute-done | bytes 2080 | tf_op jit(solution)/shard_map/ppermute | solution.py:251
  114.8 2.3 %jacobi.5 = f32[16,128]{1,0:T(8,128)} custom-call(s32[1]{0:T(128)} %bitcast.par.refs_0_, s32[16,6]{1,0:T(8,128)S(1)} %copy.12.near.refs_1_, s32[1,2]{1,0:T(1,128)S(1)} %copy-done.3, f32[8,16,128]{2,1,0:T(8,128)S(1)} %get-tuple-element.33.arranged.refs_3_, f32[6,24,128]{2,1,0:T(8,128)S(1)} %get-tuple-element.36.refs_4_, ...), custom_call_target="tpu_custom_call" | custom-call | tf_op jit(solution)/shard_map/jacobi/pallas_call | solution.py:31
  (21 shorter events, 0.8 us)
Async XLA Ops:
  0.6 0.8 copy-start
  1.5 0.7 copy-start.5
  3.6 24.9 %all-to-all-start = ((f32[32,24,128]{2,1,0:T(8,128)}), f32[32,24,128]{2,1,0:T(8,128)S(1)}, u32[]{:S(2)}, u32[]{:S(2)}) async-start(f32[32,24,128]{2,1,0:T(8,128)} %pack.1), calls=%async_computation | async-start | bytes 786432 | tf_op jit(solution)/shard_map/all_to_all | solution.py:266
  28.8 9.2 %collective-permute-start = (f32[6,4,128]{2,1,0:T(4,128)S(1)}, f32[6,4,128]{2,1,0:T(4,128)S(1)}, u32[]{:S(2)}, u32[]{:S(2)}) collective-permute-start(f32[6,4,128]{2,1,0:T(4,128)S(1)} %get-tuple-element.34), channel_id=1, source_target_pairs={{1,2},{3,4},{5,6},{7,8},{9,10},{11,12},{13,14},{15,16},{17,18},{19... | collective-permute-start | bytes 36872 | tf_op jit(solution)/shard_map/ppermute | solution.py:251
  32.1 5.9 %collective-permute-start.1 = (f32[6,4,128]{2,1,0:T(4,128)S(1)}, f32[6,4,128]{2,1,0:T(4,128)S(1)}, u32[]{:S(2)}, u32[]{:S(2)}) collective-permute-start(f32[6,4,128]{2,1,0:T(4,128)S(1)} %get-tuple-element.35), channel_id=1, source_target_pairs={{0,1},{2,3},{4,5},{6,7},{8,9},{10,11},{12,13},{14,15},{16,17},{18,... | collective-permute-start | bytes 36872 | tf_op jit(solution)/shard_map/ppermute | solution.py:251
  38.0 0.7 copy-start.1
  49.5 9.1 %collective-permute-start.2 = (f32[4,128]{1,0:T(4,128)S(1)}, f32[4,128]{1,0:T(4,128)S(1)}, u32[]{:S(2)}, u32[]{:S(2)}) collective-permute-start(f32[4,128]{1,0:T(4,128)S(1)} %get-tuple-element.40), channel_id=1, source_target_pairs={{1,2},{3,4},{5,6},{7,8},{9,10},{11,12},{13,14},{15,16},{17,18},{19... | collective-permute-start | bytes 6152 | tf_op jit(solution)/shard_map/ppermute | solution.py:251
  52.8 5.8 %collective-permute-start.3 = (f32[4,128]{1,0:T(4,128)S(1)}, f32[4,128]{1,0:T(4,128)S(1)}, u32[]{:S(2)}, u32[]{:S(2)}) collective-permute-start(f32[4,128]{1,0:T(4,128)S(1)} %get-tuple-element.41), channel_id=1, source_target_pairs={{0,1},{2,3},{4,5},{6,7},{8,9},{10,11},{12,13},{14,15},{16,17},{18,... | collective-permute-start | bytes 6152 | tf_op jit(solution)/shard_map/ppermute | solution.py:251
  58.6 0.7 copy-start.2
  59.3 0.7 copy-start.4
  60.0 11.3 %copy-start.3 = (s32[1,2]{1,0:T(1,128)S(1)}, s32[1,2]{1,0:T(1,128)}, u32[]{:S(2)}) copy-start(s32[1,2]{1,0:T(1,128)} %refs_2_.11) | copy-start | bytes 28
  62.2 9.1 %collective-permute-start.4 = (f32[4,128]{1,0:T(4,128)S(1)}, f32[4,128]{1,0:T(4,128)S(1)}, u32[]{:S(2)}, u32[]{:S(2)}) collective-permute-start(f32[4,128]{1,0:T(4,128)S(1)} %get-tuple-element.46), channel_id=1, source_target_pairs={{1,2},{3,4},{5,6},{7,8},{9,10},{11,12},{13,14},{15,16},{17,18},{19... | collective-permute-start | bytes 6152 | tf_op jit(solution)/shard_map/ppermute | solution.py:251
  65.5 5.8 %collective-permute-start.5 = (f32[4,128]{1,0:T(4,128)S(1)}, f32[4,128]{1,0:T(4,128)S(1)}, u32[]{:S(2)}, u32[]{:S(2)}) collective-permute-start(f32[4,128]{1,0:T(4,128)S(1)} %get-tuple-element.47), channel_id=1, source_target_pairs={{0,1},{2,3},{4,5},{6,7},{8,9},{10,11},{12,13},{14,15},{16,17},{18,... | collective-permute-start | bytes 6152 | tf_op jit(solution)/shard_map/ppermute | solution.py:251
  73.0 9.1 %collective-permute-start.6 = (f32[4,128]{1,0:T(4,128)S(1)}, f32[4,128]{1,0:T(4,128)S(1)}, u32[]{:S(2)}, u32[]{:S(2)}) collective-permute-start(f32[4,128]{1,0:T(4,128)S(1)} %get-tuple-element.49), channel_id=1, source_target_pairs={{1,2},{3,4},{5,6},{7,8},{9,10},{11,12},{13,14},{15,16},{17,18},{19... | collective-permute-start | bytes 6152 | tf_op jit(solution)/shard_map/ppermute | solution.py:251
  76.3 5.8 %collective-permute-start.7 = (f32[4,128]{1,0:T(4,128)S(1)}, f32[4,128]{1,0:T(4,128)S(1)}, u32[]{:S(2)}, u32[]{:S(2)}) collective-permute-start(f32[4,128]{1,0:T(4,128)S(1)} %get-tuple-element.50), channel_id=1, source_target_pairs={{0,1},{2,3},{4,5},{6,7},{8,9},{10,11},{12,13},{14,15},{16,17},{18,... | collective-permute-start | bytes 6152 | tf_op jit(solution)/shard_map/ppermute | solution.py:251
  83.9 9.1 %collective-permute-start.8 = (f32[4,128]{1,0:T(4,128)S(1)}, f32[4,128]{1,0:T(4,128)S(1)}, u32[]{:S(2)}, u32[]{:S(2)}) collective-permute-start(f32[4,128]{1,0:T(4,128)S(1)} %get-tuple-element.54), channel_id=1, source_target_pairs={{1,2},{3,4},{5,6},{7,8},{9,10},{11,12},{13,14},{15,16},{17,18},{19... | collective-permute-start | bytes 6152 | tf_op jit(solution)/shard_map/ppermute | solution.py:251
  87.2 5.8 %collective-permute-start.9 = (f32[4,128]{1,0:T(4,128)S(1)}, f32[4,128]{1,0:T(4,128)S(1)}, u32[]{:S(2)}, u32[]{:S(2)}) collective-permute-start(f32[4,128]{1,0:T(4,128)S(1)} %get-tuple-element.55), channel_id=1, source_target_pairs={{0,1},{2,3},{4,5},{6,7},{8,9},{10,11},{12,13},{14,15},{16,17},{18,... | collective-permute-start | bytes 6152 | tf_op jit(solution)/shard_map/ppermute | solution.py:251
  94.8 9.1 %collective-permute-start.10 = (f32[4,128]{1,0:T(4,128)S(1)}, f32[4,128]{1,0:T(4,128)S(1)}, u32[]{:S(2)}, u32[]{:S(2)}) collective-permute-start(f32[4,128]{1,0:T(4,128)S(1)} %get-tuple-element.57), channel_id=1, source_target_pairs={{1,2},{3,4},{5,6},{7,8},{9,10},{11,12},{13,14},{15,16},{17,18},{19... | collective-permute-start | bytes 6152 | tf_op jit(solution)/shard_map/ppermute | solution.py:251
  98.1 5.8 %collective-permute-start.11 = (f32[4,128]{1,0:T(4,128)S(1)}, f32[4,128]{1,0:T(4,128)S(1)}, u32[]{:S(2)}, u32[]{:S(2)}) collective-permute-start(f32[4,128]{1,0:T(4,128)S(1)} %get-tuple-element.58), channel_id=1, source_target_pairs={{0,1},{2,3},{4,5},{6,7},{8,9},{10,11},{12,13},{14,15},{16,17},{18,... | collective-permute-start | bytes 6152 | tf_op jit(solution)/shard_map/ppermute | solution.py:251
  105.7 9.1 %collective-permute-start.12 = (f32[4,128]{1,0:T(4,128)S(1)}, f32[4,128]{1,0:T(4,128)S(1)}, u32[]{:S(2)}, u32[]{:S(2)}) collective-permute-start(f32[4,128]{1,0:T(4,128)S(1)} %get-tuple-element.62), channel_id=1, source_target_pairs={{1,2},{3,4},{5,6},{7,8},{9,10},{11,12},{13,14},{15,16},{17,18},{19... | collective-permute-start | bytes 6152 | tf_op jit(solution)/shard_map/ppermute | solution.py:251
  109.0 5.8 %collective-permute-start.13 = (f32[4,128]{1,0:T(4,128)S(1)}, f32[4,128]{1,0:T(4,128)S(1)}, u32[]{:S(2)}, u32[]{:S(2)}) collective-permute-start(f32[4,128]{1,0:T(4,128)S(1)} %get-tuple-element.63), channel_id=1, source_target_pairs={{0,1},{2,3},{4,5},{6,7},{8,9},{10,11},{12,13},{14,15},{16,17},{18,... | collective-permute-start | bytes 6152 | tf_op jit(solution)/shard_map/ppermute | solution.py:251

commit v2 on v1

v2 whole, which is shorter than its diff:
```python
import math

import jax
import jax.numpy as jnp
from jax import lax
from jax.experimental import pallas as pl
from jax.experimental.pallas import tpu as pltpu
from jax.sharding import PartitionSpec as P

TILE = 128
GMAX = 4
SWEEPS = 3
NB = 6
TD = 16
EXT = TD + 2 * GMAX
ROWS = 17
GROUPS = 32
DEPTH = 8
CHUNK = 32
KERNEL_NORM = 21.0 / (16.0 * math.pi)
TIME_STEP = 0.05
VMEM_LIMIT = 8 * 1024 * 1024
F32 = jnp.float32
BF16 = jnp.bfloat16
VMEM = pltpu.MemorySpace.VMEM
SMEM = pltpu.MemorySpace.SMEM
AXES = ("group", "member")


def call(body, outs, scratch, name, *args, alias={}):
    specs = [
        pl.BlockSpec(memory_space=SMEM if a.dtype == jnp.int32 else VMEM) for a in args
    ]
    return pl.pallas_call(
        body,
        out_shape=[jax.ShapeDtypeStruct(shape, dtype) for shape, dtype in outs],
        in_specs=specs,
        out_specs=[pl.BlockSpec(memory_space=VMEM) for _ in outs],
        scratch_shapes=scratch,
        name=name,
        input_output_aliases=alias,
        compiler_params=pltpu.CompilerParams(vmem_limit_bytes=VMEM_LIMIT),
    )(*args)


def owner(segment):
    group, member = divmod(segment, 8)
    if member in (5, 6):
        group = group // DEPTH * DEPTH + (group + 1) % DEPTH
    elif member == 7:
        group = (group + 1) % GROUPS
    return group * 8 + member


def pack_body(mem, slot_hbm, part_hbm, out, count, slot, part, sem):
    groups = out.shape[0] // ROWS
    slots = pltpu.make_async_copy(slot_hbm, slot, sem.at[0])
    parts = pltpu.make_async_copy(part_hbm, part, sem.at[1])
    slots.start()
    parts.start()
    out[...] = jnp.zeros(out.shape, F32)
    for g in range(groups):
        count[g] = 0
        out[g * ROWS + 16 : g * ROWS + 17, :] = jnp.full((1, TILE), -1.0, F32)
    lane = lax.broadcasted_iota(jnp.int32, (1, TILE), 1)
    m = mem[0]
    slots.wait()
    parts.wait()
    for t in range(TD):
        s = slot[t]
        g = s // (TD * 8)
        along = (g // DEPTH) * DEPTH + (g + 1) % DEPTH
        g = jnp.where(m < 5, g, jnp.where(m < 7, along, (g + 1) % groups))
        n = count[g]
        count[g] = n + 1
        base = g * ROWS
        for r in range(8):
            out[pl.ds(base + n * 8 + r, 1), :] = part[r : r + 1, t * TILE : (t + 1) * TILE]
        label = pl.ds(base + 16, 1)
        here = (lane // (TILE // 2)) == n
        out[label, :] = jnp.where(here, (s % TD).astype(F32), out[label, :])


def split3(x):
    hi = x.astype(BF16).astype(F32)
    rest = x - hi
    mid = rest.astype(BF16).astype(F32)
    return hi, mid, rest - mid


def send_parts(odd, values, first, second):
    n = values.shape[-2]
    tail = values[..., n - GMAX :, :]
    head = values[..., :GMAX, :]
    first[...] = jnp.where(odd, tail, head)
    second[...] = jnp.where(odd, head, tail)


def extend(odd, values, first, second):
    left = jnp.where(odd, second, first)
    right = jnp.where(odd, first, second)
    return jnp.concatenate([values, left, right], axis=-2)


def unpack_body(mem, got, arranged, first, second):
    groups = got.shape[0] // ROWS
    odd = mem[0] % 2 == 1
    lane = lax.broadcasted_iota(jnp.int32, (groups, TILE), 1).astype(F32)
    labels = got[pl.ds(16, groups, stride=ROWS), :]
    marks = [
        jnp.where(values == lane, 1.0, 0.0)
        for values in (labels, pltpu.roll(labels, TILE // 2, 1))
    ]
    marks.append(jnp.zeros((TILE - 2 * groups, TILE), F32))
    choose = jnp.concatenate(marks, axis=0).T[:TD, : 2 * groups].astype(BF16)
    for r in range(8):
        tiles = jnp.concatenate(
            [got[pl.ds(n * 8 + r, groups, stride=ROWS), :] for n in range(2)], axis=0
        )
        moved = sum(
            jnp.dot(choose, piece.astype(BF16), preferred_element_type=F32)
            for piece in split3(tiles)
        )
        arranged[r] = moved
    send_parts(odd, arranged[0:6], first, second)


def place_of(entry, left):
    j = entry - left
    return jnp.where(j < 0, j + TD + GMAX, jnp.where(j < TD, j, j + GMAX))


def spread_columns(cols, fields, tiles, first):
    for f in range(5):
        turned = fields[f].T
        for t in range(tiles):
            cols[f, first + t] = jnp.broadcast_to(turned[:, t : t + 1], (TILE, TILE))


def columns_body(arranged, cols):
    spread_columns(cols, [arranged[f] for f in range(5)], TD, 0)


def density_body(mem, near, arranged, first, second, held, dens, ext, dist, out1, out2, cols):
    odd = mem[0] % 2 == 1
    whole = extend(odd, arranged[0:6], first[...], second[...])
    ext[...] = whole
    spread_columns(cols, [whole[f, TD:] for f in range(5)], 2 * GMAX, TD)

    def tile(s, carry):
        own = [arranged[f, pl.ds(s, 1), :] for f in range(5)]
        x_i, y_i, z_i, _, h_i = [jnp.broadcast_to(v, (CHUNK, TILE)) for v in own]
        pace = 2.0 / h_i
        total = jnp.zeros((CHUNK, TILE), F32)
        for n in range(NB):
            t = near[s * NB + n]
            for c in range(TILE // CHUNK):
                rows = pl.ds(c * CHUNK, CHUNK)
                dx = cols[0, t, rows, :] - x_i
                dy = cols[1, t, rows, :] - y_i
                dz = cols[2, t, rows, :] - z_i
                r2 = dx * dx + dy * dy + dz * dz
                r = r2 * lax.rsqrt(jnp.maximum(r2, 1e-30))
                dist[s, pl.ds(n * TILE + c * CHUNK, CHUNK), :] = r
                u = jnp.maximum(4.0 - r * pace, 0.0)
                u2 = u * u
                total = total + (cols[3, t, rows, :] * (5.0 - u)) * (u2 * u2)
        dens[pl.ds(s, 1), :] = jnp.sum(total, axis=0, keepdims=True)
        return carry

    lax.fori_loop(0, TD, tile, 0)
    h = arranged[4]
    density = (KERNEL_NORM / 256.0) * dens[...] / (h * h * h)
    dens[...] = density
    send_parts(odd, density, out1, out2)


def forces_body(near, arranged, cols, dist, forces):
    def tile(s, carry):
        h_i = jnp.broadcast_to(arranged[4, pl.ds(s, 1), :], (CHUNK, TILE))
        for n in range(NB):
            t = near[s * NB + n]
            for c in range(TILE // CHUNK):
                at = pl.ds(n * TILE + c * CHUNK, CHUNK)
                reach = cols[4, t, pl.ds(c * CHUNK, CHUNK), :] + h_i
                w = jnp.maximum(reach - dist[s, at, :], 0.0)
                p2 = reach * reach
                q = w / (p2 * p2)
                force = q * q * w
                high = force.astype(BF16)
                forces[s, at, 0:TILE] = high
                forces[s, at, TILE : 2 * TILE] = (force - high.astype(F32)).astype(BF16)
        return carry

    lax.fori_loop(0, TD, tile, 0)


def weigh(near, forces, vectors, staged, operand, result):
    count = len(vectors)
    height = staged.shape[0] // EXT
    pieces = [split3(v) for v in vectors]
    for k in range(3):
        for q in range(count):
            staged[pl.ds(k * count + q, EXT, stride=height), :] = pieces[q][k]
    for t in range(EXT):
        operand[t] = staged[t * height : (t + 1) * height, :].astype(BF16)
    for s in range(TD):
        row = jnp.concatenate([operand[near[s * NB + n]] for n in range(NB)], axis=1)
        got = jnp.dot(row, forces[s], preferred_element_type=F32)
        result[s * height : (s + 1) * height, :] = got[:, TILE:] + got[:, :TILE]
    sums = []
    for q in range(count):
        sums.append(
            sum(result[pl.ds(k * count + q, TD, stride=height), :] for k in (2, 1, 0))
        )
    return sums


def limiter_body(begin, *refs):
    if begin:
        (mem, near, arranged, ext, forces, dens, d1, d2) = refs[:8]
        (diff, out1, out2, sums, fixed, dens_ext, staged, operand, result) = refs[8:]
        odd = mem[0] % 2 == 1
        rho = extend(odd, dens[...], d1[...], d2[...])
        dens_ext[...] = rho
        e = ext[5]
    else:
        (mem, near, arranged, ext, forces, dens_ext, fixed, energy, e1, e2) = refs[:10]
        (diff, out1, out2, sums, ext_energy, staged, operand, result) = refs[10:]
        odd = mem[0] % 2 == 1
        rho = dens_ext[...]
        e = extend(odd, energy[...], e1[...], e2[...])
        ext_energy[...] = e
    v = (160.0 * KERNEL_NORM) * ext[3] / rho
    x = [ext[f] - 0.5 for f in range(3)]
    ve = v * e
    vectors = [ve] + [ve * x[f] for f in range(3)]
    if begin:
        vectors = vectors + [v] + [v * x[f] for f in range(3)]
    got = weigh(near, forces, vectors, staged, operand, result)
    if begin:
        for q in range(4):
            fixed[q] = got[4 + q]
    base = [fixed[q] for q in range(4)]
    e_i = e[:TD]
    square = jnp.zeros((TD, TILE), F32)
    for f in range(3):
        x_i = x[f][:TD]
        grad = (got[1 + f] - x_i * got[0]) - e_i * (base[1 + f] - x_i * base[0])
        square = square + grad * grad
    thick = arranged[6] * rho[:TD]
    ratio = jnp.sqrt(square) / (thick * e_i)
    value = (2.0 + ratio) / ((6.0 + 3.0 * ratio + ratio * ratio) * thick)
    diff[...] = value
    sums[0] = base[0]
    sums[1] = got[0]
    send_parts(odd, value, out1, out2)


def jacobi_body(last, mem, near, arranged, ext, forces, dens_ext, e_ext, sums, diff, d1, d2, *refs):
    if last:
        dens, new, staged, operand, result = refs
    else:
        new, out1, out2, staged, operand, result = refs
    odd = mem[0] % 2 == 1
    spread = extend(odd, diff[...], d1[...], d2[...])
    rho = dens_ext[...]
    vd = ((160.0 * KERNEL_NORM) * ext[3] / rho) * spread
    got = weigh(near, forces, [vd, vd * e_ext[...]], staged, operand, result)
    own = spread[:TD]
    scale = TIME_STEP / rho[:TD]
    rate = scale * (own * sums[0] + got[0])
    inflow = scale * (own * sums[1] + got[1])
    value = (arranged[5] + TIME_STEP * arranged[7] + inflow) / (1.0 + rate)
    new[:TD] = value
    if last:
        new[TD:] = dens[...]
    else:
        send_parts(odd, value, out1, out2)


def workspace(height):
    return [
        pltpu.VMEM((EXT * height, TILE), F32),
        pltpu.VMEM((EXT, height, TILE), BF16),
        pltpu.VMEM((TD * height, TILE), F32),
    ]


def swap(first, second):
    odd = [(owner(s), owner(s + 1)) for s in range(1, GROUPS * 8 - 1, 2)]
    even = [(owner(s), owner(s + 1)) for s in range(0, GROUPS * 8 - 1, 2)]
    got = []
    for value, pairs in ((first, odd), (second, even)):
        got.append(lax.ppermute(value, AXES, pairs + [(b, a) for a, b in pairs]))
    return got


def local(particles, new_slot, neighbours, ghosts):
    mem = lax.axis_index("member").astype(jnp.int32).reshape(1)
    outgoing = pl.pallas_call(
        pack_body,
        out_shape=jax.ShapeDtypeStruct((GROUPS * ROWS, TILE), F32),
        in_specs=[
            pl.BlockSpec(memory_space=SMEM),
            pl.BlockSpec(memory_space=pltpu.MemorySpace.HBM),
            pl.BlockSpec(memory_space=pltpu.MemorySpace.HBM),
        ],
        out_specs=pl.BlockSpec(memory_space=VMEM),
        scratch_shapes=[
            pltpu.SMEM((GROUPS,), jnp.int32),
            pltpu.SMEM((TD,), jnp.int32),
            pltpu.VMEM((8, TD * TILE), F32),
            pltpu.SemaphoreType.DMA((2,)),
        ],
        name="pack",
        compiler_params=pltpu.CompilerParams(vmem_limit_bytes=VMEM_LIMIT),
    )(mem, new_slot, particles)
    received = lax.all_to_all(
        outgoing.reshape(GROUPS * ROWS, 1, TILE), "group", split_axis=0, concat_axis=0, tiled=True
    )
    near = place_of(neighbours, ghosts[0, 0]).reshape(TD * NB)
    near = lax.ppermute(near, AXES, [(s, owner(s)) for s in range(GROUPS * 8)])
    edge = ((GMAX, TILE), F32)
    own = ((TD, TILE), F32)
    wide = ((EXT, TILE), F32)
    arranged, s1, s2 = call(
        unpack_body,
        [((8, TD, TILE), F32), ((6, GMAX, TILE), F32), ((6, GMAX, TILE), F32)],
        [],
        "unpack",
        mem,
        received.reshape(GROUPS * ROWS, TILE),
    )
    table = (mem, near)
    s1, s2 = swap(s1, s2)
    (cols,) = call(columns_body, [((5, EXT, TILE, TILE), F32)], [], "columns", arranged)
    density, ext, dist, r1, r2, cols = call(
        density_body,
        [
            own,
            ((6, EXT, TILE), F32),
            ((TD, NB * TILE, TILE), F32),
            edge,
            edge,
            ((5, EXT, TILE, TILE), F32),
        ],
        [],
        "density",
        *table,
        arranged,
        s1,
        s2,
        cols,
        alias={5: 5},
    )
    r1, r2 = swap(r1, r2)
    (forces,) = call(
        forces_body,
        [((TD, NB * TILE, 2 * TILE), BF16)],
        [],
        "forces",
        near,
        arranged,
        cols,
        dist,
    )
    shared = (*table, arranged, ext, forces)
    for step in range(SWEEPS):
        if step == 0:
            diff, d1, d2, sums, fixed, dens_ext = call(
                lambda *refs: limiter_body(True, *refs),
                [own, edge, edge, ((2, TD, TILE), F32), ((4, TD, TILE), F32), wide],
                workspace(24),
                "limiter_first",
                *shared,
                density,
                r1,
                r2,
            )
            e_ext = ext[5]
        else:
            diff, d1, d2, sums, e_ext = call(
                lambda *refs: limiter_body(False, *refs),
                [own, edge, edge, ((2, TD, TILE), F32), wide],
                workspace(16),
                "limiter",
                *shared,
                dens_ext,
                fixed,
                energy,
                e1,
                e2,
            )
        d1, d2 = swap(d1, d2)
        last = step == SWEEPS - 1
        results = call(
            lambda *refs: jacobi_body(last, *refs),
            [((2 * TD, TILE), F32)] if last else [own, edge, edge],
            workspace(8),
            "jacobi",
            *shared,
            dens_ext,
            e_ext,
            sums,
            diff,
            d1,
            d2,
            *((density,) if last else ()),
        )
        if last:
            done = results[0]
        else:
            energy, e1, e2 = results
            e1, e2 = swap(e1, e2)
    done = lax.ppermute(done, AXES, [(owner(s), s) for s in range(GROUPS * 8)])
    return (done[:TD].reshape(-1), done[TD:].reshape(-1))


def solution(mesh):
    in_specs = (
        P(None, ("group", "member")),
        P(("group", "member")),
        P(("group", "member"), None),
        P(("group", "member"), None),
    )
    out_specs = (P(("group", "member")), P(("group", "member")))
    return jax.shard_map(local, mesh=mesh, in_specs=in_specs, out_specs=out_specs, check_vma=False)
```

time: 118 us -> 101 us (0.86)
  the two profiles are of different devices: /device:TPU:2 before, /device:TPU:23 now
where the time goes in v2:
time: 101 us
  starting transfers between devices  30.6 us (30%)
  waiting for transfers between devices  24.2 us (24%)
  Pallas kernels  21.7 us (21%)
  blocking collectives  19.7 us (20%)
  local copies, waits for them, and re-layouts  2.27 us (2%)
  other arithmetic  1.34 us (1%)
    ppermute x14, starting transfers between devices, swap(): got.append(lax.ppermute(value, AXES, pairs + [(b, a) for a, b in pairs]))  25.3 us
    ppermute x14, waiting for transfers between devices, swap(): got.append(lax.ppermute(value, AXES, pairs + [(b, a) for a, b in pairs]))  21.1 us
    pallas_call x10, Pallas kernels, call(): pl.pallas_call(body, out_shape=[jax.ShapeDtypeStruct(shape, dtype) for sh...  20.8 us
    all_to_all x1, blocking collectives, local(): lax.all_to_all(outgoing.reshape(GROUPS * ROWS, 1, TILE), 'group', split_a...  19.7 us
    ppermute x1, starting transfers between devices, local(): near = lax.ppermute(near, AXES, [(s, owner(s)) for s in range(GROUPS * 8)])  3.37 us
    ppermute x1, waiting for transfers between devices, local(): done = lax.ppermute(done, AXES, [(owner(s), s) for s in range(GROUPS * 8)])  2.55 us
  transfers between devices with their start and end apart: 16, of which 13 were waited for; matrix products, arithmetic and copies ran while one was open for 2% of the time, Pallas kernels for 5%

profile of v2, /device:TPU:23, one launch (start us, length us, event | category | flops | bytes accessed | tf_op | source)
XLA Modules:
  0.0 100.6 jit_solution(11061112772206872193)
XLA Ops:
  2.1 0.9 pack.1
  3.0 19.7 %all_to_all.5 = f32[544,1,128]{2,1,0:T(1,128)S(1)} all-to-all(f32[544,1,128]{2,1,0:T(1,128)S(1)} %bitcast.14), channel_id=1, replica_groups=mesh['group'=32,'member'=8] {'group'}, dimensions={0} | all-to-all | bytes 557056 | tf_op jit(solution)/shard_map/all_to_all | solution.py:319
  23.0 6.0 %collective-permute-start.1 = (f32[6,4,128]{2,1,0:T(4,128)S(1)}, f32[6,4,128]{2,1,0:T(4,128)S(1)}, u32[]{:S(2)}, u32[]{:S(2)}) collective-permute-start(f32[6,4,128]{2,1,0:T(4,128)S(1)} %get-tuple-element.34), channel_id=1, source_target_pairs={{1,2},{3,4},{13,14},{15,8},{9,10},{11,12},{21,22},{23,16},{17,18},... | collective-permute-start | bytes 36872 | tf_op jit(solution)/shard_map/ppermute | solution.py:295
  29.1 1.3 %fusion = s32[16,6]{0,1:T(8,128)S(1)} fusion(s32[16,6]{0,1:T(8,128)} %param.6, s32[]{:T(128)} %bitcast.15), kind=kLoop, calls=%fused_computation.4 | loop fusion | flops 672 | bytes 772 | tf_op jit(solution)/shard_map/jit(_where)/select_n | solution.py:130
  30.6 3.4 %collective-permute-start = (s32[96]{0:T(128)S(1)}, s32[96]{0:T(128)S(1)}, u32[]{:S(2)}, u32[]{:S(2)}) collective-permute-start(s32[96]{0:T(128)S(1)} %reshape.23), channel_id=1, source_target_pairs={{0,0},{1,1},{2,2},{3,3},{4,4},{5,13},{6,14},{7,15},{8,8},{9,9},{10... | collective-permute-start | bytes 1160 | tf_op jit(solution)/shard_map/ppermute | solution.py:323
  34.0 1.6 %columns.1.held = f32[5,24,128,128]{3,2,1,0:T(8,128)S(1)} custom-call(f32[8,16,128]{2,1,0:T(8,128)S(1)} %get-tuple-element.33.arranged.refs_2_), custom_call_target="tpu_custom_call" | custom-call | tf_op jit(solution)/shard_map/columns/pallas_call | solution.py:34
  36.1 5.9 %density.1 = (f32[16,128]{1,0:T(8,128)S(1)}, f32[6,24,128]{2,1,0:T(8,128)S(1)}, f32[16,768,128]{2,1,0:T(8,128)S(1)}, f32[4,128]{1,0:T(4,128)S(1)}, f32[4,128]{1,...) custom-call(s32[1]{0:T(128)} %bitcast.mem.refs_0_, ...), custom_call_target="tpu_custom_call", output_to_operand_aliasing={{5}: (5, {})} | custom-call | tf_op jit(solution)/shard_map/density/pallas_call | solution.py:34
  42.1 3.1 %collective-permute-start.3 = (f32[4,128]{1,0:T(4,128)S(1)}, f32[4,128]{1,0:T(4,128)S(1)}, u32[]{:S(2)}, u32[]{:S(2)}) collective-permute-start(f32[4,128]{1,0:T(4,128)S(1)} %get-tuple-element.40), channel_id=1, source_target_pairs={{1,2},{3,4},{13,14},{15,8},{9,10},{11,12},{21,22},{23,16},{17,18},... | collective-permute-start | bytes 6152 | tf_op jit(solution)/shard_map/ppermute | solution.py:295
  45.2 3.5 %forces.1.refs_4_ = bf16[16,768,256]{2,1,0:T(8,128)(2,1)S(1)} custom-call(s32[96]{0:T(128)S(1)} %collective-permute-done.near.refs_1_, f32[8,16,128]{2,1,0:T(8,128)S(1)} %get-tuple-element.33.arranged.refs_2_, f32[5,24,128,128]{3,2,1,0:T(8,128)S(1)} %get-tuple-element.37.cols, f32[16,768,128]{2,1,0:T(8,128)S(1)} %get-tuple-element.38.dist), custom_call_target="tpu_custom_call" | custom-call | tf_op jit(solution)/shard_map/forces/pallas_call | solution.py:34
  49.4 1.8 %limiter_first.1 = (f32[16,128]{1,0:T(8,128)S(1)}, f32[4,128]{1,0:T(4,128)S(1)}, f32[4,128]{1,0:T(4,128)S(1)}, f32[2,16,128]{2,1,0:T(8,128)S(1)}, f32[4,16,128]{2,1,0:T(8,128)S(1)}, /*index=5*/f32[24,128]{1,0:T(8,128)S(1)}) custom-call(s32[1]{0:T(128)} %bitcast.mem.refs_0_, s32[96]{0:T(128)S(1)} %collective-permute-done.near.refs_1_, ...), custom_call_target="tpu_custom_call" | custom-call | tf_op jit(solution)/shard_map/limiter_first/pallas_call | solution.py:34
  51.3 3.8 %collective-permute-start.5 = (f32[4,128]{1,0:T(4,128)S(1)}, f32[4,128]{1,0:T(4,128)S(1)}, u32[]{:S(2)}, u32[]{:S(2)}) collective-permute-start(f32[4,128]{1,0:T(4,128)S(1)} %get-tuple-element.46), channel_id=1, source_target_pairs={{1,2},{3,4},{13,14},{15,8},{9,10},{11,12},{21,22},{23,16},{17,18},... | collective-permute-start | bytes 6152 | tf_op jit(solution)/shard_map/ppermute | solution.py:295
  55.5 0.8 collective-permute-done.5.refs_9_
  56.4 3.1 %collective-permute-done.6.refs_10_ = f32[4,128]{1,0:T(4,128)S(1)} collective-permute-done((f32[4,128]{1,0:T(4,128)S(1)}, f32[4,128]{1,0:T(4,128)S(1)}, u32[]{:S(2)}, u32[]{:S(2)}) %collective-permute-start.6) | collective-permute-done | bytes 2080 | tf_op jit(solution)/shard_map/ppermute | solution.py:295
  59.4 1.5 %jacobi.3 = (f32[16,128]{1,0:T(8,128)S(1)}, f32[4,128]{1,0:T(4,128)S(1)}, f32[4,128]{1,0:T(4,128)S(1)}) custom-call(s32[1]{0:T(128)} %bitcast.mem.refs_0_, s32[96]{0:T(128)S(1)} %collective-permute-done.near.refs_1_, f32[8,16,128]{2,1,0:T(8,128)S(1)} %get-tuple-element.33.arranged.refs_2_, f32[6,24,128]{2,1,0:T(8,128)S(1)} %get-tuple-element.36.refs_3_, ...), custom_call_target="tpu_custom_call" | custom-call | tf_op jit(solution)/shard_map/jacobi/pallas_call | solution.py:34
  60.9 1.9 %collective-permute-start.7 = (f32[4,128]{1,0:T(4,128)S(1)}, f32[4,128]{1,0:T(4,128)S(1)}, u32[]{:S(2)}, u32[]{:S(2)}) collective-permute-start(f32[4,128]{1,0:T(4,128)S(1)} %get-tuple-element.49), channel_id=1, source_target_pairs={{1,2},{3,4},{13,14},{15,8},{9,10},{11,12},{21,22},{23,16},{17,18},... | collective-permute-start | bytes 6152 | tf_op jit(solution)/shard_map/ppermute | solution.py:295
  63.3 2.6 %collective-permute-done.7.refs_8_ = f32[4,128]{1,0:T(4,128)S(1)} collective-permute-done((f32[4,128]{1,0:T(4,128)S(1)}, f32[4,128]{1,0:T(4,128)S(1)}, u32[]{:S(2)}, u32[]{:S(2)}) %collective-permute-start.7) | collective-permute-done | bytes 2080 | tf_op jit(solution)/shard_map/ppermute | solution.py:295
  65.9 1.3 %collective-permute-done.8.refs_9_ = f32[4,128]{1,0:T(4,128)S(1)} collective-permute-done((f32[4,128]{1,0:T(4,128)S(1)}, f32[4,128]{1,0:T(4,128)S(1)}, u32[]{:S(2)}, u32[]{:S(2)}) %collective-permute-start.8) | collective-permute-done | bytes 2080 | tf_op jit(solution)/shard_map/ppermute | solution.py:295
  67.2 1.6 %limiter.2 = (f32[16,128]{1,0:T(8,128)S(1)}, f32[4,128]{1,0:T(4,128)S(1)}, f32[4,128]{1,0:T(4,128)S(1)}, f32[2,16,128]{2,1,0:T(8,128)S(1)}, f32[24,128]{1,0:T(8,128)S(1)}) custom-call(s32[1]{0:T(128)} %bitcast.mem.refs_0_, s32[96]{0:T(128)S(1)} %collective-permute-done.near.refs_1_, f32[8,16,128]{2,1,0:T(8,128)S(1)} %get-tuple-element.33.arranged.refs_2_, ...), custom_call_target="tpu_custom_call" | custom-call | tf_op jit(solution)/shard_map/limiter/pallas_call | solution.py:34
  68.8 3.6 %collective-permute-start.9 = (f32[4,128]{1,0:T(4,128)S(1)}, f32[4,128]{1,0:T(4,128)S(1)}, u32[]{:S(2)}, u32[]{:S(2)}) collective-permute-start(f32[4,128]{1,0:T(4,128)S(1)} %get-tuple-element.54), channel_id=1, source_target_pairs={{1,2},{3,4},{13,14},{15,8},{9,10},{11,12},{21,22},{23,16},{17,18},... | collective-permute-start | bytes 6152 | tf_op jit(solution)/shard_map/ppermute | solution.py:295
  72.5 1.2 %collective-permute-done.9.refs_9_ = f32[4,128]{1,0:T(4,128)S(1)} collective-permute-done((f32[4,128]{1,0:T(4,128)S(1)}, f32[4,128]{1,0:T(4,128)S(1)}, u32[]{:S(2)}, u32[]{:S(2)}) %collective-permute-start.9) | collective-permute-done | bytes 2080 | tf_op jit(solution)/shard_map/ppermute | solution.py:295
  73.7 3.0 %collective-permute-done.10.refs_10_ = f32[4,128]{1,0:T(4,128)S(1)} collective-permute-done((f32[4,128]{1,0:T(4,128)S(1)}, f32[4,128]{1,0:T(4,128)S(1)}, u32[]{:S(2)}, u32[]{:S(2)}) %collective-permute-start.10) | collective-permute-done | bytes 2080 | tf_op jit(solution)/shard_map/ppermute | solution.py:295
  76.7 1.5 %jacobi.4 = (f32[16,128]{1,0:T(8,128)S(1)}, f32[4,128]{1,0:T(4,128)S(1)}, f32[4,128]{1,0:T(4,128)S(1)}) custom-call(s32[1]{0:T(128)} %bitcast.mem.refs_0_, s32[96]{0:T(128)S(1)} %collective-permute-done.near.refs_1_, f32[8,16,128]{2,1,0:T(8,128)S(1)} %get-tuple-element.33.arranged.refs_2_, f32[6,24,128]{2,1,0:T(8,128)S(1)} %get-tuple-element.36.refs_3_, ...), custom_call_target="tpu_custom_call" | custom-call | tf_op jit(solution)/shard_map/jacobi/pallas_call | solution.py:34
  78.2 1.9 %collective-permute-start.11 = (f32[4,128]{1,0:T(4,128)S(1)}, f32[4,128]{1,0:T(4,128)S(1)}, u32[]{:S(2)}, u32[]{:S(2)}) collective-permute-start(f32[4,128]{1,0:T(4,128)S(1)} %get-tuple-element.57), channel_id=1, source_target_pairs={{1,2},{3,4},{13,14},{15,8},{9,10},{11,12},{21,22},{23,16},{17,18},... | collective-permute-start | bytes 6152 | tf_op jit(solution)/shard_map/ppermute | solution.py:295
  80.3 2.8 %collective-permute-done.11.refs_8_ = f32[4,128]{1,0:T(4,128)S(1)} collective-permute-done((f32[4,128]{1,0:T(4,128)S(1)}, f32[4,128]{1,0:T(4,128)S(1)}, u32[]{:S(2)}, u32[]{:S(2)}) %collective-permute-start.11) | collective-permute-done | bytes 2080 | tf_op jit(solution)/shard_map/ppermute | solution.py:295
  83.1 1.3 %collective-permute-done.12.refs_9_ = f32[4,128]{1,0:T(4,128)S(1)} collective-permute-done((f32[4,128]{1,0:T(4,128)S(1)}, f32[4,128]{1,0:T(4,128)S(1)}, u32[]{:S(2)}, u32[]{:S(2)}) %collective-permute-start.12) | collective-permute-done | bytes 2080 | tf_op jit(solution)/shard_map/ppermute | solution.py:295
  84.5 1.6 %limiter.3 = (f32[16,128]{1,0:T(8,128)S(1)}, f32[4,128]{1,0:T(4,128)S(1)}, f32[4,128]{1,0:T(4,128)S(1)}, f32[2,16,128]{2,1,0:T(8,128)S(1)}, f32[24,128]{1,0:T(8,128)S(1)}) custom-call(s32[1]{0:T(128)} %bitcast.mem.refs_0_, s32[96]{0:T(128)S(1)} %collective-permute-done.near.refs_1_, f32[8,16,128]{2,1,0:T(8,128)S(1)} %get-tuple-element.33.arranged.refs_2_, ...), custom_call_target="tpu_custom_call" | custom-call | tf_op jit(solution)/shard_map/limiter/pallas_call | solution.py:34
  86.0 3.6 %collective-permute-start.13 = (f32[4,128]{1,0:T(4,128)S(1)}, f32[4,128]{1,0:T(4,128)S(1)}, u32[]{:S(2)}, u32[]{:S(2)}) collective-permute-start(f32[4,128]{1,0:T(4,128)S(1)} %get-tuple-element.62), channel_id=1, source_target_pairs={{1,2},{3,4},{13,14},{15,8},{9,10},{11,12},{21,22},{23,16},{17,18},... | collective-permute-start | bytes 6152 | tf_op jit(solution)/shard_map/ppermute | solution.py:295
  89.8 1.2 %collective-permute-done.13.refs_9_ = f32[4,128]{1,0:T(4,128)S(1)} collective-permute-done((f32[4,128]{1,0:T(4,128)S(1)}, f32[4,128]{1,0:T(4,128)S(1)}, u32[]{:S(2)}, u32[]{:S(2)}) %collective-permute-start.13) | collective-permute-done | bytes 2080 | tf_op jit(solution)/shard_map/ppermute | solution.py:295
  90.9 3.0 %collective-permute-done.14.refs_10_ = f32[4,128]{1,0:T(4,128)S(1)} collective-permute-done((f32[4,128]{1,0:T(4,128)S(1)}, f32[4,128]{1,0:T(4,128)S(1)}, u32[]{:S(2)}, u32[]{:S(2)}) %collective-permute-start.14) | collective-permute-done | bytes 2080 | tf_op jit(solution)/shard_map/ppermute | solution.py:295
  94.0 1.5 %jacobi.5 = f32[32,128]{1,0:T(8,128)S(1)} custom-call(s32[1]{0:T(128)} %bitcast.mem.refs_0_, s32[96]{0:T(128)S(1)} %collective-permute-done.near.refs_1_, f32[8,16,128]{2,1,0:T(8,128)S(1)} %get-tuple-element.33.arranged.refs_2_, f32[6,24,128]{2,1,0:T(8,128)S(1)} %get-tuple-element.36.refs_3_, bf16[16,768,256]{2,1,0:T(8,128)(2,1)S(1)} %forces.1.refs_4_, ...), custom_call_target="tpu_custom_call" | custom-call | tf_op jit(solution)/shard_map/jacobi/pallas_call | solution.py:34
  95.5 1.9 %collective-permute-start.15 = (f32[32,128]{1,0:T(8,128)S(1)}, f32[32,128]{1,0:T(8,128)S(1)}, u32[]{:S(2)}, u32[]{:S(2)}) collective-permute-start(f32[32,128]{1,0:T(8,128)S(1)} %jacobi.5), channel_id=1, source_target_pairs={{0,0},{1,1},{2,2},{3,3},{4,4},{13,5},{14,6},{15,7},{8,8},{9,9},{10... | collective-permute-start | bytes 49160 | tf_op jit(solution)/shard_map/ppermute | solution.py:416
  97.4 2.6 %collective-permute-done.15 = f32[32,128]{1,0:T(8,128)S(1)} collective-permute-done((f32[32,128]{1,0:T(8,128)S(1)}, f32[32,128]{1,0:T(8,128)S(1)}, u32[]{:S(2)}, u32[]{:S(2)}) %collective-permute-start.15) | collective-permute-done | bytes 16416 | tf_op jit(solution)/shard_map/ppermute | solution.py:416
  (21 shorter events, 5.1 us)
Async XLA Ops:
  0.6 0.8 copy-start
  1.5 0.7 copy-start.1
  23.0 13.1 %collective-permute-start.1 = (f32[6,4,128]{2,1,0:T(4,128)S(1)}, f32[6,4,128]{2,1,0:T(4,128)S(1)}, u32[]{:S(2)}, u32[]{:S(2)}) collective-permute-start(f32[6,4,128]{2,1,0:T(4,128)S(1)} %get-tuple-element.34), channel_id=1, source_target_pairs={{1,2},{3,4},{13,14},{15,8},{9,10},{11,12},{21,22},{23,16},{17,18},... | collective-permute-start | bytes 36872 | tf_op jit(solution)/shard_map/ppermute | solution.py:295
  29.0 7.1 %collective-permute-start.2 = (f32[6,4,128]{2,1,0:T(4,128)S(1)}, f32[6,4,128]{2,1,0:T(4,128)S(1)}, u32[]{:S(2)}, u32[]{:S(2)}) collective-permute-start(f32[6,4,128]{2,1,0:T(4,128)S(1)} %get-tuple-element.35), channel_id=1, source_target_pairs={{0,1},{2,3},{4,13},{14,15},{8,9},{10,11},{12,21},{22,23},{16,17},{... | collective-permute-start | bytes 36872 | tf_op jit(solution)/shard_map/ppermute | solution.py:295
  30.6 5.5 %collective-permute-start = (s32[96]{0:T(128)S(1)}, s32[96]{0:T(128)S(1)}, u32[]{:S(2)}, u32[]{:S(2)}) collective-permute-start(s32[96]{0:T(128)S(1)} %reshape.23), channel_id=1, source_target_pairs={{0,0},{1,1},{2,2},{3,3},{4,4},{5,13},{6,14},{7,15},{8,8},{9,9},{10... | collective-permute-start | bytes 1160 | tf_op jit(solution)/shard_map/ppermute | solution.py:323
  42.1 6.7 %collective-permute-start.3 = (f32[4,128]{1,0:T(4,128)S(1)}, f32[4,128]{1,0:T(4,128)S(1)}, u32[]{:S(2)}, u32[]{:S(2)}) collective-permute-start(f32[4,128]{1,0:T(4,128)S(1)} %get-tuple-element.40), channel_id=1, source_target_pairs={{1,2},{3,4},{13,14},{15,8},{9,10},{11,12},{21,22},{23,16},{17,18},... | collective-permute-start | bytes 6152 | tf_op jit(solution)/shard_map/ppermute | solution.py:295
  45.1 4.3 %collective-permute-start.4 = (f32[4,128]{1,0:T(4,128)S(1)}, f32[4,128]{1,0:T(4,128)S(1)}, u32[]{:S(2)}, u32[]{:S(2)}) collective-permute-start(f32[4,128]{1,0:T(4,128)S(1)} %get-tuple-element.41), channel_id=1, source_target_pairs={{0,1},{2,3},{4,13},{14,15},{8,9},{10,11},{12,21},{22,23},{16,17},{... | collective-permute-start | bytes 6152 | tf_op jit(solution)/shard_map/ppermute | solution.py:295
  51.3 5.1 %collective-permute-start.5 = (f32[4,128]{1,0:T(4,128)S(1)}, f32[4,128]{1,0:T(4,128)S(1)}, u32[]{:S(2)}, u32[]{:S(2)}) collective-permute-start(f32[4,128]{1,0:T(4,128)S(1)} %get-tuple-element.46), channel_id=1, source_target_pairs={{1,2},{3,4},{13,14},{15,8},{9,10},{11,12},{21,22},{23,16},{17,18},... | collective-permute-start | bytes 6152 | tf_op jit(solution)/shard_map/ppermute | solution.py:295
  55.1 4.3 %collective-permute-start.6 = (f32[4,128]{1,0:T(4,128)S(1)}, f32[4,128]{1,0:T(4,128)S(1)}, u32[]{:S(2)}, u32[]{:S(2)}) collective-permute-start(f32[4,128]{1,0:T(4,128)S(1)} %get-tuple-element.47), channel_id=1, source_target_pairs={{0,1},{2,3},{4,13},{14,15},{8,9},{10,11},{12,21},{22,23},{16,17},{... | collective-permute-start | bytes 6152 | tf_op jit(solution)/shard_map/ppermute | solution.py:295
  60.9 4.9 %collective-permute-start.7 = (f32[4,128]{1,0:T(4,128)S(1)}, f32[4,128]{1,0:T(4,128)S(1)}, u32[]{:S(2)}, u32[]{:S(2)}) collective-permute-start(f32[4,128]{1,0:T(4,128)S(1)} %get-tuple-element.49), channel_id=1, source_target_pairs={{1,2},{3,4},{13,14},{15,8},{9,10},{11,12},{21,22},{23,16},{17,18},... | collective-permute-start | bytes 6152 | tf_op jit(solution)/shard_map/ppermute | solution.py:295
  62.9 4.3 %collective-permute-start.8 = (f32[4,128]{1,0:T(4,128)S(1)}, f32[4,128]{1,0:T(4,128)S(1)}, u32[]{:S(2)}, u32[]{:S(2)}) collective-permute-start(f32[4,128]{1,0:T(4,128)S(1)} %get-tuple-element.50), channel_id=1, source_target_pairs={{0,1},{2,3},{4,13},{14,15},{8,9},{10,11},{12,21},{22,23},{16,17},{... | collective-permute-start | bytes 6152 | tf_op jit(solution)/shard_map/ppermute | solution.py:295
  68.8 4.9 %collective-permute-start.9 = (f32[4,128]{1,0:T(4,128)S(1)}, f32[4,128]{1,0:T(4,128)S(1)}, u32[]{:S(2)}, u32[]{:S(2)}) collective-permute-start(f32[4,128]{1,0:T(4,128)S(1)} %get-tuple-element.54), channel_id=1, source_target_pairs={{1,2},{3,4},{13,14},{15,8},{9,10},{11,12},{21,22},{23,16},{17,18},... | collective-permute-start | bytes 6152 | tf_op jit(solution)/shard_map/ppermute | solution.py:295
  72.4 4.3 %collective-permute-start.10 = (f32[4,128]{1,0:T(4,128)S(1)}, f32[4,128]{1,0:T(4,128)S(1)}, u32[]{:S(2)}, u32[]{:S(2)}) collective-permute-start(f32[4,128]{1,0:T(4,128)S(1)} %get-tuple-element.55), channel_id=1, source_target_pairs={{0,1},{2,3},{4,13},{14,15},{8,9},{10,11},{12,21},{22,23},{16,17},{... | collective-permute-start | bytes 6152 | tf_op jit(solution)/shard_map/ppermute | solution.py:295
  78.2 4.9 %collective-permute-start.11 = (f32[4,128]{1,0:T(4,128)S(1)}, f32[4,128]{1,0:T(4,128)S(1)}, u32[]{:S(2)}, u32[]{:S(2)}) collective-permute-start(f32[4,128]{1,0:T(4,128)S(1)} %get-tuple-element.57), channel_id=1, source_target_pairs={{1,2},{3,4},{13,14},{15,8},{9,10},{11,12},{21,22},{23,16},{17,18},... | collective-permute-start | bytes 6152 | tf_op jit(solution)/shard_map/ppermute | solution.py:295
  80.1 4.3 %collective-permute-start.12 = (f32[4,128]{1,0:T(4,128)S(1)}, f32[4,128]{1,0:T(4,128)S(1)}, u32[]{:S(2)}, u32[]{:S(2)}) collective-permute-start(f32[4,128]{1,0:T(4,128)S(1)} %get-tuple-element.58), channel_id=1, source_target_pairs={{0,1},{2,3},{4,13},{14,15},{8,9},{10,11},{12,21},{22,23},{16,17},{... | collective-permute-start | bytes 6152 | tf_op jit(solution)/shard_map/ppermute | solution.py:295
  86.0 4.9 %collective-permute-start.13 = (f32[4,128]{1,0:T(4,128)S(1)}, f32[4,128]{1,0:T(4,128)S(1)}, u32[]{:S(2)}, u32[]{:S(2)}) collective-permute-start(f32[4,128]{1,0:T(4,128)S(1)} %get-tuple-element.62), channel_id=1, source_target_pairs={{1,2},{3,4},{13,14},{15,8},{9,10},{11,12},{21,22},{23,16},{17,18},... | collective-permute-start | bytes 6152 | tf_op jit(solution)/shard_map/ppermute | solution.py:295
  89.7 4.3 %collective-permute-start.14 = (f32[4,128]{1,0:T(4,128)S(1)}, f32[4,128]{1,0:T(4,128)S(1)}, u32[]{:S(2)}, u32[]{:S(2)}) collective-permute-start(f32[4,128]{1,0:T(4,128)S(1)} %get-tuple-element.63), channel_id=1, source_target_pairs={{0,1},{2,3},{4,13},{14,15},{8,9},{10,11},{12,21},{22,23},{16,17},{... | collective-permute-start | bytes 6152 | tf_op jit(solution)/shard_map/ppermute | solution.py:295
  95.5 4.5 %collective-permute-start.15 = (f32[32,128]{1,0:T(8,128)S(1)}, f32[32,128]{1,0:T(8,128)S(1)}, u32[]{:S(2)}, u32[]{:S(2)}) collective-permute-start(f32[32,128]{1,0:T(8,128)S(1)} %jacobi.5), channel_id=1, source_target_pairs={{0,0},{1,1},{2,2},{3,3},{4,4},{13,5},{14,6},{15,7},{8,8},{9,9},{10... | collective-permute-start | bytes 49160 | tf_op jit(solution)/shard_map/ppermute | solution.py:416

commit v3 on v2

--- a/solution.py
+++ b/solution.py
@@ -16,6 +16,7 @@
 ROWS = 17
 GROUPS = 32
 DEPTH = 8
+LIST = 32
 CHUNK = 32
 KERNEL_NORM = 21.0 / (16.0 * math.pi)
 TIME_STEP = 0.05
@@ -52,32 +53,51 @@
     return group * 8 + member
 
 
-def pack_body(mem, slot_hbm, part_hbm, out, count, slot, part, sem):
-    groups = out.shape[0] // ROWS
-    slots = pltpu.make_async_copy(slot_hbm, slot, sem.at[0])
-    parts = pltpu.make_async_copy(part_hbm, part, sem.at[1])
-    slots.start()
-    parts.start()
+def moved_group(group, member):
+    along = (group // DEPTH) * DEPTH + (group + 1) % DEPTH
+    return jnp.where(member < 5, group, jnp.where(member < 7, along, (group + 1) % GROUPS))
+
+
+def home_group(group, member):
+    along = (group // DEPTH) * DEPTH + (group + DEPTH - 1) % DEPTH
+    far = (group + GROUPS - 1) % GROUPS
+    return jnp.where(member < 5, group, jnp.where(member < 7, along, far))
+
+
+def pack_body(grp, mem, ghosts_hbm, slot_hbm, near_hbm, part_hbm, out, count, ghosts, slot, near, part, sem):
+    copies = [
+        pltpu.make_async_copy(source, target, sem.at[k])
+        for k, (source, target) in enumerate(
+            [(ghosts_hbm, ghosts), (slot_hbm, slot), (near_hbm, near), (part_hbm, part)]
+        )
+    ]
+    for copy in copies:
+        copy.start()
     out[...] = jnp.zeros(out.shape, F32)
-    for g in range(groups):
+    for g in range(GROUPS):
         count[g] = 0
         out[g * ROWS + 16 : g * ROWS + 17, :] = jnp.full((1, TILE), -1.0, F32)
     lane = lax.broadcasted_iota(jnp.int32, (1, TILE), 1)
     m = mem[0]
-    slots.wait()
-    parts.wait()
+    for copy in copies:
+        copy.wait()
+    place = place_of(near[...], ghosts[0, 0]).astype(F32)
+    row = jnp.full((1, TILE), -1.0, F32)
+    for n in range(NB):
+        first = LIST + n * TD
+        piece = jnp.concatenate([place[n : n + 1], jnp.zeros((1, TILE - TD), F32)], axis=1)
+        row = jnp.where((lane >= first) & (lane < first + TD), pltpu.roll(piece, first, 1), row)
+    out[pl.ds(moved_group(grp[0], m) * ROWS + 16, 1), :] = row
     for t in range(TD):
         s = slot[t]
-        g = s // (TD * 8)
-        along = (g // DEPTH) * DEPTH + (g + 1) % DEPTH
-        g = jnp.where(m < 5, g, jnp.where(m < 7, along, (g + 1) % groups))
+        g = moved_group(s // (TD * 8), m)
         n = count[g]
         count[g] = n + 1
         base = g * ROWS
         for r in range(8):
             out[pl.ds(base + n * 8 + r, 1), :] = part[r : r + 1, t * TILE : (t + 1) * TILE]
         label = pl.ds(base + 16, 1)
-        here = (lane // (TILE // 2)) == n
+        here = (lane >= n * TD) & (lane < n * TD + TD)
         out[label, :] = jnp.where(here, (s % TD).astype(F32), out[label, :])
 
 
@@ -92,24 +112,24 @@
     n = values.shape[-2]
     tail = values[..., n - GMAX :, :]
     head = values[..., :GMAX, :]
-    first[...] = jnp.where(odd, tail, head)
-    second[...] = jnp.where(odd, head, tail)
+    first[...] = jnp.where(odd, head, tail)
+    second[...] = jnp.where(odd, tail, head)
 
 
 def extend(odd, values, first, second):
-    left = jnp.where(odd, second, first)
-    right = jnp.where(odd, first, second)
+    left = jnp.where(odd, first, second)
+    right = jnp.where(odd, second, first)
     return jnp.concatenate([values, left, right], axis=-2)
 
 
-def unpack_body(mem, got, arranged, first, second):
+def unpack_body(grp, mem, got, arranged, first, second, table):
     groups = got.shape[0] // ROWS
     odd = mem[0] % 2 == 1
     lane = lax.broadcasted_iota(jnp.int32, (groups, TILE), 1).astype(F32)
     labels = got[pl.ds(16, groups, stride=ROWS), :]
     marks = [
         jnp.where(values == lane, 1.0, 0.0)
-        for values in (labels, pltpu.roll(labels, TILE // 2, 1))
+        for values in (labels, pltpu.roll(labels, TILE - TD, 1))
     ]
     marks.append(jnp.zeros((TILE - 2 * groups, TILE), F32))
     choose = jnp.concatenate(marks, axis=0).T[:TD, : 2 * groups].astype(BF16)
@@ -122,6 +142,8 @@
             for piece in split3(tiles)
         )
         arranged[r] = moved
+    mine = pl.ds(home_group(grp[0], mem[0]) * ROWS + 16, 1)
+    table[...] = got[mine, :].astype(jnp.int32)
     send_parts(odd, arranged[0:6], first, second)
 
 
@@ -153,7 +175,7 @@
         pace = 2.0 / h_i
         total = jnp.zeros((CHUNK, TILE), F32)
         for n in range(NB):
-            t = near[s * NB + n]
+            t = near[0, LIST + n * TD + s]
             for c in range(TILE // CHUNK):
                 rows = pl.ds(c * CHUNK, CHUNK)
                 dx = cols[0, t, rows, :] - x_i
@@ -179,7 +201,7 @@
     def tile(s, carry):
         h_i = jnp.broadcast_to(arranged[4, pl.ds(s, 1), :], (CHUNK, TILE))
         for n in range(NB):
-            t = near[s * NB + n]
+            t = near[0, LIST + n * TD + s]
             for c in range(TILE // CHUNK):
                 at = pl.ds(n * TILE + c * CHUNK, CHUNK)
                 reach = cols[4, t, pl.ds(c * CHUNK, CHUNK), :] + h_i
@@ -205,7 +227,7 @@
     for t in range(EXT):
         operand[t] = staged[t * height : (t + 1) * height, :].astype(BF16)
     for s in range(TD):
-        row = jnp.concatenate([operand[near[s * NB + n]] for n in range(NB)], axis=1)
+        row = jnp.concatenate([operand[near[0, LIST + n * TD + s]] for n in range(NB)], axis=1)
         got = jnp.dot(row, forces[s], preferred_element_type=F32)
         result[s * height : (s + 1) * height, :] = got[:, TILE:] + got[:, :TILE]
     sums = []
@@ -291,44 +313,61 @@
     odd = [(owner(s), owner(s + 1)) for s in range(1, GROUPS * 8 - 1, 2)]
     even = [(owner(s), owner(s + 1)) for s in range(0, GROUPS * 8 - 1, 2)]
     got = []
-    for value, pairs in ((first, odd), (second, even)):
+    for value, pairs in ((first, even), (second, odd)):
         got.append(lax.ppermute(value, AXES, pairs + [(b, a) for a, b in pairs]))
     return got
 
 
 def local(particles, new_slot, neighbours, ghosts):
-    mem = lax.axis_index("member").astype(jnp.int32).reshape(1)
+    grp, mem = [lax.axis_index(axis).astype(jnp.int32).reshape(1) for axis in AXES]
+    hbm = pl.BlockSpec(memory_space=pltpu.MemorySpace.HBM)
     outgoing = pl.pallas_call(
         pack_body,
         out_shape=jax.ShapeDtypeStruct((GROUPS * ROWS, TILE), F32),
         in_specs=[
             pl.BlockSpec(memory_space=SMEM),
-            pl.BlockSpec(memory_space=pltpu.MemorySpace.HBM),
-            pl.BlockSpec(memory_space=pltpu.MemorySpace.HBM),
+            pl.BlockSpec(memory_space=SMEM),
+            hbm,
+            hbm,
+            hbm,
+            hbm,
         ],
         out_specs=pl.BlockSpec(memory_space=VMEM),
         scratch_shapes=[
             pltpu.SMEM((GROUPS,), jnp.int32),
+            pltpu.SMEM((1, 2), jnp.int32),
             pltpu.SMEM((TD,), jnp.int32),
+            pltpu.VMEM((NB, TD), jnp.int32),
             pltpu.VMEM((8, TD * TILE), F32),
-            pltpu.SemaphoreType.DMA((2,)),
+            pltpu.SemaphoreType.DMA((4,)),
         ],
         name="pack",
         compiler_params=pltpu.CompilerParams(vmem_limit_bytes=VMEM_LIMIT),
-    )(mem, new_slot, particles)
+    )(
+        grp,
+        mem,
+        *(
+            pltpu.with_memory_space_constraint(a, pltpu.MemorySpace.HBM)
+            for a in (ghosts, new_slot, neighbours.T, particles)
+        ),
+    )
     received = lax.all_to_all(
         outgoing.reshape(GROUPS * ROWS, 1, TILE), "group", split_axis=0, concat_axis=0, tiled=True
     )
-    near = place_of(neighbours, ghosts[0, 0]).reshape(TD * NB)
-    near = lax.ppermute(near, AXES, [(s, owner(s)) for s in range(GROUPS * 8)])
     edge = ((GMAX, TILE), F32)
     own = ((TD, TILE), F32)
     wide = ((EXT, TILE), F32)
-    arranged, s1, s2 = call(
+    arranged, s1, s2, near = call(
         unpack_body,
-        [((8, TD, TILE), F32), ((6, GMAX, TILE), F32), ((6, GMAX, TILE), F32)],
+        [
+            ((8, TD, TILE), F32),
+            ((6, GMAX, TILE), F32),
+            ((6, GMAX, TILE), F32),
+            ((1, TILE), jnp.int32),
+        ],
         [],
         "unpack",
+        grp,
         mem,
         received.reshape(GROUPS * ROWS, TILE),
     )

time: 101 us -> 93.7 us (0.928)
  the two profiles are of different devices: /device:TPU:23 before, /device:TPU:24 now
where the time goes in v3:
time: 93.7 us; the launch traced here: 93.3 us
  starting transfers between devices  32.6 us (35%)
  blocking collectives  23.8 us (25%)
  Pallas kernels  22.1 us (24%)
  waiting for transfers between devices  13.4 us (14%)
    ppermute x14, starting transfers between devices, swap(): got.append(lax.ppermute(value, AXES, pairs + [(b, a) for a, b in pairs]))  30.7 us
    all_to_all x1, blocking collectives, local(): lax.all_to_all(outgoing.reshape(GROUPS * ROWS, 1, TILE), 'group', split_a...  23.8 us
    pallas_call x10, Pallas kernels, call(): pl.pallas_call(body, out_shape=[jax.ShapeDtypeStruct(shape, dtype) for sh...  20.9 us
    ppermute x14, waiting for transfers between devices, swap(): got.append(lax.ppermute(value, AXES, pairs + [(b, a) for a, b in pairs]))  9.67 us
    ppermute x1, waiting for transfers between devices, local(): done = lax.ppermute(done, AXES, [(owner(s), s) for s in range(GROUPS * 8)])  3.7 us
    ppermute x1, starting transfers between devices, local(): done = lax.ppermute(done, AXES, [(owner(s), s) for s in range(GROUPS * 8)])  1.92 us
  transfers between devices with their start and end apart: 15, of which 7 were waited for; matrix products, arithmetic and copies ran while one was open for 0% of the time, Pallas kernels for 6%

profile of v3, /device:TPU:24, one launch (start us, length us, event | category | flops | bytes accessed | tf_op | source)
XLA Modules:
  0.0 93.3 jit_solution(9745149174465956946)
XLA Ops:
  0.6 1.2 %pack.1 = f32[544,128]{1,0:T(8,128)S(1)} custom-call(s32[1]{0:T(128)} %bitcast.1.grp, s32[1]{0:T(128)} %bitcast.mem.refs_0_, s32[1,2]{1,0:T(1,128)} %ghosts_hbm.1, s32[16]{0:T(128)} %slot_hbm.1, s32[6,16]{1,0:T(8,128)} %bitcast.15, f32[8,2048]{1,0:T(8,128)} %part_hbm.1), custom_call_target="tpu_custom_call" | custom-call | tf_op jit(solution)/shard_map/pack/pallas_call | solution.py:324
  1.9 23.8 %all_to_all.5 = f32[544,1,128]{2,1,0:T(1,128)S(1)} all-to-all(f32[544,1,128]{2,1,0:T(1,128)S(1)} %bitcast.14), channel_id=1, replica_groups=mesh['group'=32,'member'=8] {'group'}, dimensions={0} | all-to-all | bytes 557056 | tf_op jit(solution)/shard_map/all_to_all | solution.py:354
  26.0 2.6 %collective-permute-start.1 = (f32[6,4,128]{2,1,0:T(4,128)S(1)}, f32[6,4,128]{2,1,0:T(4,128)S(1)}, u32[]{:S(2)}, u32[]{:S(2)}) collective-permute-start(f32[6,4,128]{2,1,0:T(4,128)S(1)} %get-tuple-element.37), channel_id=1, source_target_pairs={{1,2},{3,4},{13,14},{15,8},{9,10},{11,12},{21,22},{23,16},{17,18},... | collective-permute-start | bytes 36872 | tf_op jit(solution)/shard_map/ppermute | solution.py:317
  28.7 1.6 %columns.1.held = f32[5,24,128,128]{3,2,1,0:T(8,128)S(1)} custom-call(f32[8,16,128]{2,1,0:T(8,128)S(1)} %get-tuple-element.35.arranged.refs_2_), custom_call_target="tpu_custom_call" | custom-call | tf_op jit(solution)/shard_map/columns/pallas_call | solution.py:35
  30.3 0.8 collective-permute-done.1.second
  31.1 5.9 %density.1 = (f32[16,128]{1,0:T(8,128)S(1)}, f32[6,24,128]{2,1,0:T(8,128)S(1)}, f32[16,768,128]{2,1,0:T(8,128)S(1)}, f32[4,128]{1,0:T(4,128)S(1)}, f32[4,128]{1,...) custom-call(s32[1]{0:T(128)} %bitcast.mem.refs_0_, ...), custom_call_target="tpu_custom_call", output_to_operand_aliasing={{5}: (5, {})} | custom-call | tf_op jit(solution)/shard_map/density/pallas_call | solution.py:35
  37.0 3.0 %collective-permute-start.2 = (f32[4,128]{1,0:T(4,128)S(1)}, f32[4,128]{1,0:T(4,128)S(1)}, u32[]{:S(2)}, u32[]{:S(2)}) collective-permute-start(f32[4,128]{1,0:T(4,128)S(1)} %get-tuple-element.42), channel_id=1, source_target_pairs={{0,1},{2,3},{4,13},{14,15},{8,9},{10,11},{12,21},{22,23},{16,17},{... | collective-permute-start | bytes 6152 | tf_op jit(solution)/shard_map/ppermute | solution.py:317
  40.0 1.9 %collective-permute-start.3 = (f32[4,128]{1,0:T(4,128)S(1)}, f32[4,128]{1,0:T(4,128)S(1)}, u32[]{:S(2)}, u32[]{:S(2)}) collective-permute-start(f32[4,128]{1,0:T(4,128)S(1)} %get-tuple-element.43), channel_id=1, source_target_pairs={{1,2},{3,4},{13,14},{15,8},{9,10},{11,12},{21,22},{23,16},{17,18},... | collective-permute-start | bytes 6152 | tf_op jit(solution)/shard_map/ppermute | solution.py:317
  41.9 3.6 %forces.1.refs_4_ = bf16[16,768,256]{2,1,0:T(8,128)(2,1)S(1)} custom-call(s32[1,128]{1,0:T(1,128)S(1)} %get-tuple-element.34.near.refs_1_, f32[8,16,128]{2,1,0:T(8,128)S(1)} %get-tuple-element.35.arranged.refs_2_, f32[5,24,128,128]{3,2,1,0:T(8,128)S(1)} %get-tuple-element.39.cols, f32[16,768,128]{2,1,0:T(8,128)S(1)} %get-tuple-element.40.dist), custom_call_target="tpu_custom_call" | custom-call | tf_op jit(solution)/shard_map/forces/pallas_call | solution.py:35
  45.5 1.8 %limiter_first.1 = (f32[16,128]{1,0:T(8,128)S(1)}, f32[4,128]{1,0:T(4,128)S(1)}, f32[4,128]{1,0:T(4,128)S(1)}, f32[2,16,128]{2,1,0:T(8,128)S(1)}, f32[4,16,128]{2,1,0:T(8,128)S(1)}, /*index=5*/f32[24,128]{1,0:T(8,128)S(1)}) custom-call(s32[1]{0:T(128)} %bitcast.mem.refs_0_, s32[1,128]{1,0:T(1,128)S(1)} %get-tuple-element.34.near.refs_1_, ...), custom_call_target="tpu_custom_call" | custom-call | tf_op jit(solution)/shard_map/limiter_first/pallas_call | solution.py:35
  47.3 0.7 collective-permute-start.4
  48.0 3.1 %collective-permute-start.5 = (f32[4,128]{1,0:T(4,128)S(1)}, f32[4,128]{1,0:T(4,128)S(1)}, u32[]{:S(2)}, u32[]{:S(2)}) collective-permute-start(f32[4,128]{1,0:T(4,128)S(1)} %get-tuple-element.49), channel_id=1, source_target_pairs={{1,2},{3,4},{13,14},{15,8},{9,10},{11,12},{21,22},{23,16},{17,18},... | collective-permute-start | bytes 6152 | tf_op jit(solution)/shard_map/ppermute | solution.py:317
  51.1 1.8 %collective-permute-done.5.refs_10_ = f32[4,128]{1,0:T(4,128)S(1)} collective-permute-done((f32[4,128]{1,0:T(4,128)S(1)}, f32[4,128]{1,0:T(4,128)S(1)}, u32[]{:S(2)}, u32[]{:S(2)}) %collective-permute-start.5) | collective-permute-done | bytes 2080 | tf_op jit(solution)/shard_map/ppermute | solution.py:317
  52.9 1.5 %jacobi.3 = (f32[16,128]{1,0:T(8,128)S(1)}, f32[4,128]{1,0:T(4,128)S(1)}, f32[4,128]{1,0:T(4,128)S(1)}) custom-call(s32[1]{0:T(128)} %bitcast.mem.refs_0_, s32[1,128]{1,0:T(1,128)S(1)} %get-tuple-element.34.near.refs_1_, f32[8,16,128]{2,1,0:T(8,128)S(1)} %get-tuple-element.35.arranged.refs_2_, f32[6,24,128]{2,1,0:T(8,128)S(1)} %get-tuple-element.38.refs_3_, ...), custom_call_target="tpu_custom_call" | custom-call | tf_op jit(solution)/shard_map/jacobi/pallas_call | solution.py:35
  54.4 2.4 %collective-permute-start.6 = (f32[4,128]{1,0:T(4,128)S(1)}, f32[4,128]{1,0:T(4,128)S(1)}, u32[]{:S(2)}, u32[]{:S(2)}) collective-permute-start(f32[4,128]{1,0:T(4,128)S(1)} %get-tuple-element.51), channel_id=1, source_target_pairs={{0,1},{2,3},{4,13},{14,15},{8,9},{10,11},{12,21},{22,23},{16,17},{... | collective-permute-start | bytes 6152 | tf_op jit(solution)/shard_map/ppermute | solution.py:317
  56.9 3.6 %collective-permute-start.7 = (f32[4,128]{1,0:T(4,128)S(1)}, f32[4,128]{1,0:T(4,128)S(1)}, u32[]{:S(2)}, u32[]{:S(2)}) collective-permute-start(f32[4,128]{1,0:T(4,128)S(1)} %get-tuple-element.52), channel_id=1, source_target_pairs={{1,2},{3,4},{13,14},{15,8},{9,10},{11,12},{21,22},{23,16},{17,18},... | collective-permute-start | bytes 6152 | tf_op jit(solution)/shard_map/ppermute | solution.py:317
  60.5 1.3 %collective-permute-done.7.refs_9_ = f32[4,128]{1,0:T(4,128)S(1)} collective-permute-done((f32[4,128]{1,0:T(4,128)S(1)}, f32[4,128]{1,0:T(4,128)S(1)}, u32[]{:S(2)}, u32[]{:S(2)}) %collective-permute-start.7) | collective-permute-done | bytes 2080 | tf_op jit(solution)/shard_map/ppermute | solution.py:317
  61.8 1.6 %limiter.2 = (f32[16,128]{1,0:T(8,128)S(1)}, f32[4,128]{1,0:T(4,128)S(1)}, f32[4,128]{1,0:T(4,128)S(1)}, f32[2,16,128]{2,1,0:T(8,128)S(1)}, f32[24,128]{1,0:T(8,128)S(1)}) custom-call(s32[1]{0:T(128)} %bitcast.mem.refs_0_, s32[1,128]{1,0:T(1,128)S(1)} %get-tuple-element.34.near.refs_1_, f32[8,16,128]{2,1,0:T(8,128)S(1)} %get-tuple-element.35.arranged.refs_2_, ...), custom_call_target="tpu_custom_call" | custom-call | tf_op jit(solution)/shard_map/limiter/pallas_call | solution.py:35
  63.4 1.3 %collective-permute-start.8 = (f32[4,128]{1,0:T(4,128)S(1)}, f32[4,128]{1,0:T(4,128)S(1)}, u32[]{:S(2)}, u32[]{:S(2)}) collective-permute-start(f32[4,128]{1,0:T(4,128)S(1)} %get-tuple-element.56), channel_id=1, source_target_pairs={{0,1},{2,3},{4,13},{14,15},{8,9},{10,11},{12,21},{22,23},{16,17},{... | collective-permute-start | bytes 6152 | tf_op jit(solution)/shard_map/ppermute | solution.py:317
  64.6 2.6 %collective-permute-start.9 = (f32[4,128]{1,0:T(4,128)S(1)}, f32[4,128]{1,0:T(4,128)S(1)}, u32[]{:S(2)}, u32[]{:S(2)}) collective-permute-start(f32[4,128]{1,0:T(4,128)S(1)} %get-tuple-element.57), channel_id=1, source_target_pairs={{1,2},{3,4},{13,14},{15,8},{9,10},{11,12},{21,22},{23,16},{17,18},... | collective-permute-start | bytes 6152 | tf_op jit(solution)/shard_map/ppermute | solution.py:317
  67.3 2.2 %collective-permute-done.9.refs_10_ = f32[4,128]{1,0:T(4,128)S(1)} collective-permute-done((f32[4,128]{1,0:T(4,128)S(1)}, f32[4,128]{1,0:T(4,128)S(1)}, u32[]{:S(2)}, u32[]{:S(2)}) %collective-permute-start.9) | collective-permute-done | bytes 2080 | tf_op jit(solution)/shard_map/ppermute | solution.py:317
  69.5 1.5 %jacobi.4 = (f32[16,128]{1,0:T(8,128)S(1)}, f32[4,128]{1,0:T(4,128)S(1)}, f32[4,128]{1,0:T(4,128)S(1)}) custom-call(s32[1]{0:T(128)} %bitcast.mem.refs_0_, s32[1,128]{1,0:T(1,128)S(1)} %get-tuple-element.34.near.refs_1_, f32[8,16,128]{2,1,0:T(8,128)S(1)} %get-tuple-element.35.arranged.refs_2_, f32[6,24,128]{2,1,0:T(8,128)S(1)} %get-tuple-element.38.refs_3_, ...), custom_call_target="tpu_custom_call" | custom-call | tf_op jit(solution)/shard_map/jacobi/pallas_call | solution.py:35
  71.0 1.8 %collective-permute-start.10 = (f32[4,128]{1,0:T(4,128)S(1)}, f32[4,128]{1,0:T(4,128)S(1)}, u32[]{:S(2)}, u32[]{:S(2)}) collective-permute-start(f32[4,128]{1,0:T(4,128)S(1)} %get-tuple-element.59), channel_id=1, source_target_pairs={{0,1},{2,3},{4,13},{14,15},{8,9},{10,11},{12,21},{22,23},{16,17},{... | collective-permute-start | bytes 6152 | tf_op jit(solution)/shard_map/ppermute | solution.py:317
  72.9 3.6 %collective-permute-start.11 = (f32[4,128]{1,0:T(4,128)S(1)}, f32[4,128]{1,0:T(4,128)S(1)}, u32[]{:S(2)}, u32[]{:S(2)}) collective-permute-start(f32[4,128]{1,0:T(4,128)S(1)} %get-tuple-element.60), channel_id=1, source_target_pairs={{1,2},{3,4},{13,14},{15,8},{9,10},{11,12},{21,22},{23,16},{17,18},... | collective-permute-start | bytes 6152 | tf_op jit(solution)/shard_map/ppermute | solution.py:317
  76.5 1.3 %collective-permute-done.11.refs_9_ = f32[4,128]{1,0:T(4,128)S(1)} collective-permute-done((f32[4,128]{1,0:T(4,128)S(1)}, f32[4,128]{1,0:T(4,128)S(1)}, u32[]{:S(2)}, u32[]{:S(2)}) %collective-permute-start.11) | collective-permute-done | bytes 2080 | tf_op jit(solution)/shard_map/ppermute | solution.py:317
  77.8 1.6 %limiter.3 = (f32[16,128]{1,0:T(8,128)S(1)}, f32[4,128]{1,0:T(4,128)S(1)}, f32[4,128]{1,0:T(4,128)S(1)}, f32[2,16,128]{2,1,0:T(8,128)S(1)}, f32[24,128]{1,0:T(8,128)S(1)}) custom-call(s32[1]{0:T(128)} %bitcast.mem.refs_0_, s32[1,128]{1,0:T(1,128)S(1)} %get-tuple-element.34.near.refs_1_, f32[8,16,128]{2,1,0:T(8,128)S(1)} %get-tuple-element.35.arranged.refs_2_, ...), custom_call_target="tpu_custom_call" | custom-call | tf_op jit(solution)/shard_map/limiter/pallas_call | solution.py:35
  79.3 1.3 %collective-permute-start.12 = (f32[4,128]{1,0:T(4,128)S(1)}, f32[4,128]{1,0:T(4,128)S(1)}, u32[]{:S(2)}, u32[]{:S(2)}) collective-permute-start(f32[4,128]{1,0:T(4,128)S(1)} %get-tuple-element.64), channel_id=1, source_target_pairs={{0,1},{2,3},{4,13},{14,15},{8,9},{10,11},{12,21},{22,23},{16,17},{... | collective-permute-start | bytes 6152 | tf_op jit(solution)/shard_map/ppermute | solution.py:317
  80.7 2.6 %collective-permute-start.13 = (f32[4,128]{1,0:T(4,128)S(1)}, f32[4,128]{1,0:T(4,128)S(1)}, u32[]{:S(2)}, u32[]{:S(2)}) collective-permute-start(f32[4,128]{1,0:T(4,128)S(1)} %get-tuple-element.65), channel_id=1, source_target_pairs={{1,2},{3,4},{13,14},{15,8},{9,10},{11,12},{21,22},{23,16},{17,18},... | collective-permute-start | bytes 6152 | tf_op jit(solution)/shard_map/ppermute | solution.py:317
  83.3 2.3 %collective-permute-done.13.refs_10_ = f32[4,128]{1,0:T(4,128)S(1)} collective-permute-done((f32[4,128]{1,0:T(4,128)S(1)}, f32[4,128]{1,0:T(4,128)S(1)}, u32[]{:S(2)}, u32[]{:S(2)}) %collective-permute-start.13) | collective-permute-done | bytes 2080 | tf_op jit(solution)/shard_map/ppermute | solution.py:317
  85.6 1.5 %jacobi.5 = f32[32,128]{1,0:T(8,128)S(1)} custom-call(s32[1]{0:T(128)} %bitcast.mem.refs_0_, s32[1,128]{1,0:T(1,128)S(1)} %get-tuple-element.34.near.refs_1_, f32[8,16,128]{2,1,0:T(8,128)S(1)} %get-tuple-element.35.arranged.refs_2_, f32[6,24,128]{2,1,0:T(8,128)S(1)} %get-tuple-element.38.refs_3_, bf16[16,768,256]{2,1,0:T(8,128)(2,1)S(1)} %forces.1.refs_4_, ...), custom_call_target="tpu_custom_call" | custom-call | tf_op jit(solution)/shard_map/jacobi/pallas_call | solution.py:35
  87.1 1.9 %collective-permute-start.14 = (f32[32,128]{1,0:T(8,128)S(1)}, f32[32,128]{1,0:T(8,128)S(1)}, u32[]{:S(2)}, u32[]{:S(2)}) collective-permute-start(f32[32,128]{1,0:T(8,128)S(1)} %jacobi.5), channel_id=1, source_target_pairs={{0,0},{1,1},{2,2},{3,3},{4,4},{13,5},{14,6},{15,7},{8,8},{9,9},{10... | collective-permute-start | bytes 49160 | tf_op jit(solution)/shard_map/ppermute | solution.py:455
  89.0 3.7 %collective-permute-done.14 = f32[32,128]{1,0:T(8,128)S(1)} collective-permute-done((f32[32,128]{1,0:T(8,128)S(1)}, f32[32,128]{1,0:T(8,128)S(1)}, u32[]{:S(2)}, u32[]{:S(2)}) %collective-permute-start.14) | collective-permute-done | bytes 16416 | tf_op jit(solution)/shard_map/ppermute | solution.py:455
  (12 shorter events, 1.0 us)
Async XLA Ops:
  26.0 4.3 %collective-permute-start = (f32[6,4,128]{2,1,0:T(4,128)S(1)}, f32[6,4,128]{2,1,0:T(4,128)S(1)}, u32[]{:S(2)}, u32[]{:S(2)}) collective-permute-start(f32[6,4,128]{2,1,0:T(4,128)S(1)} %get-tuple-element.36), channel_id=1, source_target_pairs={{0,1},{2,3},{4,13},{14,15},{8,9},{10,11},{12,21},{22,23},{16,17},{... | collective-permute-start | bytes 36872 | tf_op jit(solution)/shard_map/ppermute | solution.py:317
  26.0 5.0 %collective-permute-start.1 = (f32[6,4,128]{2,1,0:T(4,128)S(1)}, f32[6,4,128]{2,1,0:T(4,128)S(1)}, u32[]{:S(2)}, u32[]{:S(2)}) collective-permute-start(f32[6,4,128]{2,1,0:T(4,128)S(1)} %get-tuple-element.37), channel_id=1, source_target_pairs={{1,2},{3,4},{13,14},{15,8},{9,10},{11,12},{21,22},{23,16},{17,18},... | collective-permute-start | bytes 36872 | tf_op jit(solution)/shard_map/ppermute | solution.py:317
  37.0 8.5 %collective-permute-start.2 = (f32[4,128]{1,0:T(4,128)S(1)}, f32[4,128]{1,0:T(4,128)S(1)}, u32[]{:S(2)}, u32[]{:S(2)}) collective-permute-start(f32[4,128]{1,0:T(4,128)S(1)} %get-tuple-element.42), channel_id=1, source_target_pairs={{0,1},{2,3},{4,13},{14,15},{8,9},{10,11},{12,21},{22,23},{16,17},{... | collective-permute-start | bytes 6152 | tf_op jit(solution)/shard_map/ppermute | solution.py:317
  40.0 5.5 %collective-permute-start.3 = (f32[4,128]{1,0:T(4,128)S(1)}, f32[4,128]{1,0:T(4,128)S(1)}, u32[]{:S(2)}, u32[]{:S(2)}) collective-permute-start(f32[4,128]{1,0:T(4,128)S(1)} %get-tuple-element.43), channel_id=1, source_target_pairs={{1,2},{3,4},{13,14},{15,8},{9,10},{11,12},{21,22},{23,16},{17,18},... | collective-permute-start | bytes 6152 | tf_op jit(solution)/shard_map/ppermute | solution.py:317
  47.3 3.8 %collective-permute-start.4 = (f32[4,128]{1,0:T(4,128)S(1)}, f32[4,128]{1,0:T(4,128)S(1)}, u32[]{:S(2)}, u32[]{:S(2)}) collective-permute-start(f32[4,128]{1,0:T(4,128)S(1)} %get-tuple-element.48), channel_id=1, source_target_pairs={{0,1},{2,3},{4,13},{14,15},{8,9},{10,11},{12,21},{22,23},{16,17},{... | collective-permute-start | bytes 6152 | tf_op jit(solution)/shard_map/ppermute | solution.py:317
  48.0 4.9 %collective-permute-start.5 = (f32[4,128]{1,0:T(4,128)S(1)}, f32[4,128]{1,0:T(4,128)S(1)}, u32[]{:S(2)}, u32[]{:S(2)}) collective-permute-start(f32[4,128]{1,0:T(4,128)S(1)} %get-tuple-element.49), channel_id=1, source_target_pairs={{1,2},{3,4},{13,14},{15,8},{9,10},{11,12},{21,22},{23,16},{17,18},... | collective-permute-start | bytes 6152 | tf_op jit(solution)/shard_map/ppermute | solution.py:317
  54.4 6.1 %collective-permute-start.6 = (f32[4,128]{1,0:T(4,128)S(1)}, f32[4,128]{1,0:T(4,128)S(1)}, u32[]{:S(2)}, u32[]{:S(2)}) collective-permute-start(f32[4,128]{1,0:T(4,128)S(1)} %get-tuple-element.51), channel_id=1, source_target_pairs={{0,1},{2,3},{4,13},{14,15},{8,9},{10,11},{12,21},{22,23},{16,17},{... | collective-permute-start | bytes 6152 | tf_op jit(solution)/shard_map/ppermute | solution.py:317
  56.9 4.9 %collective-permute-start.7 = (f32[4,128]{1,0:T(4,128)S(1)}, f32[4,128]{1,0:T(4,128)S(1)}, u32[]{:S(2)}, u32[]{:S(2)}) collective-permute-start(f32[4,128]{1,0:T(4,128)S(1)} %get-tuple-element.52), channel_id=1, source_target_pairs={{1,2},{3,4},{13,14},{15,8},{9,10},{11,12},{21,22},{23,16},{17,18},... | collective-permute-start | bytes 6152 | tf_op jit(solution)/shard_map/ppermute | solution.py:317
  63.4 3.9 %collective-permute-start.8 = (f32[4,128]{1,0:T(4,128)S(1)}, f32[4,128]{1,0:T(4,128)S(1)}, u32[]{:S(2)}, u32[]{:S(2)}) collective-permute-start(f32[4,128]{1,0:T(4,128)S(1)} %get-tuple-element.56), channel_id=1, source_target_pairs={{0,1},{2,3},{4,13},{14,15},{8,9},{10,11},{12,21},{22,23},{16,17},{... | collective-permute-start | bytes 6152 | tf_op jit(solution)/shard_map/ppermute | solution.py:317
  64.6 4.9 %collective-permute-start.9 = (f32[4,128]{1,0:T(4,128)S(1)}, f32[4,128]{1,0:T(4,128)S(1)}, u32[]{:S(2)}, u32[]{:S(2)}) collective-permute-start(f32[4,128]{1,0:T(4,128)S(1)} %get-tuple-element.57), channel_id=1, source_target_pairs={{1,2},{3,4},{13,14},{15,8},{9,10},{11,12},{21,22},{23,16},{17,18},... | collective-permute-start | bytes 6152 | tf_op jit(solution)/shard_map/ppermute | solution.py:317
  71.0 5.4 %collective-permute-start.10 = (f32[4,128]{1,0:T(4,128)S(1)}, f32[4,128]{1,0:T(4,128)S(1)}, u32[]{:S(2)}, u32[]{:S(2)}) collective-permute-start(f32[4,128]{1,0:T(4,128)S(1)} %get-tuple-element.59), channel_id=1, source_target_pairs={{0,1},{2,3},{4,13},{14,15},{8,9},{10,11},{12,21},{22,23},{16,17},{... | collective-permute-start | bytes 6152 | tf_op jit(solution)/shard_map/ppermute | solution.py:317
  72.9 4.9 %collective-permute-start.11 = (f32[4,128]{1,0:T(4,128)S(1)}, f32[4,128]{1,0:T(4,128)S(1)}, u32[]{:S(2)}, u32[]{:S(2)}) collective-permute-start(f32[4,128]{1,0:T(4,128)S(1)} %get-tuple-element.60), channel_id=1, source_target_pairs={{1,2},{3,4},{13,14},{15,8},{9,10},{11,12},{21,22},{23,16},{17,18},... | collective-permute-start | bytes 6152 | tf_op jit(solution)/shard_map/ppermute | solution.py:317
  79.3 3.9 %collective-permute-start.12 = (f32[4,128]{1,0:T(4,128)S(1)}, f32[4,128]{1,0:T(4,128)S(1)}, u32[]{:S(2)}, u32[]{:S(2)}) collective-permute-start(f32[4,128]{1,0:T(4,128)S(1)} %get-tuple-element.64), channel_id=1, source_target_pairs={{0,1},{2,3},{4,13},{14,15},{8,9},{10,11},{12,21},{22,23},{16,17},{... | collective-permute-start | bytes 6152 | tf_op jit(solution)/shard_map/ppermute | solution.py:317
  80.7 4.9 %collective-permute-start.13 = (f32[4,128]{1,0:T(4,128)S(1)}, f32[4,128]{1,0:T(4,128)S(1)}, u32[]{:S(2)}, u32[]{:S(2)}) collective-permute-start(f32[4,128]{1,0:T(4,128)S(1)} %get-tuple-element.65), channel_id=1, source_target_pairs={{1,2},{3,4},{13,14},{15,8},{9,10},{11,12},{21,22},{23,16},{17,18},... | collective-permute-start | bytes 6152 | tf_op jit(solution)/shard_map/ppermute | solution.py:317
  87.1 5.6 %collective-permute-start.14 = (f32[32,128]{1,0:T(8,128)S(1)}, f32[32,128]{1,0:T(8,128)S(1)}, u32[]{:S(2)}, u32[]{:S(2)}) collective-permute-start(f32[32,128]{1,0:T(8,128)S(1)} %jacobi.5), channel_id=1, source_target_pairs={{0,0},{1,1},{2,2},{3,3},{4,4},{13,5},{14,6},{15,7},{8,8},{9,9},{10... | collective-permute-start | bytes 49160 | tf_op jit(solution)/shard_map/ppermute | solution.py:455

commit v4 on v3

--- a/solution.py
+++ b/solution.py
@@ -17,6 +17,7 @@
 GROUPS = 32
 DEPTH = 8
 LIST = 32
+HALF = TD // 2
 CHUNK = 32
 KERNEL_NORM = 21.0 / (16.0 * math.pi)
 TIME_STEP = 0.05
@@ -30,7 +31,7 @@
 
 def call(body, outs, scratch, name, *args, alias={}):
     specs = [
-        pl.BlockSpec(memory_space=SMEM if a.dtype == jnp.int32 else VMEM) for a in args
+        pl.BlockSpec(memory_space=SMEM if a.shape == (1,) else VMEM) for a in args
     ]
     return pl.pallas_call(
         body,
@@ -82,6 +83,9 @@
     for copy in copies:
         copy.wait()
     place = place_of(near[...], ghosts[0, 0]).astype(F32)
+    place = jnp.concatenate(
+        [place[:, GMAX : GMAX + HALF], place[:, :GMAX], place[:, GMAX + HALF :]], axis=1
+    )
     row = jnp.full((1, TILE), -1.0, F32)
     for n in range(NB):
         first = LIST + n * TD
@@ -98,7 +102,7 @@
             out[pl.ds(base + n * 8 + r, 1), :] = part[r : r + 1, t * TILE : (t + 1) * TILE]
         label = pl.ds(base + 16, 1)
         here = (lane >= n * TD) & (lane < n * TD + TD)
-        out[label, :] = jnp.where(here, (s % TD).astype(F32), out[label, :])
+        out[label, :] = jnp.where(here, rank(s % TD).astype(F32), out[label, :])
 
 
 def split3(x):
@@ -111,7 +115,7 @@
 def send_parts(odd, values, first, second):
     n = values.shape[-2]
     tail = values[..., n - GMAX :, :]
-    head = values[..., :GMAX, :]
+    head = values[..., n - HALF : n - GMAX, :]
     first[...] = jnp.where(odd, head, tail)
     second[...] = jnp.where(odd, tail, head)
 
@@ -149,7 +153,14 @@
 
 def place_of(entry, left):
     j = entry - left
-    return jnp.where(j < 0, j + TD + GMAX, jnp.where(j < TD, j, j + GMAX))
+    return jnp.where(j < 0, j + TD + GMAX, jnp.where(j < TD, rank(j), j + GMAX))
+
+
+def rank(tile):
+    return jnp.where(tile < GMAX, tile + HALF, jnp.where(tile < GMAX + HALF, tile - GMAX, tile))
+
+
+LISTED = [pltpu.SMEM((1, TILE), jnp.int32), pltpu.SemaphoreType.DMA]
 
 
 def spread_columns(cols, fields, tiles, first):
@@ -163,11 +174,16 @@
     spread_columns(cols, [arranged[f] for f in range(5)], TD, 0)
 
 
-def density_body(mem, near, arranged, first, second, held, dens, ext, dist, out1, out2, cols):
+def density_body(
+    mem, table, arranged, first, second, held, dens, ext, dist, out1, out2, cols, near, sem
+):
+    listed = pltpu.make_async_copy(table, near, sem)
+    listed.start()
     odd = mem[0] % 2 == 1
     whole = extend(odd, arranged[0:6], first[...], second[...])
     ext[...] = whole
     spread_columns(cols, [whole[f, TD:] for f in range(5)], 2 * GMAX, TD)
+    listed.wait()
 
     def tile(s, carry):
         own = [arranged[f, pl.ds(s, 1), :] for f in range(5)]
@@ -197,7 +213,11 @@
     send_parts(odd, density, out1, out2)
 
 
-def forces_body(near, arranged, cols, dist, forces):
+def forces_body(table, arranged, cols, dist, forces, near, sem):
+    listed = pltpu.make_async_copy(table, near, sem)
+    listed.start()
+    listed.wait()
+
     def tile(s, carry):
         h_i = jnp.broadcast_to(arranged[4, pl.ds(s, 1), :], (CHUNK, TILE))
         for n in range(NB):
@@ -217,96 +237,156 @@
     lax.fori_loop(0, TD, tile, 0)
 
 
-def weigh(near, forces, vectors, staged, operand, result):
+def prepare(vectors, staged, operand):
     count = len(vectors)
-    height = staged.shape[0] // EXT
+    height = operand.shape[1]
     pieces = [split3(v) for v in vectors]
     for k in range(3):
         for q in range(count):
             staged[pl.ds(k * count + q, EXT, stride=height), :] = pieces[q][k]
     for t in range(EXT):
         operand[t] = staged[t * height : (t + 1) * height, :].astype(BF16)
-    for s in range(TD):
+
+
+def weigh(listed, near, forces, operand, result, count, tiles):
+    height = operand.shape[1]
+    listed.wait()
+    for k, s in enumerate(tiles):
         row = jnp.concatenate([operand[near[0, LIST + n * TD + s]] for n in range(NB)], axis=1)
         got = jnp.dot(row, forces[s], preferred_element_type=F32)
-        result[s * height : (s + 1) * height, :] = got[:, TILE:] + got[:, :TILE]
+        result[k * height : (k + 1) * height, :] = got[:, TILE:] + got[:, :TILE]
     sums = []
     for q in range(count):
-        sums.append(
-            sum(result[pl.ds(k * count + q, TD, stride=height), :] for k in (2, 1, 0))
-        )
+        parts = [result[pl.ds(k * count + q, len(tiles), stride=height), :] for k in (2, 1, 0)]
+        sums.append(parts[0] + parts[1] + parts[2])
     return sums
 
 
-def limiter_body(begin, *refs):
+def start_list(table, near, sem):
+    listed = pltpu.make_async_copy(table, near, sem)
+    listed.start()
+    return listed
+
+
+def limit(got, base, x, e, kappa, rho):
+    square = jnp.zeros(e.shape, F32)
+    for f in range(3):
+        grad = (got[1 + f] - x[f] * got[0]) - e * (base[1 + f] - x[f] * base[0])
+        square = square + grad * grad
+    thick = kappa * rho
+    ratio = jnp.sqrt(square) / (thick * e)
+    return (2.0 + ratio) / ((6.0 + 3.0 * ratio + ratio * ratio) * thick)
+
+
+INNER = range(HALF)
+EDGE = range(HALF, TD)
+
+
+def limiter_part(tiles, begin, listed, near, arranged, ext, forces, rho, e, fixed, operand, result, diff, sums):
+    rows = slice(tiles[0], tiles[-1] + 1)
+    got = weigh(listed, near, forces, operand, result, 8 if begin else 4, tiles)
     if begin:
-        (mem, near, arranged, ext, forces, dens, d1, d2) = refs[:8]
-        (diff, out1, out2, sums, fixed, dens_ext, staged, operand, result) = refs[8:]
+        for q in range(4):
+            fixed[q] = got[4 + q]
+    base = [fixed[q] for q in range(4)]
+    x = [ext[f, rows] - 0.5 for f in range(3)]
+    value = limit(got, base, x, e[rows], arranged[6, rows], rho[rows])
+    diff[...] = value
+    sums[0] = base[0]
+    sums[1] = got[0]
+    return value
+
+
+def limiter_edge(begin, *refs):
+    *refs, staged, result, near, sem = refs
+    listed = start_list(refs[1], near, sem)
+    if begin:
+        (mem, _, arranged, ext, forces, dens, d1, d2) = refs[:8]
+        (diff, out1, out2, sums, operand, fixed, dens_ext) = refs[8:]
         odd = mem[0] % 2 == 1
         rho = extend(odd, dens[...], d1[...], d2[...])
         dens_ext[...] = rho
         e = ext[5]
     else:
-        (mem, near, arranged, ext, forces, dens_ext, fixed, energy, e1, e2) = refs[:10]
-        (diff, out1, out2, sums, ext_energy, staged, operand, result) = refs[10:]
+        (mem, _, arranged, ext, forces, dens_ext, fixed, e_inner, e_edge, e1, e2) = refs[:11]
+        (diff, out1, out2, sums, operand, e_ext) = refs[11:]
         odd = mem[0] % 2 == 1
         rho = dens_ext[...]
-        e = extend(odd, energy[...], e1[...], e2[...])
-        ext_energy[...] = e
+        e = extend(odd, jnp.concatenate([e_inner[...], e_edge[...]], axis=0), e1[...], e2[...])
+        e_ext[...] = e
     v = (160.0 * KERNEL_NORM) * ext[3] / rho
     x = [ext[f] - 0.5 for f in range(3)]
     ve = v * e
     vectors = [ve] + [ve * x[f] for f in range(3)]
     if begin:
         vectors = vectors + [v] + [v * x[f] for f in range(3)]
-    got = weigh(near, forces, vectors, staged, operand, result)
+    prepare(vectors, staged, operand)
+    value = limiter_part(
+        EDGE, begin, listed, near, arranged, ext, forces, rho, e, fixed, operand, result, diff, sums
+    )
+    send_parts(odd, value, out1, out2)
+
+
+def limiter_inner(begin, *refs):
+    *refs, result, near, sem = refs
+    listed = start_list(refs[0], near, sem)
+    (_, arranged, ext, forces, rho, e_ext, operand) = refs[:7]
     if begin:
-        for q in range(4):
-            fixed[q] = got[4 + q]
-    base = [fixed[q] for q in range(4)]
-    e_i = e[:TD]
-    square = jnp.zeros((TD, TILE), F32)
-    for f in range(3):
-        x_i = x[f][:TD]
-        grad = (got[1 + f] - x_i * got[0]) - e_i * (base[1 + f] - x_i * base[0])
-        square = square + grad * grad
-    thick = arranged[6] * rho[:TD]
-    ratio = jnp.sqrt(square) / (thick * e_i)
-    value = (2.0 + ratio) / ((6.0 + 3.0 * ratio + ratio * ratio) * thick)
-    diff[...] = value
-    sums[0] = base[0]
-    sums[1] = got[0]
-    send_parts(odd, value, out1, out2)
-
-
-def jacobi_body(last, mem, near, arranged, ext, forces, dens_ext, e_ext, sums, diff, d1, d2, *refs):
-    if last:
-        dens, new, staged, operand, result = refs
+        diff, sums, fixed = refs[7:]
+        e = e_ext[5]
     else:
-        new, out1, out2, staged, operand, result = refs
-    odd = mem[0] % 2 == 1
-    spread = extend(odd, diff[...], d1[...], d2[...])
-    rho = dens_ext[...]
-    vd = ((160.0 * KERNEL_NORM) * ext[3] / rho) * spread
-    got = weigh(near, forces, [vd, vd * e_ext[...]], staged, operand, result)
-    own = spread[:TD]
-    scale = TIME_STEP / rho[:TD]
+        fixed, diff, sums = refs[7:]
+        e = e_ext[...]
+    limiter_part(
+        INNER, begin, listed, near, arranged, ext, forces, rho, e, fixed, operand, result, diff, sums
+    )
+
+
+def step_energy(arranged, rows, rho, sums, own, got):
+    scale = TIME_STEP / rho[rows]
     rate = scale * (own * sums[0] + got[0])
     inflow = scale * (own * sums[1] + got[1])
-    value = (arranged[5] + TIME_STEP * arranged[7] + inflow) / (1.0 + rate)
-    new[:TD] = value
+    return (arranged[5, rows] + TIME_STEP * arranged[7, rows] + inflow) / (1.0 + rate)
+
+
+def jacobi_edge(last, *refs):
+    *refs, staged, result, near, sem = refs
+    listed = start_list(refs[1], near, sem)
+    (mem, _, arranged, ext, forces, rho, e_ext, inner_sums, sums, inner, edge, d1, d2) = refs[:13]
+    odd = mem[0] % 2 == 1
+    own = jnp.concatenate([inner[...], edge[...]], axis=0)
+    spread = extend(odd, own, d1[...], d2[...])
+    vd = ((160.0 * KERNEL_NORM) * ext[3] / rho[...]) * spread
+    e = e_ext[5] if len(e_ext.shape) == 3 else e_ext[...]
     if last:
-        new[TD:] = dens[...]
+        dens, done, operand = refs[13:]
     else:
+        new, out1, out2, operand = refs[13:]
+    prepare([vd, vd * e], staged, operand)
+    if last:
+        got = weigh(listed, near, forces, operand, result, 2, range(TD))
+        both = [jnp.concatenate([inner_sums[q], sums[q]], axis=0) for q in range(2)]
+        value = step_energy(arranged, slice(0, TD), rho, both, own, got)
+        for k, v in enumerate((value, dens[...])):
+            done[k * TD : k * TD + GMAX] = v[HALF : HALF + GMAX]
+            done[k * TD + GMAX : k * TD + GMAX + HALF] = v[:HALF]
+            done[k * TD + GMAX + HALF : (k + 1) * TD] = v[HALF + GMAX :]
+    else:
+        got = weigh(listed, near, forces, operand, result, 2, EDGE)
+        value = step_energy(arranged, slice(HALF, TD), rho, sums, edge[...], got)
+        new[...] = value
         send_parts(odd, value, out1, out2)
 
 
-def workspace(height):
-    return [
-        pltpu.VMEM((EXT * height, TILE), F32),
-        pltpu.VMEM((EXT, height, TILE), BF16),
-        pltpu.VMEM((TD * height, TILE), F32),
-    ]
+def jacobi_inner(table, arranged, forces, rho, operand, sums, inner, new, result, near, sem):
+    listed = start_list(table, near, sem)
+    got = weigh(listed, near, forces, operand, result, 2, INNER)
+    new[...] = step_energy(arranged, slice(0, HALF), rho, sums, inner[...], got)
+
+
+def workspace(height, tiles, staged):
+    stage = [pltpu.VMEM((EXT * height, TILE), F32)] if staged else []
+    return stage + [pltpu.VMEM((tiles * height, TILE), F32), *LISTED]
 
 
 def swap(first, second):
@@ -384,7 +464,7 @@
             edge,
             ((5, EXT, TILE, TILE), F32),
         ],
-        [],
+        LISTED,
         "density",
         *table,
         arranged,
@@ -397,7 +477,7 @@
     (forces,) = call(
         forces_body,
         [((TD, NB * TILE, 2 * TILE), BF16)],
-        [],
+        LISTED,
         "forces",
         near,
         arranged,
@@ -405,43 +485,71 @@
         dist,
     )
     shared = (*table, arranged, ext, forces)
+    half = ((HALF, TILE), F32)
+    pair = ((2, HALF, TILE), F32)
+    four = ((4, HALF, TILE), F32)
     for step in range(SWEEPS):
-        if step == 0:
-            diff, d1, d2, sums, fixed, dens_ext = call(
-                lambda *refs: limiter_body(True, *refs),
-                [own, edge, edge, ((2, TD, TILE), F32), ((4, TD, TILE), F32), wide],
-                workspace(24),
-                "limiter_first",
+        begin = step == 0
+        height = 24 if begin else 16
+        operand = ((EXT, height, TILE), BF16)
+        if begin:
+            diff, d1, d2, sums, rows, fixed, dens_ext = call(
+                lambda *refs: limiter_edge(True, *refs),
+                [half, edge, edge, pair, operand, four, wide],
+                workspace(height, HALF, True),
+                "limiter_first_edge",
                 *shared,
                 density,
                 r1,
                 r2,
             )
-            e_ext = ext[5]
+            e_ext = ext
         else:
-            diff, d1, d2, sums, e_ext = call(
-                lambda *refs: limiter_body(False, *refs),
-                [own, edge, edge, ((2, TD, TILE), F32), wide],
-                workspace(16),
-                "limiter",
+            diff, d1, d2, sums, rows, e_ext = call(
+                lambda *refs: limiter_edge(False, *refs),
+                [half, edge, edge, pair, operand, wide],
+                workspace(height, HALF, True),
+                "limiter_edge",
                 *shared,
                 dens_ext,
                 fixed,
-                energy,
+                e_inner,
+                e_edge,
                 e1,
                 e2,
             )
         d1, d2 = swap(d1, d2)
+        results = call(
+            lambda *refs: limiter_inner(begin, *refs),
+            [half, pair, four] if begin else [half, pair],
+            workspace(height, HALF, False),
+            "limiter_first_inner" if begin else "limiter_inner",
+            near,
+            arranged,
+            ext,
+            forces,
+            dens_ext,
+            e_ext,
+            rows,
+            *(() if begin else (inner_fixed,)),
+        )
+        if begin:
+            inner_diff, inner_sums, inner_fixed = results
+        else:
+            inner_diff, inner_sums = results
         last = step == SWEEPS - 1
+        operand = ((EXT, 8, TILE), BF16)
         results = call(
-            lambda *refs: jacobi_body(last, *refs),
-            [((2 * TD, TILE), F32)] if last else [own, edge, edge],
-            workspace(8),
-            "jacobi",
+            lambda *refs: jacobi_edge(last, *refs),
+            [((2 * TD, TILE), F32), operand] if last else [half, edge, edge, operand],
+            workspace(8, TD if last else HALF, True),
+            "jacobi_last" if last else "jacobi_edge",
             *shared,
             dens_ext,
             e_ext,
+            inner_sums,
             sums,
+            inner_diff,
             diff,
             d1,
             d2,
@@ -450,8 +558,21 @@
         if last:
             done = results[0]
         else:
-            energy, e1, e2 = results
+            e_edge, e1, e2, rows = results
             e1, e2 = swap(e1, e2)
+            (e_inner,) = call(
+                jacobi_inner,
+                [half],
+                workspace(8, HALF, False),
+                "jacobi_inner",
+                near,
+                arranged,
+                forces,
+                dens_ext,
+                rows,
+                inner_sums,
+                inner_diff,
+            )
     done = lax.ppermute(done, AXES, [(owner(s), s) for s in range(GROUPS * 8)])
     return (done[:TD].reshape(-1), done[TD:].reshape(-1))
 

time: 93.7 us -> 91.4 us (0.975)
  waiting for transfers between devices: 13.4 us -> 7.58 us
  Pallas kernels: 22.1 us -> 25.5 us
    ppermute x14, waiting for transfers between devices: 9.67 us -> 3.88 us  [swap(): got.append(lax.ppermute(value, AXES, pairs + [(b, a) for a, b in pairs]))]
    pallas_call x10 -> x15, Pallas kernels: 20.9 us -> 24.2 us  [call(): pl.pallas_call(body, out_shape=[jax.ShapeDtypeStruct(shape, dtype) for sh...]
  transfers between devices with their start and end apart: 15 -> 15, of which waited for: 7 -> 7; matrix products, arithmetic and copies ran while one was open for 0% -> 0% of each run, Pallas kernels for 6% -> 12%
where the time goes in v4:
time: 91.4 us; the launch traced here: 91 us
  starting transfers between devices  32.7 us (36%)
  Pallas kernels  25.5 us (28%)
  blocking collectives  23.8 us (26%)
  waiting for transfers between devices  7.58 us (8%)
    ppermute x14, starting transfers between devices, swap(): got.append(lax.ppermute(value, AXES, pairs + [(b, a) for a, b in pairs]))  30.8 us
    pallas_call x15, Pallas kernels, call(): pl.pallas_call(body, out_shape=[jax.ShapeDtypeStruct(shape, dtype) for sh...  24.2 us
    all_to_all x1, blocking collectives, local(): lax.all_to_all(outgoing.reshape(GROUPS * ROWS, 1, TILE), 'group', split_a...  23.8 us
    ppermute x14, waiting for transfers between devices, swap(): got.append(lax.ppermute(value, AXES, pairs + [(b, a) for a, b in pairs]))  3.88 us
    ppermute x1, waiting for transfers between devices, local(): done = lax.ppermute(done, AXES, [(owner(s), s) for s in range(GROUPS * 8)])  3.7 us
    ppermute x1, starting transfers between devices, local(): done = lax.ppermute(done, AXES, [(owner(s), s) for s in range(GROUPS * 8)])  1.92 us
  transfers between devices with their start and end apart: 15, of which 7 were waited for; matrix products, arithmetic and copies ran while one was open for 0% of the time, Pallas kernels for 12%

profile of v4, /device:TPU:24, one launch (start us, length us, event | category | flops | bytes accessed | tf_op | source)
XLA Modules:
  0.0 91.0 jit_solution(18134402830847488381)
XLA Ops:
  0.6 1.3 %pack.1 = f32[544,128]{1,0:T(8,128)S(1)} custom-call(s32[1]{0:T(128)} %bitcast.1.grp, s32[1]{0:T(128)} %bitcast.mem.refs_0_, s32[1,2]{1,0:T(1,128)} %ghosts_hbm.1, s32[16]{0:T(128)} %slot_hbm.1, s32[6,16]{1,0:T(8,128)} %bitcast.13, f32[8,2048]{1,0:T(8,128)} %part_hbm.1), custom_call_target="tpu_custom_call" | custom-call | tf_op jit(solution)/shard_map/pack/pallas_call | solution.py:404
  2.0 23.8 %all_to_all.5 = f32[544,1,128]{2,1,0:T(1,128)S(1)} all-to-all(f32[544,1,128]{2,1,0:T(1,128)S(1)} %bitcast.12), channel_id=1, replica_groups=mesh['group'=32,'member'=8] {'group'}, dimensions={0} | all-to-all | bytes 557056 | tf_op jit(solution)/shard_map/all_to_all | solution.py:434
  26.1 2.6 %collective-permute-start.1 = (f32[6,4,128]{2,1,0:T(4,128)S(1)}, f32[6,4,128]{2,1,0:T(4,128)S(1)}, u32[]{:S(2)}, u32[]{:S(2)}) collective-permute-start(f32[6,4,128]{2,1,0:T(4,128)S(1)} %get-tuple-element.50), channel_id=1, source_target_pairs={{1,2},{3,4},{13,14},{15,8},{9,10},{11,12},{21,22},{23,16},{17,18},... | collective-permute-start | bytes 36872 | tf_op jit(solution)/shard_map/ppermute | solution.py:397
  28.8 1.6 %columns.1.held = f32[5,24,128,128]{3,2,1,0:T(8,128)S(1)} custom-call(f32[8,16,128]{2,1,0:T(8,128)S(1)} %get-tuple-element.48.arranged.refs_2_.refs_1_), custom_call_target="tpu_custom_call" | custom-call | tf_op jit(solution)/shard_map/columns/pallas_call | solution.py:36
  31.1 5.4 %density.1 = (f32[16,128]{1,0:T(8,128)S(1)}, f32[6,24,128]{2,1,0:T(8,128)S(1)}, f32[16,768,128]{2,1,0:T(8,128)S(1)}, f32[4,128]{1,0:T(4,128)S(1)}, f32[4,128]{1,...) custom-call(s32[1]{0:T(128)} %bitcast.mem.refs_0_, ...), custom_call_target="tpu_custom_call", output_to_operand_aliasing={{5}: (5, {})} | custom-call | tf_op jit(solution)/shard_map/density/pallas_call | solution.py:36
  36.5 3.0 %collective-permute-start.2 = (f32[4,128]{1,0:T(4,128)S(1)}, f32[4,128]{1,0:T(4,128)S(1)}, u32[]{:S(2)}, u32[]{:S(2)}) collective-permute-start(f32[4,128]{1,0:T(4,128)S(1)} %get-tuple-element.55), channel_id=1, source_target_pairs={{0,1},{2,3},{4,13},{14,15},{8,9},{10,11},{12,21},{22,23},{16,17},{... | collective-permute-start | bytes 6152 | tf_op jit(solution)/shard_map/ppermute | solution.py:397
  39.6 1.9 %collective-permute-start.3 = (f32[4,128]{1,0:T(4,128)S(1)}, f32[4,128]{1,0:T(4,128)S(1)}, u32[]{:S(2)}, u32[]{:S(2)}) collective-permute-start(f32[4,128]{1,0:T(4,128)S(1)} %get-tuple-element.56), channel_id=1, source_target_pairs={{1,2},{3,4},{13,14},{15,8},{9,10},{11,12},{21,22},{23,16},{17,18},... | collective-permute-start | bytes 6152 | tf_op jit(solution)/shard_map/ppermute | solution.py:397
  41.5 3.6 %forces.1.refs_4_.refs_3_ = bf16[16,768,256]{2,1,0:T(8,128)(2,1)S(1)} custom-call(s32[1,128]{1,0:T(1,128)S(1)} %get-tuple-element.47.table.refs_1_.refs_0_, f32[8,16,128]{2,1,0:T(8,128)S(1)} %get-tuple-element.48.arranged.refs_2_.refs_1_, f32[5,24,128,128]{3,2,1,0:T(8,128)S(1)} %get-tuple-element.52.cols, f32[16,768,128]{2,1,0:T(8,128)S(1)} %get-tuple-element.53.dist), custom_call_target="tpu_custom_call" | custom-call | tf_op jit(solution)/shard_map/forces/pallas_call | solution.py:36
  45.1 1.2 %limiter_first_edge.1 = (f32[8,128]{1,0:T(8,128)S(1)}, f32[4,128]{1,0:T(4,128)S(1)}, f32[4,128]{1,0:T(4,128)S(1)}, f32[2,8,128]{2,1,0:T(8,128)S(1)}, bf16[24,24,...) custom-call(s32[1]{0:T(128)} %bitcast.mem.refs_0_, ...), custom_call_target="tpu_custom_call" | custom-call | tf_op jit(solution)/shard_map/limiter_first_edge/pallas_call | solution.py:36
  47.0 3.1 %collective-permute-start.5 = (f32[4,128]{1,0:T(4,128)S(1)}, f32[4,128]{1,0:T(4,128)S(1)}, u32[]{:S(2)}, u32[]{:S(2)}) collective-permute-start(f32[4,128]{1,0:T(4,128)S(1)} %get-tuple-element.65), channel_id=1, source_target_pairs={{1,2},{3,4},{13,14},{15,8},{9,10},{11,12},{21,22},{23,16},{17,18},... | collective-permute-start | bytes 6152 | tf_op jit(solution)/shard_map/ppermute | solution.py:397
  50.1 1.2 %limiter_first_inner.1 = (f32[8,128]{1,0:T(8,128)S(1)}, f32[2,8,128]{2,1,0:T(8,128)S(1)}, f32[4,8,128]{2,1,0:T(8,128)S(1)}) custom-call(s32[1,128]{1,0:T(1,128)S(1)} %get-tuple-element.47.table.refs_1_.refs_0_, f32[8,16,128]{2,1,0:T(8,128)S(1)} %get-tuple-element.48.arranged.refs_2_.refs_1_, ...), custom_call_target="tpu_custom_call" | custom-call | tf_op jit(solution)/shard_map/limiter_first_inner/pallas_call | solution.py:36
  51.9 1.1 %jacobi_edge.2 = (f32[8,128]{1,0:T(8,128)S(1)}, f32[4,128]{1,0:T(4,128)S(1)}, f32[4,128]{1,0:T(4,128)S(1)}, bf16[24,8,128]{2,1,0:T(8,128)(2,1)S(1)}) custom-call(s32[1]{0:T(128)} %bitcast.mem.refs_0_, s32[1,128]{1,0:T(1,128)S(1)} %get-tuple-element.47.table.refs_1_.refs_0_, f32[8,16,128]{2,1,0:T(8,128)S(1)} %get-tuple-element.48.arranged.refs_2_.refs_1_, ...), custom_call_target="tpu_custom_call" | custom-call | tf_op jit(solution)/shard_map/jacobi_edge/pallas_call | solution.py:36
  53.0 2.5 %collective-permute-start.6 = (f32[4,128]{1,0:T(4,128)S(1)}, f32[4,128]{1,0:T(4,128)S(1)}, u32[]{:S(2)}, u32[]{:S(2)}) collective-permute-start(f32[4,128]{1,0:T(4,128)S(1)} %get-tuple-element.68), channel_id=1, source_target_pairs={{0,1},{2,3},{4,13},{14,15},{8,9},{10,11},{12,21},{22,23},{16,17},{... | collective-permute-start | bytes 6152 | tf_op jit(solution)/shard_map/ppermute | solution.py:397
  55.5 3.6 %collective-permute-start.7 = (f32[4,128]{1,0:T(4,128)S(1)}, f32[4,128]{1,0:T(4,128)S(1)}, u32[]{:S(2)}, u32[]{:S(2)}) collective-permute-start(f32[4,128]{1,0:T(4,128)S(1)} %get-tuple-element.69), channel_id=1, source_target_pairs={{1,2},{3,4},{13,14},{15,8},{9,10},{11,12},{21,22},{23,16},{17,18},... | collective-permute-start | bytes 6152 | tf_op jit(solution)/shard_map/ppermute | solution.py:397
  59.1 1.1 %jacobi_inner.2.refs_7_ = f32[8,128]{1,0:T(8,128)S(1)} custom-call(s32[1,128]{1,0:T(1,128)S(1)} %get-tuple-element.47.table.refs_1_.refs_0_, f32[8,16,128]{2,1,0:T(8,128)S(1)} %get-tuple-element.48.arranged.refs_2_.refs_1_, bf16[16,768,256]{2,1,0:T(8,128)(2,1)S(1)} %forces.1.refs_4_.refs_3_, f32[24,128]{1,0:T(8,128)S(1)} %get-tuple-element.57.refs_4_.refs_5_.rho, ...), custom_call_target="tpu_custom_call" | custom-call | tf_op jit(solution)/shard_map/jacobi_inner/pallas_call | solution.py:36
  60.4 1.1 %limiter_edge.2 = (f32[8,128]{1,0:T(8,128)S(1)}, f32[4,128]{1,0:T(4,128)S(1)}, f32[4,128]{1,0:T(4,128)S(1)}, f32[2,8,128]{2,1,0:T(8,128)S(1)}, bf16[24,16,128]{2,1,0:T(8,128)(2,1)S(1)}, /*index=5*/f32[24,128]{1,0:T(8,128)S(1)}) custom-call(s32[1]{0:T(128)} %bitcast.mem.refs_0_, s32[1,128]{1,0:T(1,128)S(1)} %get-tuple-element.47.table.refs_1_.refs_0_, ...), custom_call_target="tpu_custom_call" | custom-call | tf_op jit(solution)/shard_map/limiter_edge/pallas_call | solution.py:36
  61.5 1.3 %collective-permute-start.8 = (f32[4,128]{1,0:T(4,128)S(1)}, f32[4,128]{1,0:T(4,128)S(1)}, u32[]{:S(2)}, u32[]{:S(2)}) collective-permute-start(f32[4,128]{1,0:T(4,128)S(1)} %get-tuple-element.77), channel_id=1, source_target_pairs={{0,1},{2,3},{4,13},{14,15},{8,9},{10,11},{12,21},{22,23},{16,17},{... | collective-permute-start | bytes 6152 | tf_op jit(solution)/shard_map/ppermute | solution.py:397
  62.8 2.6 %collective-permute-start.9 = (f32[4,128]{1,0:T(4,128)S(1)}, f32[4,128]{1,0:T(4,128)S(1)}, u32[]{:S(2)}, u32[]{:S(2)}) collective-permute-start(f32[4,128]{1,0:T(4,128)S(1)} %get-tuple-element.78), channel_id=1, source_target_pairs={{1,2},{3,4},{13,14},{15,8},{9,10},{11,12},{21,22},{23,16},{17,18},... | collective-permute-start | bytes 6152 | tf_op jit(solution)/shard_map/ppermute | solution.py:397
  65.4 1.1 %limiter_inner.2 = (f32[8,128]{1,0:T(8,128)S(1)}, f32[2,8,128]{2,1,0:T(8,128)S(1)}) custom-call(s32[1,128]{1,0:T(1,128)S(1)} %get-tuple-element.47.table.refs_1_.refs_0_, f32[8,16,128]{2,1,0:T(8,128)S(1)} %get-tuple-element.48.arranged.refs_2_.refs_1_, f32[6,24,128]{2,1,0:T(8,128)S(1)} %get-tuple-element.51.refs_3_.refs_2_.refs_5_.refs_6_, ...), custom_call_target="tpu_custom_call" | custom-call | tf_op jit(solution)/shard_map/limiter_inner/pallas_call | solution.py:36
  66.6 1.1 %collective-permute-done.9.refs_12_ = f32[4,128]{1,0:T(4,128)S(1)} collective-permute-done((f32[4,128]{1,0:T(4,128)S(1)}, f32[4,128]{1,0:T(4,128)S(1)}, u32[]{:S(2)}, u32[]{:S(2)}) %collective-permute-start.9) | collective-permute-done | bytes 2080 | tf_op jit(solution)/shard_map/ppermute | solution.py:397
  67.7 1.1 %jacobi_edge.3 = (f32[8,128]{1,0:T(8,128)S(1)}, f32[4,128]{1,0:T(4,128)S(1)}, f32[4,128]{1,0:T(4,128)S(1)}, bf16[24,8,128]{2,1,0:T(8,128)(2,1)S(1)}) custom-call(s32[1]{0:T(128)} %bitcast.mem.refs_0_, s32[1,128]{1,0:T(1,128)S(1)} %get-tuple-element.47.table.refs_1_.refs_0_, f32[8,16,128]{2,1,0:T(8,128)S(1)} %get-tuple-element.48.arranged.refs_2_.refs_1_, ...), custom_call_target="tpu_custom_call" | custom-call | tf_op jit(solution)/shard_map/jacobi_edge/pallas_call | solution.py:36
  68.8 1.8 %collective-permute-start.10 = (f32[4,128]{1,0:T(4,128)S(1)}, f32[4,128]{1,0:T(4,128)S(1)}, u32[]{:S(2)}, u32[]{:S(2)}) collective-permute-start(f32[4,128]{1,0:T(4,128)S(1)} %get-tuple-element.81), channel_id=1, source_target_pairs={{0,1},{2,3},{4,13},{14,15},{8,9},{10,11},{12,21},{22,23},{16,17},{... | collective-permute-start | bytes 6152 | tf_op jit(solution)/shard_map/ppermute | solution.py:397
  70.6 3.6 %collective-permute-start.11 = (f32[4,128]{1,0:T(4,128)S(1)}, f32[4,128]{1,0:T(4,128)S(1)}, u32[]{:S(2)}, u32[]{:S(2)}) collective-permute-start(f32[4,128]{1,0:T(4,128)S(1)} %get-tuple-element.82), channel_id=1, source_target_pairs={{1,2},{3,4},{13,14},{15,8},{9,10},{11,12},{21,22},{23,16},{17,18},... | collective-permute-start | bytes 6152 | tf_op jit(solution)/shard_map/ppermute | solution.py:397
  74.3 1.1 %jacobi_inner.3.refs_7_ = f32[8,128]{1,0:T(8,128)S(1)} custom-call(s32[1,128]{1,0:T(1,128)S(1)} %get-tuple-element.47.table.refs_1_.refs_0_, f32[8,16,128]{2,1,0:T(8,128)S(1)} %get-tuple-element.48.arranged.refs_2_.refs_1_, bf16[16,768,256]{2,1,0:T(8,128)(2,1)S(1)} %forces.1.refs_4_.refs_3_, f32[24,128]{1,0:T(8,128)S(1)} %get-tuple-element.57.refs_4_.refs_5_.rho, ...), custom_call_target="tpu_custom_call" | custom-call | tf_op jit(solution)/shard_map/jacobi_inner/pallas_call | solution.py:36
  75.5 1.1 %limiter_edge.3 = (f32[8,128]{1,0:T(8,128)S(1)}, f32[4,128]{1,0:T(4,128)S(1)}, f32[4,128]{1,0:T(4,128)S(1)}, f32[2,8,128]{2,1,0:T(8,128)S(1)}, bf16[24,16,128]{2,1,0:T(8,128)(2,1)S(1)}, /*index=5*/f32[24,128]{1,0:T(8,128)S(1)}) custom-call(s32[1]{0:T(128)} %bitcast.mem.refs_0_, s32[1,128]{1,0:T(1,128)S(1)} %get-tuple-element.47.table.refs_1_.refs_0_, ...), custom_call_target="tpu_custom_call" | custom-call | tf_op jit(solution)/shard_map/limiter_edge/pallas_call | solution.py:36
  76.7 1.3 %collective-permute-start.12 = (f32[4,128]{1,0:T(4,128)S(1)}, f32[4,128]{1,0:T(4,128)S(1)}, u32[]{:S(2)}, u32[]{:S(2)}) collective-permute-start(f32[4,128]{1,0:T(4,128)S(1)} %get-tuple-element.89), channel_id=1, source_target_pairs={{0,1},{2,3},{4,13},{14,15},{8,9},{10,11},{12,21},{22,23},{16,17},{... | collective-permute-start | bytes 6152 | tf_op jit(solution)/shard_map/ppermute | solution.py:397
  78.0 2.7 %collective-permute-start.13 = (f32[4,128]{1,0:T(4,128)S(1)}, f32[4,128]{1,0:T(4,128)S(1)}, u32[]{:S(2)}, u32[]{:S(2)}) collective-permute-start(f32[4,128]{1,0:T(4,128)S(1)} %get-tuple-element.90), channel_id=1, source_target_pairs={{1,2},{3,4},{13,14},{15,8},{9,10},{11,12},{21,22},{23,16},{17,18},... | collective-permute-start | bytes 6152 | tf_op jit(solution)/shard_map/ppermute | solution.py:397
  80.7 1.1 %limiter_inner.3 = (f32[8,128]{1,0:T(8,128)S(1)}, f32[2,8,128]{2,1,0:T(8,128)S(1)}) custom-call(s32[1,128]{1,0:T(1,128)S(1)} %get-tuple-element.47.table.refs_1_.refs_0_, f32[8,16,128]{2,1,0:T(8,128)S(1)} %get-tuple-element.48.arranged.refs_2_.refs_1_, f32[6,24,128]{2,1,0:T(8,128)S(1)} %get-tuple-element.51.refs_3_.refs_2_.refs_5_.refs_6_, ...), custom_call_target="tpu_custom_call" | custom-call | tf_op jit(solution)/shard_map/limiter_inner/pallas_call | solution.py:36
  81.8 1.1 %collective-permute-done.13.refs_12_ = f32[4,128]{1,0:T(4,128)S(1)} collective-permute-done((f32[4,128]{1,0:T(4,128)S(1)}, f32[4,128]{1,0:T(4,128)S(1)}, u32[]{:S(2)}, u32[]{:S(2)}) %collective-permute-start.13) | collective-permute-done | bytes 2080 | tf_op jit(solution)/shard_map/ppermute | solution.py:397
  82.9 1.9 %jacobi_last.1 = (f32[32,128]{1,0:T(8,128)S(1)}, bf16[24,8,128]{2,1,0:T(8,128)(2,1)}) custom-call(s32[1]{0:T(128)} %bitcast.mem.refs_0_, s32[1,128]{1,0:T(1,128)S(1)} %get-tuple-element.47.table.refs_1_.refs_0_, f32[8,16,128]{2,1,0:T(8,128)S(1)} %get-tuple-element.48.arranged.refs_2_.refs_1_, ...), custom_call_target="tpu_custom_call" | custom-call | tf_op jit(solution)/shard_map/jacobi_last/pallas_call | solution.py:36
  84.8 1.9 %collective-permute-start.14 = (f32[32,128]{1,0:T(8,128)S(1)}, f32[32,128]{1,0:T(8,128)S(1)}, u32[]{:S(2)}, u32[]{:S(2)}) collective-permute-start(f32[32,128]{1,0:T(8,128)S(1)} %get-tuple-element.91), channel_id=1, source_target_pairs={{0,0},{1,1},{2,2},{3,3},{4,4},{13,5},{14,6},{15,7},{8,8},{9,9},{10... | collective-permute-start | bytes 49160 | tf_op jit(solution)/shard_map/ppermute | solution.py:576
  86.7 3.7 %collective-permute-done.14 = f32[32,128]{1,0:T(8,128)S(1)} collective-permute-done((f32[32,128]{1,0:T(8,128)S(1)}, f32[32,128]{1,0:T(8,128)S(1)}, u32[]{:S(2)}, u32[]{:S(2)}) %collective-permute-start.14) | collective-permute-done | bytes 16416 | tf_op jit(solution)/shard_map/ppermute | solution.py:576
  (16 shorter events, 3.4 us)
Async XLA Ops:
  26.1 4.3 %collective-permute-start = (f32[6,4,128]{2,1,0:T(4,128)S(1)}, f32[6,4,128]{2,1,0:T(4,128)S(1)}, u32[]{:S(2)}, u32[]{:S(2)}) collective-permute-start(f32[6,4,128]{2,1,0:T(4,128)S(1)} %get-tuple-element.49), channel_id=1, source_target_pairs={{0,1},{2,3},{4,13},{14,15},{8,9},{10,11},{12,21},{22,23},{16,17},{... | collective-permute-start | bytes 36872 | tf_op jit(solution)/shard_map/ppermute | solution.py:397
  26.1 5.0 %collective-permute-start.1 = (f32[6,4,128]{2,1,0:T(4,128)S(1)}, f32[6,4,128]{2,1,0:T(4,128)S(1)}, u32[]{:S(2)}, u32[]{:S(2)}) collective-permute-start(f32[6,4,128]{2,1,0:T(4,128)S(1)} %get-tuple-element.50), channel_id=1, source_target_pairs={{1,2},{3,4},{13,14},{15,8},{9,10},{11,12},{21,22},{23,16},{17,18},... | collective-permute-start | bytes 36872 | tf_op jit(solution)/shard_map/ppermute | solution.py:397
  36.5 8.5 %collective-permute-start.2 = (f32[4,128]{1,0:T(4,128)S(1)}, f32[4,128]{1,0:T(4,128)S(1)}, u32[]{:S(2)}, u32[]{:S(2)}) collective-permute-start(f32[4,128]{1,0:T(4,128)S(1)} %get-tuple-element.55), channel_id=1, source_target_pairs={{0,1},{2,3},{4,13},{14,15},{8,9},{10,11},{12,21},{22,23},{16,17},{... | collective-permute-start | bytes 6152 | tf_op jit(solution)/shard_map/ppermute | solution.py:397
  39.6 5.5 %collective-permute-start.3 = (f32[4,128]{1,0:T(4,128)S(1)}, f32[4,128]{1,0:T(4,128)S(1)}, u32[]{:S(2)}, u32[]{:S(2)}) collective-permute-start(f32[4,128]{1,0:T(4,128)S(1)} %get-tuple-element.56), channel_id=1, source_target_pairs={{1,2},{3,4},{13,14},{15,8},{9,10},{11,12},{21,22},{23,16},{17,18},... | collective-permute-start | bytes 6152 | tf_op jit(solution)/shard_map/ppermute | solution.py:397
  46.3 5.0 %collective-permute-start.4 = (f32[4,128]{1,0:T(4,128)S(1)}, f32[4,128]{1,0:T(4,128)S(1)}, u32[]{:S(2)}, u32[]{:S(2)}) collective-permute-start(f32[4,128]{1,0:T(4,128)S(1)} %get-tuple-element.64), channel_id=1, source_target_pairs={{0,1},{2,3},{4,13},{14,15},{8,9},{10,11},{12,21},{22,23},{16,17},{... | collective-permute-start | bytes 6152 | tf_op jit(solution)/shard_map/ppermute | solution.py:397
  47.0 4.9 %collective-permute-start.5 = (f32[4,128]{1,0:T(4,128)S(1)}, f32[4,128]{1,0:T(4,128)S(1)}, u32[]{:S(2)}, u32[]{:S(2)}) collective-permute-start(f32[4,128]{1,0:T(4,128)S(1)} %get-tuple-element.65), channel_id=1, source_target_pairs={{1,2},{3,4},{13,14},{15,8},{9,10},{11,12},{21,22},{23,16},{17,18},... | collective-permute-start | bytes 6152 | tf_op jit(solution)/shard_map/ppermute | solution.py:397
  53.0 7.2 %collective-permute-start.6 = (f32[4,128]{1,0:T(4,128)S(1)}, f32[4,128]{1,0:T(4,128)S(1)}, u32[]{:S(2)}, u32[]{:S(2)}) collective-permute-start(f32[4,128]{1,0:T(4,128)S(1)} %get-tuple-element.68), channel_id=1, source_target_pairs={{0,1},{2,3},{4,13},{14,15},{8,9},{10,11},{12,21},{22,23},{16,17},{... | collective-permute-start | bytes 6152 | tf_op jit(solution)/shard_map/ppermute | solution.py:397
  55.5 4.9 %collective-permute-start.7 = (f32[4,128]{1,0:T(4,128)S(1)}, f32[4,128]{1,0:T(4,128)S(1)}, u32[]{:S(2)}, u32[]{:S(2)}) collective-permute-start(f32[4,128]{1,0:T(4,128)S(1)} %get-tuple-element.69), channel_id=1, source_target_pairs={{1,2},{3,4},{13,14},{15,8},{9,10},{11,12},{21,22},{23,16},{17,18},... | collective-permute-start | bytes 6152 | tf_op jit(solution)/shard_map/ppermute | solution.py:397
  61.5 5.0 %collective-permute-start.8 = (f32[4,128]{1,0:T(4,128)S(1)}, f32[4,128]{1,0:T(4,128)S(1)}, u32[]{:S(2)}, u32[]{:S(2)}) collective-permute-start(f32[4,128]{1,0:T(4,128)S(1)} %get-tuple-element.77), channel_id=1, source_target_pairs={{0,1},{2,3},{4,13},{14,15},{8,9},{10,11},{12,21},{22,23},{16,17},{... | collective-permute-start | bytes 6152 | tf_op jit(solution)/shard_map/ppermute | solution.py:397
  62.8 4.9 %collective-permute-start.9 = (f32[4,128]{1,0:T(4,128)S(1)}, f32[4,128]{1,0:T(4,128)S(1)}, u32[]{:S(2)}, u32[]{:S(2)}) collective-permute-start(f32[4,128]{1,0:T(4,128)S(1)} %get-tuple-element.78), channel_id=1, source_target_pairs={{1,2},{3,4},{13,14},{15,8},{9,10},{11,12},{21,22},{23,16},{17,18},... | collective-permute-start | bytes 6152 | tf_op jit(solution)/shard_map/ppermute | solution.py:397
  68.8 6.6 %collective-permute-start.10 = (f32[4,128]{1,0:T(4,128)S(1)}, f32[4,128]{1,0:T(4,128)S(1)}, u32[]{:S(2)}, u32[]{:S(2)}) collective-permute-start(f32[4,128]{1,0:T(4,128)S(1)} %get-tuple-element.81), channel_id=1, source_target_pairs={{0,1},{2,3},{4,13},{14,15},{8,9},{10,11},{12,21},{22,23},{16,17},{... | collective-permute-start | bytes 6152 | tf_op jit(solution)/shard_map/ppermute | solution.py:397
  70.6 4.9 %collective-permute-start.11 = (f32[4,128]{1,0:T(4,128)S(1)}, f32[4,128]{1,0:T(4,128)S(1)}, u32[]{:S(2)}, u32[]{:S(2)}) collective-permute-start(f32[4,128]{1,0:T(4,128)S(1)} %get-tuple-element.82), channel_id=1, source_target_pairs={{1,2},{3,4},{13,14},{15,8},{9,10},{11,12},{21,22},{23,16},{17,18},... | collective-permute-start | bytes 6152 | tf_op jit(solution)/shard_map/ppermute | solution.py:397
  76.7 5.1 %collective-permute-start.12 = (f32[4,128]{1,0:T(4,128)S(1)}, f32[4,128]{1,0:T(4,128)S(1)}, u32[]{:S(2)}, u32[]{:S(2)}) collective-permute-start(f32[4,128]{1,0:T(4,128)S(1)} %get-tuple-element.89), channel_id=1, source_target_pairs={{0,1},{2,3},{4,13},{14,15},{8,9},{10,11},{12,21},{22,23},{16,17},{... | collective-permute-start | bytes 6152 | tf_op jit(solution)/shard_map/ppermute | solution.py:397
  78.0 4.9 %collective-permute-start.13 = (f32[4,128]{1,0:T(4,128)S(1)}, f32[4,128]{1,0:T(4,128)S(1)}, u32[]{:S(2)}, u32[]{:S(2)}) collective-permute-start(f32[4,128]{1,0:T(4,128)S(1)} %get-tuple-element.90), channel_id=1, source_target_pairs={{1,2},{3,4},{13,14},{15,8},{9,10},{11,12},{21,22},{23,16},{17,18},... | collective-permute-start | bytes 6152 | tf_op jit(solution)/shard_map/ppermute | solution.py:397
  84.8 5.6 %collective-permute-start.14 = (f32[32,128]{1,0:T(8,128)S(1)}, f32[32,128]{1,0:T(8,128)S(1)}, u32[]{:S(2)}, u32[]{:S(2)}) collective-permute-start(f32[32,128]{1,0:T(8,128)S(1)} %get-tuple-element.91), channel_id=1, source_target_pairs={{0,0},{1,1},{2,2},{3,3},{4,4},{13,5},{14,6},{15,7},{8,8},{9,9},{10... | collective-permute-start | bytes 49160 | tf_op jit(solution)/shard_map/ppermute | solution.py:576

commit v5 on v4

--- a/solution.py
+++ b/solution.py
@@ -164,10 +164,11 @@
 
 
 def spread_columns(cols, fields, tiles, first):
+    turned = jnp.concatenate(fields, axis=0).T
     for f in range(5):
-        turned = fields[f].T
         for t in range(tiles):
-            cols[f, first + t] = jnp.broadcast_to(turned[:, t : t + 1], (TILE, TILE))
+            at = f * tiles + t
+            cols[f, first + t] = jnp.broadcast_to(turned[:, at : at + 1], (TILE, TILE))
 
 
 def columns_body(arranged, cols):
@@ -230,8 +231,8 @@
                 q = w / (p2 * p2)
                 force = q * q * w
                 high = force.astype(BF16)
-                forces[s, at, 0:TILE] = high
-                forces[s, at, TILE : 2 * TILE] = (force - high.astype(F32)).astype(BF16)
+                forces[s, 0, at, :] = high
+                forces[s, 1, at, :] = (force - high.astype(F32)).astype(BF16)
         return carry
 
     lax.fori_loop(0, TD, tile, 0)
@@ -253,7 +254,8 @@
     listed.wait()
     for k, s in enumerate(tiles):
         row = jnp.concatenate([operand[near[0, LIST + n * TD + s]] for n in range(NB)], axis=1)
-        got = jnp.dot(row, forces[s], preferred_element_type=F32)
+        both = jnp.concatenate([forces[s, 0], forces[s, 1]], axis=1)
+        got = jnp.dot(row, both, preferred_element_type=F32)
         result[k * height : (k + 1) * height, :] = got[:, TILE:] + got[:, :TILE]
     sums = []
     for q in range(count):
@@ -476,7 +478,7 @@
     r1, r2 = swap(r1, r2)
     (forces,) = call(
         forces_body,
-        [((TD, NB * TILE, 2 * TILE), BF16)],
+        [((TD, 2, NB * TILE, TILE), BF16)],
         LISTED,
         "forces",
         near,
@@ -541,8 +543,8 @@
         operand = ((EXT, 8, TILE), BF16)
         results = call(
             lambda *refs: jacobi_edge(last, *refs),
-            [((2 * TD, TILE), F32), operand] if last else [half, edge, edge, operand],
-            workspace(8, TD if last else HALF, True),
+            [((2 * TD, TILE), F32)] if last else [half, edge, edge, operand],
+            ([pltpu.VMEM(*operand)] if last else []) + workspace(8, TD if last else HALF, True),
             "jacobi_last" if last else "jacobi_edge",
             *shared,
             dens_ext,

time: 91.4 us -> 90.6 us (level)
  no operation moved by 1% of the time
where the time goes in v5:
time: 90.6 us; the launch traced here: 90.2 us
  starting transfers between devices  32.3 us (36%)
  Pallas kernels  24.7 us (27%)
  blocking collectives  23.8 us (26%)
  waiting for transfers between devices  7.94 us (9%)
    ppermute x14, starting transfers between devices, swap(): got.append(lax.ppermute(value, AXES, pairs + [(b, a) for a, b in pairs]))  30.4 us
    all_to_all x1, blocking collectives, local(): lax.all_to_all(outgoing.reshape(GROUPS * ROWS, 1, TILE), 'group', split_a...  23.8 us
    pallas_call x15, Pallas kernels, call(): pl.pallas_call(body, out_shape=[jax.ShapeDtypeStruct(shape, dtype) for sh...  23.4 us
    ppermute x14, waiting for transfers between devices, swap(): got.append(lax.ppermute(value, AXES, pairs + [(b, a) for a, b in pairs]))  4.23 us
    ppermute x1, waiting for transfers between devices, local(): done = lax.ppermute(done, AXES, [(owner(s), s) for s in range(GROUPS * 8)])  3.7 us
    ppermute x1, starting transfers between devices, local(): done = lax.ppermute(done, AXES, [(owner(s), s) for s in range(GROUPS * 8)])  1.92 us
  transfers between devices with their start and end apart: 15, of which 7 were waited for; matrix products, arithmetic and copies ran while one was open for 0% of the time, Pallas kernels for 12%

profile of v5, /device:TPU:24, one launch (start us, length us, event | category | flops | bytes accessed | tf_op | source)
XLA Modules:
  0.0 90.2 jit_solution(12865602814890777333)
XLA Ops:
  0.6 1.3 %pack.1 = f32[544,128]{1,0:T(8,128)S(1)} custom-call(s32[1]{0:T(128)} %bitcast.1.grp, s32[1]{0:T(128)} %bitcast.mem.refs_0_, s32[1,2]{1,0:T(1,128)} %ghosts_hbm.1, s32[16]{0:T(128)} %slot_hbm.1, s32[6,16]{1,0:T(8,128)} %bitcast.13, f32[8,2048]{1,0:T(8,128)} %part_hbm.1), custom_call_target="tpu_custom_call" | custom-call | tf_op jit(solution)/shard_map/pack/pallas_call | solution.py:406
  2.0 23.8 %all_to_all.5 = f32[544,1,128]{2,1,0:T(1,128)S(1)} all-to-all(f32[544,1,128]{2,1,0:T(1,128)S(1)} %bitcast.12), channel_id=1, replica_groups=mesh['group'=32,'member'=8] {'group'}, dimensions={0} | all-to-all | bytes 557056 | tf_op jit(solution)/shard_map/all_to_all | solution.py:436
  26.1 2.6 %collective-permute-start.1 = (f32[6,4,128]{2,1,0:T(4,128)S(1)}, f32[6,4,128]{2,1,0:T(4,128)S(1)}, u32[]{:S(2)}, u32[]{:S(2)}) collective-permute-start(f32[6,4,128]{2,1,0:T(4,128)S(1)} %get-tuple-element.49), channel_id=1, source_target_pairs={{1,2},{3,4},{13,14},{15,8},{9,10},{11,12},{21,22},{23,16},{17,18},... | collective-permute-start | bytes 36872 | tf_op jit(solution)/shard_map/ppermute | solution.py:399
  28.8 1.6 %columns.1.held = f32[5,24,128,128]{3,2,1,0:T(8,128)S(1)} custom-call(f32[8,16,128]{2,1,0:T(8,128)S(1)} %get-tuple-element.47.arranged.refs_2_.refs_1_), custom_call_target="tpu_custom_call" | custom-call | tf_op jit(solution)/shard_map/columns/pallas_call | solution.py:36
  31.1 5.4 %density.1 = (f32[16,128]{1,0:T(8,128)S(1)}, f32[6,24,128]{2,1,0:T(8,128)S(1)}, f32[16,768,128]{2,1,0:T(8,128)S(1)}, f32[4,128]{1,0:T(4,128)S(1)}, f32[4,128]{1,...) custom-call(s32[1]{0:T(128)} %bitcast.mem.refs_0_, ...), custom_call_target="tpu_custom_call", output_to_operand_aliasing={{5}: (5, {})} | custom-call | tf_op jit(solution)/shard_map/density/pallas_call | solution.py:36
  36.5 3.0 %collective-permute-start.2 = (f32[4,128]{1,0:T(4,128)S(1)}, f32[4,128]{1,0:T(4,128)S(1)}, u32[]{:S(2)}, u32[]{:S(2)}) collective-permute-start(f32[4,128]{1,0:T(4,128)S(1)} %get-tuple-element.54), channel_id=1, source_target_pairs={{0,1},{2,3},{4,13},{14,15},{8,9},{10,11},{12,21},{22,23},{16,17},{... | collective-permute-start | bytes 6152 | tf_op jit(solution)/shard_map/ppermute | solution.py:399
  39.5 1.9 %collective-permute-start.3 = (f32[4,128]{1,0:T(4,128)S(1)}, f32[4,128]{1,0:T(4,128)S(1)}, u32[]{:S(2)}, u32[]{:S(2)}) collective-permute-start(f32[4,128]{1,0:T(4,128)S(1)} %get-tuple-element.55), channel_id=1, source_target_pairs={{1,2},{3,4},{13,14},{15,8},{9,10},{11,12},{21,22},{23,16},{17,18},... | collective-permute-start | bytes 6152 | tf_op jit(solution)/shard_map/ppermute | solution.py:399
  41.5 3.2 %forces.1.refs_4_.refs_3_ = bf16[16,2,768,128]{3,2,1,0:T(8,128)(2,1)S(1)} custom-call(s32[1,128]{1,0:T(1,128)S(1)} %get-tuple-element.46.table.refs_1_.refs_0_, f32[8,16,128]{2,1,0:T(8,128)S(1)} %get-tuple-element.47.arranged.refs_2_.refs_1_, f32[5,24,128,128]{3,2,1,0:T(8,128)S(1)} %get-tuple-element.51.cols, f32[16,768,128]{2,1,0:T(8,128)S(1)} %get-tuple-element.52.dist), custom_call_target="tpu_custom_call" | custom-call | tf_op jit(solution)/shard_map/forces/pallas_call | solution.py:36
  44.7 1.3 %limiter_first_edge.1 = (f32[8,128]{1,0:T(8,128)S(1)}, f32[4,128]{1,0:T(4,128)S(1)}, f32[4,128]{1,0:T(4,128)S(1)}, f32[2,8,128]{2,1,0:T(8,128)S(1)}, bf16[24,24,...) custom-call(s32[1]{0:T(128)} %bitcast.mem.refs_0_, ...), custom_call_target="tpu_custom_call" | custom-call | tf_op jit(solution)/shard_map/limiter_first_edge/pallas_call | solution.py:36
  47.0 2.7 %collective-permute-start.5 = (f32[4,128]{1,0:T(4,128)S(1)}, f32[4,128]{1,0:T(4,128)S(1)}, u32[]{:S(2)}, u32[]{:S(2)}) collective-permute-start(f32[4,128]{1,0:T(4,128)S(1)} %get-tuple-element.64), channel_id=1, source_target_pairs={{1,2},{3,4},{13,14},{15,8},{9,10},{11,12},{21,22},{23,16},{17,18},... | collective-permute-start | bytes 6152 | tf_op jit(solution)/shard_map/ppermute | solution.py:399
  49.7 1.2 %limiter_first_inner.1 = (f32[8,128]{1,0:T(8,128)S(1)}, f32[2,8,128]{2,1,0:T(8,128)S(1)}, f32[4,8,128]{2,1,0:T(8,128)S(1)}) custom-call(s32[1,128]{1,0:T(1,128)S(1)} %get-tuple-element.46.table.refs_1_.refs_0_, f32[8,16,128]{2,1,0:T(8,128)S(1)} %get-tuple-element.47.arranged.refs_2_.refs_1_, ...), custom_call_target="tpu_custom_call" | custom-call | tf_op jit(solution)/shard_map/limiter_first_inner/pallas_call | solution.py:36
  51.9 1.1 %jacobi_edge.2 = (f32[8,128]{1,0:T(8,128)S(1)}, f32[4,128]{1,0:T(4,128)S(1)}, f32[4,128]{1,0:T(4,128)S(1)}, bf16[24,8,128]{2,1,0:T(8,128)(2,1)S(1)}) custom-call(s32[1]{0:T(128)} %bitcast.mem.refs_0_, s32[1,128]{1,0:T(1,128)S(1)} %get-tuple-element.46.table.refs_1_.refs_0_, f32[8,16,128]{2,1,0:T(8,128)S(1)} %get-tuple-element.47.arranged.refs_2_.refs_1_, ...), custom_call_target="tpu_custom_call" | custom-call | tf_op jit(solution)/shard_map/jacobi_edge/pallas_call | solution.py:36
  53.0 2.1 %collective-permute-start.6 = (f32[4,128]{1,0:T(4,128)S(1)}, f32[4,128]{1,0:T(4,128)S(1)}, u32[]{:S(2)}, u32[]{:S(2)}) collective-permute-start(f32[4,128]{1,0:T(4,128)S(1)} %get-tuple-element.67), channel_id=1, source_target_pairs={{0,1},{2,3},{4,13},{14,15},{8,9},{10,11},{12,21},{22,23},{16,17},{... | collective-permute-start | bytes 6152 | tf_op jit(solution)/shard_map/ppermute | solution.py:399
  55.1 3.6 %collective-permute-start.7 = (f32[4,128]{1,0:T(4,128)S(1)}, f32[4,128]{1,0:T(4,128)S(1)}, u32[]{:S(2)}, u32[]{:S(2)}) collective-permute-start(f32[4,128]{1,0:T(4,128)S(1)} %get-tuple-element.68), channel_id=1, source_target_pairs={{1,2},{3,4},{13,14},{15,8},{9,10},{11,12},{21,22},{23,16},{17,18},... | collective-permute-start | bytes 6152 | tf_op jit(solution)/shard_map/ppermute | solution.py:399
  58.7 1.1 %jacobi_inner.2.refs_7_ = f32[8,128]{1,0:T(8,128)S(1)} custom-call(s32[1,128]{1,0:T(1,128)S(1)} %get-tuple-element.46.table.refs_1_.refs_0_, f32[8,16,128]{2,1,0:T(8,128)S(1)} %get-tuple-element.47.arranged.refs_2_.refs_1_, bf16[16,2,768,128]{3,2,1,0:T(8,128)(2,1)S(1)} %forces.1.refs_4_.refs_3_, f32[24,128]{1,0:T(8,128)S(1)} %get-tuple-element.56.refs_4_.refs_5_.rho, ...), custom_call_target="tpu_custom_call" | custom-call | tf_op jit(solution)/shard_map/jacobi_inner/pallas_call | solution.py:36
  60.0 1.1 %limiter_edge.2 = (f32[8,128]{1,0:T(8,128)S(1)}, f32[4,128]{1,0:T(4,128)S(1)}, f32[4,128]{1,0:T(4,128)S(1)}, f32[2,8,128]{2,1,0:T(8,128)S(1)}, bf16[24,16,128]{2,1,0:T(8,128)(2,1)S(1)}, /*index=5*/f32[24,128]{1,0:T(8,128)S(1)}) custom-call(s32[1]{0:T(128)} %bitcast.mem.refs_0_, s32[1,128]{1,0:T(1,128)S(1)} %get-tuple-element.46.table.refs_1_.refs_0_, ...), custom_call_target="tpu_custom_call" | custom-call | tf_op jit(solution)/shard_map/limiter_edge/pallas_call | solution.py:36
  61.1 1.3 %collective-permute-start.8 = (f32[4,128]{1,0:T(4,128)S(1)}, f32[4,128]{1,0:T(4,128)S(1)}, u32[]{:S(2)}, u32[]{:S(2)}) collective-permute-start(f32[4,128]{1,0:T(4,128)S(1)} %get-tuple-element.76), channel_id=1, source_target_pairs={{0,1},{2,3},{4,13},{14,15},{8,9},{10,11},{12,21},{22,23},{16,17},{... | collective-permute-start | bytes 6152 | tf_op jit(solution)/shard_map/ppermute | solution.py:399
  62.4 2.6 %collective-permute-start.9 = (f32[4,128]{1,0:T(4,128)S(1)}, f32[4,128]{1,0:T(4,128)S(1)}, u32[]{:S(2)}, u32[]{:S(2)}) collective-permute-start(f32[4,128]{1,0:T(4,128)S(1)} %get-tuple-element.77), channel_id=1, source_target_pairs={{1,2},{3,4},{13,14},{15,8},{9,10},{11,12},{21,22},{23,16},{17,18},... | collective-permute-start | bytes 6152 | tf_op jit(solution)/shard_map/ppermute | solution.py:399
  65.1 1.1 %limiter_inner.2 = (f32[8,128]{1,0:T(8,128)S(1)}, f32[2,8,128]{2,1,0:T(8,128)S(1)}) custom-call(s32[1,128]{1,0:T(1,128)S(1)} %get-tuple-element.46.table.refs_1_.refs_0_, f32[8,16,128]{2,1,0:T(8,128)S(1)} %get-tuple-element.47.arranged.refs_2_.refs_1_, f32[6,24,128]{2,1,0:T(8,128)S(1)} %get-tuple-element.50.refs_3_.refs_2_.refs_5_.refs_6_, ...), custom_call_target="tpu_custom_call" | custom-call | tf_op jit(solution)/shard_map/limiter_inner/pallas_call | solution.py:36
  66.2 1.1 %collective-permute-done.9.refs_12_ = f32[4,128]{1,0:T(4,128)S(1)} collective-permute-done((f32[4,128]{1,0:T(4,128)S(1)}, f32[4,128]{1,0:T(4,128)S(1)}, u32[]{:S(2)}, u32[]{:S(2)}) %collective-permute-start.9) | collective-permute-done | bytes 2080 | tf_op jit(solution)/shard_map/ppermute | solution.py:399
  67.3 1.1 %jacobi_edge.3 = (f32[8,128]{1,0:T(8,128)S(1)}, f32[4,128]{1,0:T(4,128)S(1)}, f32[4,128]{1,0:T(4,128)S(1)}, bf16[24,8,128]{2,1,0:T(8,128)(2,1)S(1)}) custom-call(s32[1]{0:T(128)} %bitcast.mem.refs_0_, s32[1,128]{1,0:T(1,128)S(1)} %get-tuple-element.46.table.refs_1_.refs_0_, f32[8,16,128]{2,1,0:T(8,128)S(1)} %get-tuple-element.47.arranged.refs_2_.refs_1_, ...), custom_call_target="tpu_custom_call" | custom-call | tf_op jit(solution)/shard_map/jacobi_edge/pallas_call | solution.py:36
  68.4 1.8 %collective-permute-start.10 = (f32[4,128]{1,0:T(4,128)S(1)}, f32[4,128]{1,0:T(4,128)S(1)}, u32[]{:S(2)}, u32[]{:S(2)}) collective-permute-start(f32[4,128]{1,0:T(4,128)S(1)} %get-tuple-element.80), channel_id=1, source_target_pairs={{0,1},{2,3},{4,13},{14,15},{8,9},{10,11},{12,21},{22,23},{16,17},{... | collective-permute-start | bytes 6152 | tf_op jit(solution)/shard_map/ppermute | solution.py:399
  70.3 3.6 %collective-permute-start.11 = (f32[4,128]{1,0:T(4,128)S(1)}, f32[4,128]{1,0:T(4,128)S(1)}, u32[]{:S(2)}, u32[]{:S(2)}) collective-permute-start(f32[4,128]{1,0:T(4,128)S(1)} %get-tuple-element.81), channel_id=1, source_target_pairs={{1,2},{3,4},{13,14},{15,8},{9,10},{11,12},{21,22},{23,16},{17,18},... | collective-permute-start | bytes 6152 | tf_op jit(solution)/shard_map/ppermute | solution.py:399
  73.9 1.1 %jacobi_inner.3.refs_7_ = f32[8,128]{1,0:T(8,128)S(1)} custom-call(s32[1,128]{1,0:T(1,128)S(1)} %get-tuple-element.46.table.refs_1_.refs_0_, f32[8,16,128]{2,1,0:T(8,128)S(1)} %get-tuple-element.47.arranged.refs_2_.refs_1_, bf16[16,2,768,128]{3,2,1,0:T(8,128)(2,1)S(1)} %forces.1.refs_4_.refs_3_, f32[24,128]{1,0:T(8,128)S(1)} %get-tuple-element.56.refs_4_.refs_5_.rho, ...), custom_call_target="tpu_custom_call" | custom-call | tf_op jit(solution)/shard_map/jacobi_inner/pallas_call | solution.py:36
  75.1 1.1 %limiter_edge.3 = (f32[8,128]{1,0:T(8,128)S(1)}, f32[4,128]{1,0:T(4,128)S(1)}, f32[4,128]{1,0:T(4,128)S(1)}, f32[2,8,128]{2,1,0:T(8,128)S(1)}, bf16[24,16,128]{2,1,0:T(8,128)(2,1)S(1)}, /*index=5*/f32[24,128]{1,0:T(8,128)S(1)}) custom-call(s32[1]{0:T(128)} %bitcast.mem.refs_0_, s32[1,128]{1,0:T(1,128)S(1)} %get-tuple-element.46.table.refs_1_.refs_0_, ...), custom_call_target="tpu_custom_call" | custom-call | tf_op jit(solution)/shard_map/limiter_edge/pallas_call | solution.py:36
  76.3 1.3 %collective-permute-start.12 = (f32[4,128]{1,0:T(4,128)S(1)}, f32[4,128]{1,0:T(4,128)S(1)}, u32[]{:S(2)}, u32[]{:S(2)}) collective-permute-start(f32[4,128]{1,0:T(4,128)S(1)} %get-tuple-element.88), channel_id=1, source_target_pairs={{0,1},{2,3},{4,13},{14,15},{8,9},{10,11},{12,21},{22,23},{16,17},{... | collective-permute-start | bytes 6152 | tf_op jit(solution)/shard_map/ppermute | solution.py:399
  77.6 2.7 %collective-permute-start.13 = (f32[4,128]{1,0:T(4,128)S(1)}, f32[4,128]{1,0:T(4,128)S(1)}, u32[]{:S(2)}, u32[]{:S(2)}) collective-permute-start(f32[4,128]{1,0:T(4,128)S(1)} %get-tuple-element.89), channel_id=1, source_target_pairs={{1,2},{3,4},{13,14},{15,8},{9,10},{11,12},{21,22},{23,16},{17,18},... | collective-permute-start | bytes 6152 | tf_op jit(solution)/shard_map/ppermute | solution.py:399
  80.3 1.1 %limiter_inner.3 = (f32[8,128]{1,0:T(8,128)S(1)}, f32[2,8,128]{2,1,0:T(8,128)S(1)}) custom-call(s32[1,128]{1,0:T(1,128)S(1)} %get-tuple-element.46.table.refs_1_.refs_0_, f32[8,16,128]{2,1,0:T(8,128)S(1)} %get-tuple-element.47.arranged.refs_2_.refs_1_, f32[6,24,128]{2,1,0:T(8,128)S(1)} %get-tuple-element.50.refs_3_.refs_2_.refs_5_.refs_6_, ...), custom_call_target="tpu_custom_call" | custom-call | tf_op jit(solution)/shard_map/limiter_inner/pallas_call | solution.py:36
  81.4 1.1 %collective-permute-done.13.refs_12_ = f32[4,128]{1,0:T(4,128)S(1)} collective-permute-done((f32[4,128]{1,0:T(4,128)S(1)}, f32[4,128]{1,0:T(4,128)S(1)}, u32[]{:S(2)}, u32[]{:S(2)}) %collective-permute-start.13) | collective-permute-done | bytes 2080 | tf_op jit(solution)/shard_map/ppermute | solution.py:399
  82.5 1.5 %jacobi_last.1 = f32[32,128]{1,0:T(8,128)S(1)} custom-call(s32[1]{0:T(128)} %bitcast.mem.refs_0_, s32[1,128]{1,0:T(1,128)S(1)} %get-tuple-element.46.table.refs_1_.refs_0_, f32[8,16,128]{2,1,0:T(8,128)S(1)} %get-tuple-element.47.arranged.refs_2_.refs_1_, f32[6,24,128]{2,1,0:T(8,128)S(1)} %get-tuple-element.50.refs_3_.refs_2_.refs_5_.refs_6_, ...), custom_call_target="tpu_custom_call" | custom-call | tf_op jit(solution)/shard_map/jacobi_last/pallas_call | solution.py:36
  84.0 1.9 %collective-permute-start.14 = (f32[32,128]{1,0:T(8,128)S(1)}, f32[32,128]{1,0:T(8,128)S(1)}, u32[]{:S(2)}, u32[]{:S(2)}) collective-permute-start(f32[32,128]{1,0:T(8,128)S(1)} %jacobi_last.1), channel_id=1, source_target_pairs={{0,0},{1,1},{2,2},{3,3},{4,4},{13,5},{14,6},{15,7},{8,8},{9,9},{10... | collective-permute-start | bytes 49160 | tf_op jit(solution)/shard_map/ppermute | solution.py:578
  85.9 3.7 %collective-permute-done.14 = f32[32,128]{1,0:T(8,128)S(1)} collective-permute-done((f32[32,128]{1,0:T(8,128)S(1)}, f32[32,128]{1,0:T(8,128)S(1)}, u32[]{:S(2)}, u32[]{:S(2)}) %collective-permute-start.14) | collective-permute-done | bytes 16416 | tf_op jit(solution)/shard_map/ppermute | solution.py:578
  (16 shorter events, 4.1 us)
Async XLA Ops:
  26.1 4.3 %collective-permute-start = (f32[6,4,128]{2,1,0:T(4,128)S(1)}, f32[6,4,128]{2,1,0:T(4,128)S(1)}, u32[]{:S(2)}, u32[]{:S(2)}) collective-permute-start(f32[6,4,128]{2,1,0:T(4,128)S(1)} %get-tuple-element.48), channel_id=1, source_target_pairs={{0,1},{2,3},{4,13},{14,15},{8,9},{10,11},{12,21},{22,23},{16,17},{... | collective-permute-start | bytes 36872 | tf_op jit(solution)/shard_map/ppermute | solution.py:399
  26.1 5.0 %collective-permute-start.1 = (f32[6,4,128]{2,1,0:T(4,128)S(1)}, f32[6,4,128]{2,1,0:T(4,128)S(1)}, u32[]{:S(2)}, u32[]{:S(2)}) collective-permute-start(f32[6,4,128]{2,1,0:T(4,128)S(1)} %get-tuple-element.49), channel_id=1, source_target_pairs={{1,2},{3,4},{13,14},{15,8},{9,10},{11,12},{21,22},{23,16},{17,18},... | collective-permute-start | bytes 36872 | tf_op jit(solution)/shard_map/ppermute | solution.py:399
  36.5 8.2 %collective-permute-start.2 = (f32[4,128]{1,0:T(4,128)S(1)}, f32[4,128]{1,0:T(4,128)S(1)}, u32[]{:S(2)}, u32[]{:S(2)}) collective-permute-start(f32[4,128]{1,0:T(4,128)S(1)} %get-tuple-element.54), channel_id=1, source_target_pairs={{0,1},{2,3},{4,13},{14,15},{8,9},{10,11},{12,21},{22,23},{16,17},{... | collective-permute-start | bytes 6152 | tf_op jit(solution)/shard_map/ppermute | solution.py:399
  39.5 5.1 %collective-permute-start.3 = (f32[4,128]{1,0:T(4,128)S(1)}, f32[4,128]{1,0:T(4,128)S(1)}, u32[]{:S(2)}, u32[]{:S(2)}) collective-permute-start(f32[4,128]{1,0:T(4,128)S(1)} %get-tuple-element.55), channel_id=1, source_target_pairs={{1,2},{3,4},{13,14},{15,8},{9,10},{11,12},{21,22},{23,16},{17,18},... | collective-permute-start | bytes 6152 | tf_op jit(solution)/shard_map/ppermute | solution.py:399
  46.0 5.0 %collective-permute-start.4 = (f32[4,128]{1,0:T(4,128)S(1)}, f32[4,128]{1,0:T(4,128)S(1)}, u32[]{:S(2)}, u32[]{:S(2)}) collective-permute-start(f32[4,128]{1,0:T(4,128)S(1)} %get-tuple-element.63), channel_id=1, source_target_pairs={{0,1},{2,3},{4,13},{14,15},{8,9},{10,11},{12,21},{22,23},{16,17},{... | collective-permute-start | bytes 6152 | tf_op jit(solution)/shard_map/ppermute | solution.py:399
  47.0 4.9 %collective-permute-start.5 = (f32[4,128]{1,0:T(4,128)S(1)}, f32[4,128]{1,0:T(4,128)S(1)}, u32[]{:S(2)}, u32[]{:S(2)}) collective-permute-start(f32[4,128]{1,0:T(4,128)S(1)} %get-tuple-element.64), channel_id=1, source_target_pairs={{1,2},{3,4},{13,14},{15,8},{9,10},{11,12},{21,22},{23,16},{17,18},... | collective-permute-start | bytes 6152 | tf_op jit(solution)/shard_map/ppermute | solution.py:399
  53.0 6.8 %collective-permute-start.6 = (f32[4,128]{1,0:T(4,128)S(1)}, f32[4,128]{1,0:T(4,128)S(1)}, u32[]{:S(2)}, u32[]{:S(2)}) collective-permute-start(f32[4,128]{1,0:T(4,128)S(1)} %get-tuple-element.67), channel_id=1, source_target_pairs={{0,1},{2,3},{4,13},{14,15},{8,9},{10,11},{12,21},{22,23},{16,17},{... | collective-permute-start | bytes 6152 | tf_op jit(solution)/shard_map/ppermute | solution.py:399
  55.1 4.9 %collective-permute-start.7 = (f32[4,128]{1,0:T(4,128)S(1)}, f32[4,128]{1,0:T(4,128)S(1)}, u32[]{:S(2)}, u32[]{:S(2)}) collective-permute-start(f32[4,128]{1,0:T(4,128)S(1)} %get-tuple-element.68), channel_id=1, source_target_pairs={{1,2},{3,4},{13,14},{15,8},{9,10},{11,12},{21,22},{23,16},{17,18},... | collective-permute-start | bytes 6152 | tf_op jit(solution)/shard_map/ppermute | solution.py:399
  61.1 5.0 %collective-permute-start.8 = (f32[4,128]{1,0:T(4,128)S(1)}, f32[4,128]{1,0:T(4,128)S(1)}, u32[]{:S(2)}, u32[]{:S(2)}) collective-permute-start(f32[4,128]{1,0:T(4,128)S(1)} %get-tuple-element.76), channel_id=1, source_target_pairs={{0,1},{2,3},{4,13},{14,15},{8,9},{10,11},{12,21},{22,23},{16,17},{... | collective-permute-start | bytes 6152 | tf_op jit(solution)/shard_map/ppermute | solution.py:399
  62.4 4.9 %collective-permute-start.9 = (f32[4,128]{1,0:T(4,128)S(1)}, f32[4,128]{1,0:T(4,128)S(1)}, u32[]{:S(2)}, u32[]{:S(2)}) collective-permute-start(f32[4,128]{1,0:T(4,128)S(1)} %get-tuple-element.77), channel_id=1, source_target_pairs={{1,2},{3,4},{13,14},{15,8},{9,10},{11,12},{21,22},{23,16},{17,18},... | collective-permute-start | bytes 6152 | tf_op jit(solution)/shard_map/ppermute | solution.py:399
  68.4 6.5 %collective-permute-start.10 = (f32[4,128]{1,0:T(4,128)S(1)}, f32[4,128]{1,0:T(4,128)S(1)}, u32[]{:S(2)}, u32[]{:S(2)}) collective-permute-start(f32[4,128]{1,0:T(4,128)S(1)} %get-tuple-element.80), channel_id=1, source_target_pairs={{0,1},{2,3},{4,13},{14,15},{8,9},{10,11},{12,21},{22,23},{16,17},{... | collective-permute-start | bytes 6152 | tf_op jit(solution)/shard_map/ppermute | solution.py:399
  70.3 4.9 %collective-permute-start.11 = (f32[4,128]{1,0:T(4,128)S(1)}, f32[4,128]{1,0:T(4,128)S(1)}, u32[]{:S(2)}, u32[]{:S(2)}) collective-permute-start(f32[4,128]{1,0:T(4,128)S(1)} %get-tuple-element.81), channel_id=1, source_target_pairs={{1,2},{3,4},{13,14},{15,8},{9,10},{11,12},{21,22},{23,16},{17,18},... | collective-permute-start | bytes 6152 | tf_op jit(solution)/shard_map/ppermute | solution.py:399
  76.3 5.1 %collective-permute-start.12 = (f32[4,128]{1,0:T(4,128)S(1)}, f32[4,128]{1,0:T(4,128)S(1)}, u32[]{:S(2)}, u32[]{:S(2)}) collective-permute-start(f32[4,128]{1,0:T(4,128)S(1)} %get-tuple-element.88), channel_id=1, source_target_pairs={{0,1},{2,3},{4,13},{14,15},{8,9},{10,11},{12,21},{22,23},{16,17},{... | collective-permute-start | bytes 6152 | tf_op jit(solution)/shard_map/ppermute | solution.py:399
  77.6 4.9 %collective-permute-start.13 = (f32[4,128]{1,0:T(4,128)S(1)}, f32[4,128]{1,0:T(4,128)S(1)}, u32[]{:S(2)}, u32[]{:S(2)}) collective-permute-start(f32[4,128]{1,0:T(4,128)S(1)} %get-tuple-element.89), channel_id=1, source_target_pairs={{1,2},{3,4},{13,14},{15,8},{9,10},{11,12},{21,22},{23,16},{17,18},... | collective-permute-start | bytes 6152 | tf_op jit(solution)/shard_map/ppermute | solution.py:399
  84.0 5.6 %collective-permute-start.14 = (f32[32,128]{1,0:T(8,128)S(1)}, f32[32,128]{1,0:T(8,128)S(1)}, u32[]{:S(2)}, u32[]{:S(2)}) collective-permute-start(f32[32,128]{1,0:T(8,128)S(1)} %jacobi_last.1), channel_id=1, source_target_pairs={{0,0},{1,1},{2,2},{3,3},{4,4},{13,5},{14,6},{15,7},{8,8},{9,9},{10... | collective-permute-start | bytes 49160 | tf_op jit(solution)/shard_map/ppermute | solution.py:578

commit v6 on v5

--- a/solution.py
+++ b/solution.py
@@ -175,18 +175,26 @@
     spread_columns(cols, [arranged[f] for f in range(5)], TD, 0)
 
 
-def density_body(
+def density_edge(
     mem, table, arranged, first, second, held, dens, ext, dist, out1, out2, cols, near, sem
 ):
-    listed = pltpu.make_async_copy(table, near, sem)
-    listed.start()
+    listed = start_list(table, near, sem)
     odd = mem[0] % 2 == 1
     whole = extend(odd, arranged[0:6], first[...], second[...])
     ext[...] = whole
     spread_columns(cols, [whole[f, TD:] for f in range(5)], 2 * GMAX, TD)
     listed.wait()
-
-    def tile(s, carry):
+    send_parts(odd, find_density(HALF, near, arranged, cols, dens, dist), out1, out2)
+
+
+def density_inner(table, arranged, cols, dens, dist, near, sem):
+    start_list(table, near, sem).wait()
+    find_density(0, near, arranged, cols, dens, dist)
+
+
+def find_density(begin, near, arranged, cols, dens, dist):
+    def tile(k, carry):
+        s = begin + k
         own = [arranged[f, pl.ds(s, 1), :] for f in range(5)]
         x_i, y_i, z_i, _, h_i = [jnp.broadcast_to(v, (CHUNK, TILE)) for v in own]
         pace = 2.0 / h_i
@@ -200,42 +208,42 @@
                 dz = cols[2, t, rows, :] - z_i
                 r2 = dx * dx + dy * dy + dz * dz
                 r = r2 * lax.rsqrt(jnp.maximum(r2, 1e-30))
-                dist[s, pl.ds(n * TILE + c * CHUNK, CHUNK), :] = r
+                dist[k, pl.ds(n * TILE + c * CHUNK, CHUNK), :] = r
                 u = jnp.maximum(4.0 - r * pace, 0.0)
                 u2 = u * u
                 total = total + (cols[3, t, rows, :] * (5.0 - u)) * (u2 * u2)
-        dens[pl.ds(s, 1), :] = jnp.sum(total, axis=0, keepdims=True)
+        dens[pl.ds(k, 1), :] = jnp.sum(total, axis=0, keepdims=True)
         return carry
 
-    lax.fori_loop(0, TD, tile, 0)
-    h = arranged[4]
+    lax.fori_loop(0, HALF, tile, 0)
+    h = arranged[4, begin : begin + HALF]
     density = (KERNEL_NORM / 256.0) * dens[...] / (h * h * h)
     dens[...] = density
-    send_parts(odd, density, out1, out2)
-
-
-def forces_body(table, arranged, cols, dist, forces, near, sem):
-    listed = pltpu.make_async_copy(table, near, sem)
-    listed.start()
-    listed.wait()
-
-    def tile(s, carry):
+    return density
+
+
+def forces_body(begin, table, arranged, cols, dist, *refs):
+    *_, forces, near, sem = refs
+    start_list(table, near, sem).wait()
+
+    def tile(k, carry):
+        s = begin + k
         h_i = jnp.broadcast_to(arranged[4, pl.ds(s, 1), :], (CHUNK, TILE))
         for n in range(NB):
             t = near[0, LIST + n * TD + s]
             for c in range(TILE // CHUNK):
                 at = pl.ds(n * TILE + c * CHUNK, CHUNK)
                 reach = cols[4, t, pl.ds(c * CHUNK, CHUNK), :] + h_i
-                w = jnp.maximum(reach - dist[s, at, :], 0.0)
+                w = jnp.maximum(reach - dist[k, at, :], 0.0)
                 p2 = reach * reach
                 q = w / (p2 * p2)
                 force = q * q * w
                 high = force.astype(BF16)
-                forces[s, 0, at, :] = high
-                forces[s, 1, at, :] = (force - high.astype(F32)).astype(BF16)
+                forces[k, 0, at, :] = high
+                forces[k, 1, at, :] = (force - high.astype(F32)).astype(BF16)
         return carry
 
-    lax.fori_loop(0, TD, tile, 0)
+    lax.fori_loop(0, HALF, tile, 0)
 
 
 def prepare(vectors, staged, operand):
@@ -254,7 +262,8 @@
     listed.wait()
     for k, s in enumerate(tiles):
         row = jnp.concatenate([operand[near[0, LIST + n * TD + s]] for n in range(NB)], axis=1)
-        both = jnp.concatenate([forces[s, 0], forces[s, 1]], axis=1)
+        block = forces[k // HALF] if isinstance(forces, tuple) else forces
+        both = jnp.concatenate([block[k % HALF, 0], block[k % HALF, 1]], axis=1)
         got = jnp.dot(row, both, preferred_element_type=F32)
         result[k * height : (k + 1) * height, :] = got[:, TILE:] + got[:, :TILE]
     sums = []
@@ -303,10 +312,10 @@
     *refs, staged, result, near, sem = refs
     listed = start_list(refs[1], near, sem)
     if begin:
-        (mem, _, arranged, ext, forces, dens, d1, d2) = refs[:8]
-        (diff, out1, out2, sums, operand, fixed, dens_ext) = refs[8:]
+        (mem, _, arranged, ext, forces, dens_inner, dens, d1, d2) = refs[:9]
+        (diff, out1, out2, sums, operand, fixed, dens_ext) = refs[9:]
         odd = mem[0] % 2 == 1
-        rho = extend(odd, dens[...], d1[...], d2[...])
+        rho = extend(odd, jnp.concatenate([dens_inner[...], dens[...]], axis=0), d1[...], d2[...])
         dens_ext[...] = rho
         e = ext[5]
     else:
@@ -361,15 +370,15 @@
     vd = ((160.0 * KERNEL_NORM) * ext[3] / rho[...]) * spread
     e = e_ext[5] if len(e_ext.shape) == 3 else e_ext[...]
     if last:
-        dens, done, operand = refs[13:]
+        inner_forces, done, operand = refs[13:]
     else:
         new, out1, out2, operand = refs[13:]
     prepare([vd, vd * e], staged, operand)
     if last:
-        got = weigh(listed, near, forces, operand, result, 2, range(TD))
+        got = weigh(listed, near, (inner_forces, forces), operand, result, 2, range(TD))
         both = [jnp.concatenate([inner_sums[q], sums[q]], axis=0) for q in range(2)]
         value = step_energy(arranged, slice(0, TD), rho, both, own, got)
-        for k, v in enumerate((value, dens[...])):
+        for k, v in enumerate((value, rho[:TD])):
             done[k * TD : k * TD + GMAX] = v[HALF : HALF + GMAX]
             done[k * TD + GMAX : k * TD + GMAX + HALF] = v[:HALF]
             done[k * TD + GMAX + HALF : (k + 1) * TD] = v[HALF + GMAX :]
@@ -456,18 +465,14 @@
     table = (mem, near)
     s1, s2 = swap(s1, s2)
     (cols,) = call(columns_body, [((5, EXT, TILE, TILE), F32)], [], "columns", arranged)
-    density, ext, dist, r1, r2, cols = call(
-        density_body,
-        [
-            own,
-            ((6, EXT, TILE), F32),
-            ((TD, NB * TILE, TILE), F32),
-            edge,
-            edge,
-            ((5, EXT, TILE, TILE), F32),
-        ],
+    half = ((HALF, TILE), F32)
+    apart = ((HALF, NB * TILE, TILE), F32)
+    block = ((HALF, 2, NB * TILE, TILE), BF16)
+    dens, ext, dist, r1, r2, cols = call(
+        density_edge,
+        [half, ((6, EXT, TILE), F32), apart, edge, edge, ((5, EXT, TILE, TILE), F32)],
         LISTED,
-        "density",
+        "density_edge",
         *table,
         arranged,
         s1,
@@ -476,18 +481,20 @@
         alias={5: 5},
     )
     r1, r2 = swap(r1, r2)
+    dens_inner, inner_dist = call(
+        density_inner, [half, apart], LISTED, "density_inner", near, arranged, cols
+    )
     (forces,) = call(
-        forces_body,
-        [((TD, 2, NB * TILE, TILE), BF16)],
+        lambda *refs: forces_body(HALF, *refs),
+        [block],
         LISTED,
-        "forces",
+        "forces_edge",
         near,
         arranged,
         cols,
         dist,
     )
     shared = (*table, arranged, ext, forces)
-    half = ((HALF, TILE), F32)
     pair = ((2, HALF, TILE), F32)
     four = ((4, HALF, TILE), F32)
     for step in range(SWEEPS):
@@ -501,7 +508,8 @@
                 workspace(height, HALF, True),
                 "limiter_first_edge",
                 *shared,
-                density,
+                dens_inner,
+                dens,
                 r1,
                 r2,
             )
@@ -521,6 +529,18 @@
                 e2,
             )
         d1, d2 = swap(d1, d2)
+        if begin:
+            (inner_forces,) = call(
+                lambda *refs: forces_body(0, *refs),
+                [block],
+                LISTED,
+                "forces_inner",
+                near,
+                arranged,
+                cols,
+                inner_dist,
+                diff,
+            )
         results = call(
             lambda *refs: limiter_inner(begin, *refs),
             [half, pair, four] if begin else [half, pair],
@@ -529,7 +549,7 @@
             near,
             arranged,
             ext,
-            forces,
+            inner_forces,
             dens_ext,
             e_ext,
             rows,
@@ -555,7 +575,7 @@
             diff,
             d1,
             d2,
-            *((density,) if last else ()),
+            *((inner_forces,) if last else ()),
         )
         if last:
             done = results[0]
@@ -569,7 +589,7 @@
                 "jacobi_inner",
                 near,
                 arranged,
-                forces,
+                inner_forces,
                 dens_ext,
                 rows,
                 inner_sums,

time: 90.6 us -> 90.5 us (level)
  Pallas kernels: 24.7 us -> 25.8 us
  starting transfers between devices: 32.3 us -> 31.2 us
    ppermute x14, starting transfers between devices: 30.4 us -> 29.2 us  [swap(): got.append(lax.ppermute(value, AXES, pairs + [(b, a) for a, b in pairs]))]
    pallas_call x15 -> x17, Pallas kernels: 23.4 us -> 24.5 us  [call(): pl.pallas_call(body, out_shape=[jax.ShapeDtypeStruct(shape, dtype) for sh...]
  transfers between devices with their start and end apart: 15 -> 15, of which waited for: 7 -> 6; matrix products, arithmetic and copies ran while one was open for 0% -> 0% of each run, Pallas kernels for 12% -> 15%
where the time goes in v6:
time: 90.5 us; the launch traced here: 90.1 us
  starting transfers between devices  31.2 us (34%)
  Pallas kernels  25.8 us (29%)
  blocking collectives  23.8 us (26%)
  waiting for transfers between devices  7.87 us (9%)
  between operations  0.92 us (1%)
    ppermute x14, starting transfers between devices, swap(): got.append(lax.ppermute(value, AXES, pairs + [(b, a) for a, b in pairs]))  29.2 us
    pallas_call x17, Pallas kernels, call(): pl.pallas_call(body, out_shape=[jax.ShapeDtypeStruct(shape, dtype) for sh...  24.5 us
    all_to_all x1, blocking collectives, local(): lax.all_to_all(outgoing.reshape(GROUPS * ROWS, 1, TILE), 'group', split_a...  23.8 us
    ppermute x14, waiting for transfers between devices, swap(): got.append(lax.ppermute(value, AXES, pairs + [(b, a) for a, b in pairs]))  4.16 us
    ppermute x1, waiting for transfers between devices, local(): done = lax.ppermute(done, AXES, [(owner(s), s) for s in range(GROUPS * 8)])  3.7 us
    ppermute x1, starting transfers between devices, local(): done = lax.ppermute(done, AXES, [(owner(s), s) for s in range(GROUPS * 8)])  1.92 us
  transfers between devices with their start and end apart: 15, of which 6 were waited for; matrix products, arithmetic and copies ran while one was open for 0% of the time, Pallas kernels for 15%

profile of v6, /device:TPU:24, one launch (start us, length us, event | category | flops | bytes accessed | tf_op | source)
XLA Modules:
  0.0 90.1 jit_solution(13516252561327823496)
XLA Ops:
  0.6 1.3 %pack.1 = f32[544,128]{1,0:T(8,128)S(1)} custom-call(s32[1]{0:T(128)} %bitcast.1.grp, s32[1]{0:T(128)} %bitcast.mem.refs_0_, s32[1,2]{1,0:T(1,128)} %ghosts_hbm.1, s32[16]{0:T(128)} %slot_hbm.1, s32[6,16]{1,0:T(8,128)} %bitcast.13, f32[8,2048]{1,0:T(8,128)} %part_hbm.1), custom_call_target="tpu_custom_call" | custom-call | tf_op jit(solution)/shard_map/pack/pallas_call | solution.py:415
  2.0 23.8 %all_to_all.5 = f32[544,1,128]{2,1,0:T(1,128)S(1)} all-to-all(f32[544,1,128]{2,1,0:T(1,128)S(1)} %bitcast.12), channel_id=1, replica_groups=mesh['group'=32,'member'=8] {'group'}, dimensions={0} | all-to-all | bytes 557056 | tf_op jit(solution)/shard_map/all_to_all | solution.py:445
  26.1 2.6 %collective-permute-start.1 = (f32[6,4,128]{2,1,0:T(4,128)S(1)}, f32[6,4,128]{2,1,0:T(4,128)S(1)}, u32[]{:S(2)}, u32[]{:S(2)}) collective-permute-start(f32[6,4,128]{2,1,0:T(4,128)S(1)} %get-tuple-element.51), channel_id=1, source_target_pairs={{1,2},{3,4},{13,14},{15,8},{9,10},{11,12},{21,22},{23,16},{17,18},... | collective-permute-start | bytes 36872 | tf_op jit(solution)/shard_map/ppermute | solution.py:408
  28.8 1.6 %columns.1.held = f32[5,24,128,128]{3,2,1,0:T(8,128)S(1)} custom-call(f32[8,16,128]{2,1,0:T(8,128)S(1)} %get-tuple-element.49.arranged.refs_1_.refs_2_), custom_call_target="tpu_custom_call" | custom-call | tf_op jit(solution)/shard_map/columns/pallas_call | solution.py:36
  31.1 3.2 %density_edge.1 = (f32[8,128]{1,0:T(8,128)S(1)}, f32[6,24,128]{2,1,0:T(8,128)S(1)}, f32[8,768,128]{2,1,0:T(8,128)S(1)}, f32[4,128]{1,0:T(4,128)S(1)}, f32[4,128]...) custom-call(s32[1]{0:T(128)} %bitcast.mem.refs_0_, ...), custom_call_target="tpu_custom_call", output_to_operand_aliasing={{5}: (5, {})} | custom-call | tf_op jit(solution)/shard_map/density_edge/pallas_call | solution.py:36
  34.3 3.0 %collective-permute-start.2 = (f32[4,128]{1,0:T(4,128)S(1)}, f32[4,128]{1,0:T(4,128)S(1)}, u32[]{:S(2)}, u32[]{:S(2)}) collective-permute-start(f32[4,128]{1,0:T(4,128)S(1)} %get-tuple-element.57), channel_id=1, source_target_pairs={{0,1},{2,3},{4,13},{14,15},{8,9},{10,11},{12,21},{22,23},{16,17},{... | collective-permute-start | bytes 6152 | tf_op jit(solution)/shard_map/ppermute | solution.py:408
  37.3 1.9 %collective-permute-start.3 = (f32[4,128]{1,0:T(4,128)S(1)}, f32[4,128]{1,0:T(4,128)S(1)}, u32[]{:S(2)}, u32[]{:S(2)}) collective-permute-start(f32[4,128]{1,0:T(4,128)S(1)} %get-tuple-element.58), channel_id=1, source_target_pairs={{1,2},{3,4},{13,14},{15,8},{9,10},{11,12},{21,22},{23,16},{17,18},... | collective-permute-start | bytes 6152 | tf_op jit(solution)/shard_map/ppermute | solution.py:408
  39.2 2.8 %density_inner.1 = (f32[8,128]{1,0:T(8,128)S(1)}, f32[8,768,128]{2,1,0:T(8,128)S(1)}) custom-call(s32[1,128]{1,0:T(1,128)S(1)} %get-tuple-element.48.table.refs_0_.refs_1_, f32[8,16,128]{2,1,0:T(8,128)S(1)} %get-tuple-element.49.arranged.refs_1_.refs_2_, f32[5,24,128,128]{3,2,1,0:T(8,128)S(1)} %get-tuple-element.53.refs_2_.cols), custom_call_target="tpu_custom_call" | custom-call | tf_op jit(solution)/shard_map/density_inner/pallas_call | solution.py:36
  42.0 1.9 %forces_edge.1.refs_4_ = bf16[8,2,768,128]{3,2,1,0:T(8,128)(2,1)S(1)} custom-call(s32[1,128]{1,0:T(1,128)S(1)} %get-tuple-element.48.table.refs_0_.refs_1_, f32[8,16,128]{2,1,0:T(8,128)S(1)} %get-tuple-element.49.arranged.refs_1_.refs_2_, f32[5,24,128,128]{3,2,1,0:T(8,128)S(1)} %get-tuple-element.53.refs_2_.cols, f32[8,768,128]{2,1,0:T(8,128)S(1)} %get-tuple-element.54.refs_3_), custom_call_target="tpu_custom_call" | custom-call | tf_op jit(solution)/shard_map/forces_edge/pallas_call | solution.py:36
  43.9 1.3 %limiter_first_edge.1 = (f32[8,128]{1,0:T(8,128)S(1)}, f32[4,128]{1,0:T(4,128)S(1)}, f32[4,128]{1,0:T(4,128)S(1)}, f32[2,8,128]{2,1,0:T(8,128)S(1)}, bf16[24,24,...) custom-call(s32[1]{0:T(128)} %bitcast.mem.refs_0_, ...), custom_call_target="tpu_custom_call" | custom-call | tf_op jit(solution)/shard_map/limiter_first_edge/pallas_call | solution.py:36
  45.6 3.3 %collective-permute-start.5 = (f32[4,128]{1,0:T(4,128)S(1)}, f32[4,128]{1,0:T(4,128)S(1)}, u32[]{:S(2)}, u32[]{:S(2)}) collective-permute-start(f32[4,128]{1,0:T(4,128)S(1)} %get-tuple-element.68), channel_id=1, source_target_pairs={{1,2},{3,4},{13,14},{15,8},{9,10},{11,12},{21,22},{23,16},{17,18},... | collective-permute-start | bytes 6152 | tf_op jit(solution)/shard_map/ppermute | solution.py:408
  48.9 1.9 %forces_inner.1.refs_3_.forces.refs_13_ = bf16[8,2,768,128]{3,2,1,0:T(8,128)(2,1)S(1)} custom-call(s32[1,128]{1,0:T(1,128)S(1)} %get-tuple-element.48.table.refs_0_.refs_1_, f32[8,16,128]{2,1,0:T(8,128)S(1)} %get-tuple-element.49.arranged.refs_1_.refs_2_, f32[5,24,128,128]{3,2,1,0:T(8,128)S(1)} %get-tuple-element.53.refs_2_.cols, ...), custom_call_target="tpu_custom_call" | custom-call | tf_op jit(solution)/shard_map/forces_inner/pallas_call | solution.py:36
  50.8 1.2 %limiter_first_inner.1 = (f32[8,128]{1,0:T(8,128)S(1)}, f32[2,8,128]{2,1,0:T(8,128)S(1)}, f32[4,8,128]{2,1,0:T(8,128)S(1)}) custom-call(s32[1,128]{1,0:T(1,128)S(1)} %get-tuple-element.48.table.refs_0_.refs_1_, f32[8,16,128]{2,1,0:T(8,128)S(1)} %get-tuple-element.49.arranged.refs_1_.refs_2_, ...), custom_call_target="tpu_custom_call" | custom-call | tf_op jit(solution)/shard_map/limiter_first_inner/pallas_call | solution.py:36
  52.1 1.1 %jacobi_edge.2 = (f32[8,128]{1,0:T(8,128)S(1)}, f32[4,128]{1,0:T(4,128)S(1)}, f32[4,128]{1,0:T(4,128)S(1)}, bf16[24,8,128]{2,1,0:T(8,128)(2,1)S(1)}) custom-call(s32[1]{0:T(128)} %bitcast.mem.refs_0_, s32[1,128]{1,0:T(1,128)S(1)} %get-tuple-element.48.table.refs_0_.refs_1_, f32[8,16,128]{2,1,0:T(8,128)S(1)} %get-tuple-element.49.arranged.refs_1_.refs_2_, ...), custom_call_target="tpu_custom_call" | custom-call | tf_op jit(solution)/shard_map/jacobi_edge/pallas_call | solution.py:36
  53.2 1.3 %collective-permute-start.6 = (f32[4,128]{1,0:T(4,128)S(1)}, f32[4,128]{1,0:T(4,128)S(1)}, u32[]{:S(2)}, u32[]{:S(2)}) collective-permute-start(f32[4,128]{1,0:T(4,128)S(1)} %get-tuple-element.71), channel_id=1, source_target_pairs={{0,1},{2,3},{4,13},{14,15},{8,9},{10,11},{12,21},{22,23},{16,17},{... | collective-permute-start | bytes 6152 | tf_op jit(solution)/shard_map/ppermute | solution.py:408
  54.5 3.6 %collective-permute-start.7 = (f32[4,128]{1,0:T(4,128)S(1)}, f32[4,128]{1,0:T(4,128)S(1)}, u32[]{:S(2)}, u32[]{:S(2)}) collective-permute-start(f32[4,128]{1,0:T(4,128)S(1)} %get-tuple-element.72), channel_id=1, source_target_pairs={{1,2},{3,4},{13,14},{15,8},{9,10},{11,12},{21,22},{23,16},{17,18},... | collective-permute-start | bytes 6152 | tf_op jit(solution)/shard_map/ppermute | solution.py:408
  59.4 1.1 %limiter_edge.2 = (f32[8,128]{1,0:T(8,128)S(1)}, f32[4,128]{1,0:T(4,128)S(1)}, f32[4,128]{1,0:T(4,128)S(1)}, f32[2,8,128]{2,1,0:T(8,128)S(1)}, bf16[24,16,128]{2,1,0:T(8,128)(2,1)S(1)}, /*index=5*/f32[24,128]{1,0:T(8,128)S(1)}) custom-call(s32[1]{0:T(128)} %bitcast.mem.refs_0_, s32[1,128]{1,0:T(1,128)S(1)} %get-tuple-element.48.table.refs_0_.refs_1_, ...), custom_call_target="tpu_custom_call" | custom-call | tf_op jit(solution)/shard_map/limiter_edge/pallas_call | solution.py:36
  60.5 1.8 %collective-permute-start.8 = (f32[4,128]{1,0:T(4,128)S(1)}, f32[4,128]{1,0:T(4,128)S(1)}, u32[]{:S(2)}, u32[]{:S(2)}) collective-permute-start(f32[4,128]{1,0:T(4,128)S(1)} %get-tuple-element.80), channel_id=1, source_target_pairs={{0,1},{2,3},{4,13},{14,15},{8,9},{10,11},{12,21},{22,23},{16,17},{... | collective-permute-start | bytes 6152 | tf_op jit(solution)/shard_map/ppermute | solution.py:408
  62.3 2.2 %collective-permute-start.9 = (f32[4,128]{1,0:T(4,128)S(1)}, f32[4,128]{1,0:T(4,128)S(1)}, u32[]{:S(2)}, u32[]{:S(2)}) collective-permute-start(f32[4,128]{1,0:T(4,128)S(1)} %get-tuple-element.81), channel_id=1, source_target_pairs={{1,2},{3,4},{13,14},{15,8},{9,10},{11,12},{21,22},{23,16},{17,18},... | collective-permute-start | bytes 6152 | tf_op jit(solution)/shard_map/ppermute | solution.py:408
  64.6 1.1 %limiter_inner.2 = (f32[8,128]{1,0:T(8,128)S(1)}, f32[2,8,128]{2,1,0:T(8,128)S(1)}) custom-call(s32[1,128]{1,0:T(1,128)S(1)} %get-tuple-element.48.table.refs_0_.refs_1_, f32[8,16,128]{2,1,0:T(8,128)S(1)} %get-tuple-element.49.arranged.refs_1_.refs_2_, f32[6,24,128]{2,1,0:T(8,128)S(1)} %get-tuple-element.52.refs_3_.refs_2_.refs_5_.refs_6_, ...), custom_call_target="tpu_custom_call" | custom-call | tf_op jit(solution)/shard_map/limiter_inner/pallas_call | solution.py:36
  65.7 1.5 %collective-permute-done.9.refs_12_ = f32[4,128]{1,0:T(4,128)S(1)} collective-permute-done((f32[4,128]{1,0:T(4,128)S(1)}, f32[4,128]{1,0:T(4,128)S(1)}, u32[]{:S(2)}, u32[]{:S(2)}) %collective-permute-start.9) | collective-permute-done | bytes 2080 | tf_op jit(solution)/shard_map/ppermute | solution.py:408
  67.2 1.1 %jacobi_edge.3 = (f32[8,128]{1,0:T(8,128)S(1)}, f32[4,128]{1,0:T(4,128)S(1)}, f32[4,128]{1,0:T(4,128)S(1)}, bf16[24,8,128]{2,1,0:T(8,128)(2,1)S(1)}) custom-call(s32[1]{0:T(128)} %bitcast.mem.refs_0_, s32[1,128]{1,0:T(1,128)S(1)} %get-tuple-element.48.table.refs_0_.refs_1_, f32[8,16,128]{2,1,0:T(8,128)S(1)} %get-tuple-element.49.arranged.refs_1_.refs_2_, ...), custom_call_target="tpu_custom_call" | custom-call | tf_op jit(solution)/shard_map/jacobi_edge/pallas_call | solution.py:36
  68.3 1.3 %collective-permute-start.10 = (f32[4,128]{1,0:T(4,128)S(1)}, f32[4,128]{1,0:T(4,128)S(1)}, u32[]{:S(2)}, u32[]{:S(2)}) collective-permute-start(f32[4,128]{1,0:T(4,128)S(1)} %get-tuple-element.84), channel_id=1, source_target_pairs={{0,1},{2,3},{4,13},{14,15},{8,9},{10,11},{12,21},{22,23},{16,17},{... | collective-permute-start | bytes 6152 | tf_op jit(solution)/shard_map/ppermute | solution.py:408
  69.6 3.6 %collective-permute-start.11 = (f32[4,128]{1,0:T(4,128)S(1)}, f32[4,128]{1,0:T(4,128)S(1)}, u32[]{:S(2)}, u32[]{:S(2)}) collective-permute-start(f32[4,128]{1,0:T(4,128)S(1)} %get-tuple-element.85), channel_id=1, source_target_pairs={{1,2},{3,4},{13,14},{15,8},{9,10},{11,12},{21,22},{23,16},{17,18},... | collective-permute-start | bytes 6152 | tf_op jit(solution)/shard_map/ppermute | solution.py:408
  74.5 1.1 %limiter_edge.3 = (f32[8,128]{1,0:T(8,128)S(1)}, f32[4,128]{1,0:T(4,128)S(1)}, f32[4,128]{1,0:T(4,128)S(1)}, f32[2,8,128]{2,1,0:T(8,128)S(1)}, bf16[24,16,128]{2,1,0:T(8,128)(2,1)S(1)}, /*index=5*/f32[24,128]{1,0:T(8,128)S(1)}) custom-call(s32[1]{0:T(128)} %bitcast.mem.refs_0_, s32[1,128]{1,0:T(1,128)S(1)} %get-tuple-element.48.table.refs_0_.refs_1_, ...), custom_call_target="tpu_custom_call" | custom-call | tf_op jit(solution)/shard_map/limiter_edge/pallas_call | solution.py:36
  75.7 1.8 %collective-permute-start.12 = (f32[4,128]{1,0:T(4,128)S(1)}, f32[4,128]{1,0:T(4,128)S(1)}, u32[]{:S(2)}, u32[]{:S(2)}) collective-permute-start(f32[4,128]{1,0:T(4,128)S(1)} %get-tuple-element.92), channel_id=1, source_target_pairs={{0,1},{2,3},{4,13},{14,15},{8,9},{10,11},{12,21},{22,23},{16,17},{... | collective-permute-start | bytes 6152 | tf_op jit(solution)/shard_map/ppermute | solution.py:408
  77.5 2.2 %collective-permute-start.13 = (f32[4,128]{1,0:T(4,128)S(1)}, f32[4,128]{1,0:T(4,128)S(1)}, u32[]{:S(2)}, u32[]{:S(2)}) collective-permute-start(f32[4,128]{1,0:T(4,128)S(1)} %get-tuple-element.93), channel_id=1, source_target_pairs={{1,2},{3,4},{13,14},{15,8},{9,10},{11,12},{21,22},{23,16},{17,18},... | collective-permute-start | bytes 6152 | tf_op jit(solution)/shard_map/ppermute | solution.py:408
  79.7 1.1 %limiter_inner.3 = (f32[8,128]{1,0:T(8,128)S(1)}, f32[2,8,128]{2,1,0:T(8,128)S(1)}) custom-call(s32[1,128]{1,0:T(1,128)S(1)} %get-tuple-element.48.table.refs_0_.refs_1_, f32[8,16,128]{2,1,0:T(8,128)S(1)} %get-tuple-element.49.arranged.refs_1_.refs_2_, f32[6,24,128]{2,1,0:T(8,128)S(1)} %get-tuple-element.52.refs_3_.refs_2_.refs_5_.refs_6_, ...), custom_call_target="tpu_custom_call" | custom-call | tf_op jit(solution)/shard_map/limiter_inner/pallas_call | solution.py:36
  80.8 1.5 %collective-permute-done.13.refs_12_ = f32[4,128]{1,0:T(4,128)S(1)} collective-permute-done((f32[4,128]{1,0:T(4,128)S(1)}, f32[4,128]{1,0:T(4,128)S(1)}, u32[]{:S(2)}, u32[]{:S(2)}) %collective-permute-start.13) | collective-permute-done | bytes 2080 | tf_op jit(solution)/shard_map/ppermute | solution.py:408
  82.4 1.5 %jacobi_last.1 = f32[32,128]{1,0:T(8,128)S(1)} custom-call(s32[1]{0:T(128)} %bitcast.mem.refs_0_, s32[1,128]{1,0:T(1,128)S(1)} %get-tuple-element.48.table.refs_0_.refs_1_, f32[8,16,128]{2,1,0:T(8,128)S(1)} %get-tuple-element.49.arranged.refs_1_.refs_2_, f32[6,24,128]{2,1,0:T(8,128)S(1)} %get-tuple-element.52.refs_3_.refs_2_.refs_5_.refs_6_, ...), custom_call_target="tpu_custom_call" | custom-call | tf_op jit(solution)/shard_map/jacobi_last/pallas_call | solution.py:36
  83.9 1.9 %collective-permute-start.14 = (f32[32,128]{1,0:T(8,128)S(1)}, f32[32,128]{1,0:T(8,128)S(1)}, u32[]{:S(2)}, u32[]{:S(2)}) collective-permute-start(f32[32,128]{1,0:T(8,128)S(1)} %jacobi_last.1), channel_id=1, source_target_pairs={{0,0},{1,1},{2,2},{3,3},{4,4},{13,5},{14,6},{15,7},{8,8},{9,9},{10... | collective-permute-start | bytes 49160 | tf_op jit(solution)/shard_map/ppermute | solution.py:598
  85.8 3.7 %collective-permute-done.14 = f32[32,128]{1,0:T(8,128)S(1)} collective-permute-done((f32[32,128]{1,0:T(8,128)S(1)}, f32[32,128]{1,0:T(8,128)S(1)}, u32[]{:S(2)}, u32[]{:S(2)}) %collective-permute-start.14) | collective-permute-done | bytes 16416 | tf_op jit(solution)/shard_map/ppermute | solution.py:598
  (18 shorter events, 4.7 us)
Async XLA Ops:
  26.1 4.3 %collective-permute-start = (f32[6,4,128]{2,1,0:T(4,128)S(1)}, f32[6,4,128]{2,1,0:T(4,128)S(1)}, u32[]{:S(2)}, u32[]{:S(2)}) collective-permute-start(f32[6,4,128]{2,1,0:T(4,128)S(1)} %get-tuple-element.50), channel_id=1, source_target_pairs={{0,1},{2,3},{4,13},{14,15},{8,9},{10,11},{12,21},{22,23},{16,17},{... | collective-permute-start | bytes 36872 | tf_op jit(solution)/shard_map/ppermute | solution.py:408
  26.1 5.0 %collective-permute-start.1 = (f32[6,4,128]{2,1,0:T(4,128)S(1)}, f32[6,4,128]{2,1,0:T(4,128)S(1)}, u32[]{:S(2)}, u32[]{:S(2)}) collective-permute-start(f32[6,4,128]{2,1,0:T(4,128)S(1)} %get-tuple-element.51), channel_id=1, source_target_pairs={{1,2},{3,4},{13,14},{15,8},{9,10},{11,12},{21,22},{23,16},{17,18},... | collective-permute-start | bytes 36872 | tf_op jit(solution)/shard_map/ppermute | solution.py:408
  34.3 9.6 %collective-permute-start.2 = (f32[4,128]{1,0:T(4,128)S(1)}, f32[4,128]{1,0:T(4,128)S(1)}, u32[]{:S(2)}, u32[]{:S(2)}) collective-permute-start(f32[4,128]{1,0:T(4,128)S(1)} %get-tuple-element.57), channel_id=1, source_target_pairs={{0,1},{2,3},{4,13},{14,15},{8,9},{10,11},{12,21},{22,23},{16,17},{... | collective-permute-start | bytes 6152 | tf_op jit(solution)/shard_map/ppermute | solution.py:408
  37.3 6.6 %collective-permute-start.3 = (f32[4,128]{1,0:T(4,128)S(1)}, f32[4,128]{1,0:T(4,128)S(1)}, u32[]{:S(2)}, u32[]{:S(2)}) collective-permute-start(f32[4,128]{1,0:T(4,128)S(1)} %get-tuple-element.58), channel_id=1, source_target_pairs={{1,2},{3,4},{13,14},{15,8},{9,10},{11,12},{21,22},{23,16},{17,18},... | collective-permute-start | bytes 6152 | tf_op jit(solution)/shard_map/ppermute | solution.py:408
  45.2 6.9 %collective-permute-start.4 = (f32[4,128]{1,0:T(4,128)S(1)}, f32[4,128]{1,0:T(4,128)S(1)}, u32[]{:S(2)}, u32[]{:S(2)}) collective-permute-start(f32[4,128]{1,0:T(4,128)S(1)} %get-tuple-element.67), channel_id=1, source_target_pairs={{0,1},{2,3},{4,13},{14,15},{8,9},{10,11},{12,21},{22,23},{16,17},{... | collective-permute-start | bytes 6152 | tf_op jit(solution)/shard_map/ppermute | solution.py:408
  45.6 6.5 %collective-permute-start.5 = (f32[4,128]{1,0:T(4,128)S(1)}, f32[4,128]{1,0:T(4,128)S(1)}, u32[]{:S(2)}, u32[]{:S(2)}) collective-permute-start(f32[4,128]{1,0:T(4,128)S(1)} %get-tuple-element.68), channel_id=1, source_target_pairs={{1,2},{3,4},{13,14},{15,8},{9,10},{11,12},{21,22},{23,16},{17,18},... | collective-permute-start | bytes 6152 | tf_op jit(solution)/shard_map/ppermute | solution.py:408
  53.2 6.0 %collective-permute-start.6 = (f32[4,128]{1,0:T(4,128)S(1)}, f32[4,128]{1,0:T(4,128)S(1)}, u32[]{:S(2)}, u32[]{:S(2)}) collective-permute-start(f32[4,128]{1,0:T(4,128)S(1)} %get-tuple-element.71), channel_id=1, source_target_pairs={{0,1},{2,3},{4,13},{14,15},{8,9},{10,11},{12,21},{22,23},{16,17},{... | collective-permute-start | bytes 6152 | tf_op jit(solution)/shard_map/ppermute | solution.py:408
  54.5 4.9 %collective-permute-start.7 = (f32[4,128]{1,0:T(4,128)S(1)}, f32[4,128]{1,0:T(4,128)S(1)}, u32[]{:S(2)}, u32[]{:S(2)}) collective-permute-start(f32[4,128]{1,0:T(4,128)S(1)} %get-tuple-element.72), channel_id=1, source_target_pairs={{1,2},{3,4},{13,14},{15,8},{9,10},{11,12},{21,22},{23,16},{17,18},... | collective-permute-start | bytes 6152 | tf_op jit(solution)/shard_map/ppermute | solution.py:408
  60.5 5.2 %collective-permute-start.8 = (f32[4,128]{1,0:T(4,128)S(1)}, f32[4,128]{1,0:T(4,128)S(1)}, u32[]{:S(2)}, u32[]{:S(2)}) collective-permute-start(f32[4,128]{1,0:T(4,128)S(1)} %get-tuple-element.80), channel_id=1, source_target_pairs={{0,1},{2,3},{4,13},{14,15},{8,9},{10,11},{12,21},{22,23},{16,17},{... | collective-permute-start | bytes 6152 | tf_op jit(solution)/shard_map/ppermute | solution.py:408
  62.3 4.9 %collective-permute-start.9 = (f32[4,128]{1,0:T(4,128)S(1)}, f32[4,128]{1,0:T(4,128)S(1)}, u32[]{:S(2)}, u32[]{:S(2)}) collective-permute-start(f32[4,128]{1,0:T(4,128)S(1)} %get-tuple-element.81), channel_id=1, source_target_pairs={{1,2},{3,4},{13,14},{15,8},{9,10},{11,12},{21,22},{23,16},{17,18},... | collective-permute-start | bytes 6152 | tf_op jit(solution)/shard_map/ppermute | solution.py:408
  68.3 6.0 %collective-permute-start.10 = (f32[4,128]{1,0:T(4,128)S(1)}, f32[4,128]{1,0:T(4,128)S(1)}, u32[]{:S(2)}, u32[]{:S(2)}) collective-permute-start(f32[4,128]{1,0:T(4,128)S(1)} %get-tuple-element.84), channel_id=1, source_target_pairs={{0,1},{2,3},{4,13},{14,15},{8,9},{10,11},{12,21},{22,23},{16,17},{... | collective-permute-start | bytes 6152 | tf_op jit(solution)/shard_map/ppermute | solution.py:408
  69.6 4.9 %collective-permute-start.11 = (f32[4,128]{1,0:T(4,128)S(1)}, f32[4,128]{1,0:T(4,128)S(1)}, u32[]{:S(2)}, u32[]{:S(2)}) collective-permute-start(f32[4,128]{1,0:T(4,128)S(1)} %get-tuple-element.85), channel_id=1, source_target_pairs={{1,2},{3,4},{13,14},{15,8},{9,10},{11,12},{21,22},{23,16},{17,18},... | collective-permute-start | bytes 6152 | tf_op jit(solution)/shard_map/ppermute | solution.py:408
  75.7 5.2 %collective-permute-start.12 = (f32[4,128]{1,0:T(4,128)S(1)}, f32[4,128]{1,0:T(4,128)S(1)}, u32[]{:S(2)}, u32[]{:S(2)}) collective-permute-start(f32[4,128]{1,0:T(4,128)S(1)} %get-tuple-element.92), channel_id=1, source_target_pairs={{0,1},{2,3},{4,13},{14,15},{8,9},{10,11},{12,21},{22,23},{16,17},{... | collective-permute-start | bytes 6152 | tf_op jit(solution)/shard_map/ppermute | solution.py:408
  77.5 4.9 %collective-permute-start.13 = (f32[4,128]{1,0:T(4,128)S(1)}, f32[4,128]{1,0:T(4,128)S(1)}, u32[]{:S(2)}, u32[]{:S(2)}) collective-permute-start(f32[4,128]{1,0:T(4,128)S(1)} %get-tuple-element.93), channel_id=1, source_target_pairs={{1,2},{3,4},{13,14},{15,8},{9,10},{11,12},{21,22},{23,16},{17,18},... | collective-permute-start | bytes 6152 | tf_op jit(solution)/shard_map/ppermute | solution.py:408
  83.9 5.6 %collective-permute-start.14 = (f32[32,128]{1,0:T(8,128)S(1)}, f32[32,128]{1,0:T(8,128)S(1)}, u32[]{:S(2)}, u32[]{:S(2)}) collective-permute-start(f32[32,128]{1,0:T(8,128)S(1)} %jacobi_last.1), channel_id=1, source_target_pairs={{0,0},{1,1},{2,2},{3,3},{4,4},{13,5},{14,6},{15,7},{8,8},{9,9},{10... | collective-permute-start | bytes 49160 | tf_op jit(solution)/shard_map/ppermute | solution.py:598

commit v7 on v6

--- a/solution.py
+++ b/solution.py
@@ -80,7 +80,7 @@
         out[g * ROWS + 16 : g * ROWS + 17, :] = jnp.full((1, TILE), -1.0, F32)
     lane = lax.broadcasted_iota(jnp.int32, (1, TILE), 1)
     m = mem[0]
-    for copy in copies:
+    for copy in copies[:3]:
         copy.wait()
     place = place_of(near[...], ghosts[0, 0]).astype(F32)
     place = jnp.concatenate(
@@ -92,6 +92,7 @@
         piece = jnp.concatenate([place[n : n + 1], jnp.zeros((1, TILE - TD), F32)], axis=1)
         row = jnp.where((lane >= first) & (lane < first + TD), pltpu.roll(piece, first, 1), row)
     out[pl.ds(moved_group(grp[0], m) * ROWS + 16, 1), :] = row
+    copies[3].wait()
     for t in range(TD):
         s = slot[t]
         g = moved_group(s // (TD * 8), m)

time: 90.5 us -> 90.4 us (level)
  no operation moved by 1% of the time
where the time goes in v7:
time: 90.4 us; the launch traced here: 90 us
  starting transfers between devices  31.2 us (35%)
  Pallas kernels  25.7 us (28%)
  blocking collectives  23.8 us (26%)
  waiting for transfers between devices  7.87 us (9%)
  between operations  0.92 us (1%)
    ppermute x14, starting transfers between devices, swap(): got.append(lax.ppermute(value, AXES, pairs + [(b, a) for a, b in pairs]))  29.2 us
    pallas_call x17, Pallas kernels, call(): pl.pallas_call(body, out_shape=[jax.ShapeDtypeStruct(shape, dtype) for sh...  24.5 us
    all_to_all x1, blocking collectives, local(): lax.all_to_all(outgoing.reshape(GROUPS * ROWS, 1, TILE), 'group', split_a...  23.8 us
    ppermute x14, waiting for transfers between devices, swap(): got.append(lax.ppermute(value, AXES, pairs + [(b, a) for a, b in pairs]))  4.16 us
    ppermute x1, waiting for transfers between devices, local(): done = lax.ppermute(done, AXES, [(owner(s), s) for s in range(GROUPS * 8)])  3.7 us
    ppermute x1, starting transfers between devices, local(): done = lax.ppermute(done, AXES, [(owner(s), s) for s in range(GROUPS * 8)])  1.92 us
  transfers between devices with their start and end apart: 15, of which 6 were waited for; matrix products, arithmetic and copies ran while one was open for 0% of the time, Pallas kernels for 15%

profile of v7, /device:TPU:24, one launch (start us, length us, event | category | flops | bytes accessed | tf_op | source)
XLA Modules:
  0.0 90.0 jit_solution(15183590649326394417)
XLA Ops:
  0.6 1.2 %pack.1 = f32[544,128]{1,0:T(8,128)S(1)} custom-call(s32[1]{0:T(128)} %bitcast.1.grp, s32[1]{0:T(128)} %bitcast.mem.refs_0_, s32[1,2]{1,0:T(1,128)} %ghosts_hbm.1, s32[16]{0:T(128)} %slot_hbm.1, s32[6,16]{1,0:T(8,128)} %bitcast.13, f32[8,2048]{1,0:T(8,128)} %part_hbm.1), custom_call_target="tpu_custom_call" | custom-call | tf_op jit(solution)/shard_map/pack/pallas_call | solution.py:416
  1.9 23.8 %all_to_all.5 = f32[544,1,128]{2,1,0:T(1,128)S(1)} all-to-all(f32[544,1,128]{2,1,0:T(1,128)S(1)} %bitcast.12), channel_id=1, replica_groups=mesh['group'=32,'member'=8] {'group'}, dimensions={0} | all-to-all | bytes 557056 | tf_op jit(solution)/shard_map/all_to_all | solution.py:446
  26.0 2.6 %collective-permute-start.1 = (f32[6,4,128]{2,1,0:T(4,128)S(1)}, f32[6,4,128]{2,1,0:T(4,128)S(1)}, u32[]{:S(2)}, u32[]{:S(2)}) collective-permute-start(f32[6,4,128]{2,1,0:T(4,128)S(1)} %get-tuple-element.51), channel_id=1, source_target_pairs={{1,2},{3,4},{13,14},{15,8},{9,10},{11,12},{21,22},{23,16},{17,18},... | collective-permute-start | bytes 36872 | tf_op jit(solution)/shard_map/ppermute | solution.py:409
  28.7 1.6 %columns.1.held = f32[5,24,128,128]{3,2,1,0:T(8,128)S(1)} custom-call(f32[8,16,128]{2,1,0:T(8,128)S(1)} %get-tuple-element.49.arranged.refs_1_.refs_2_), custom_call_target="tpu_custom_call" | custom-call | tf_op jit(solution)/shard_map/columns/pallas_call | solution.py:36
  31.0 3.2 %density_edge.1 = (f32[8,128]{1,0:T(8,128)S(1)}, f32[6,24,128]{2,1,0:T(8,128)S(1)}, f32[8,768,128]{2,1,0:T(8,128)S(1)}, f32[4,128]{1,0:T(4,128)S(1)}, f32[4,128]...) custom-call(s32[1]{0:T(128)} %bitcast.mem.refs_0_, ...), custom_call_target="tpu_custom_call", output_to_operand_aliasing={{5}: (5, {})} | custom-call | tf_op jit(solution)/shard_map/density_edge/pallas_call | solution.py:36
  34.2 3.0 %collective-permute-start.2 = (f32[4,128]{1,0:T(4,128)S(1)}, f32[4,128]{1,0:T(4,128)S(1)}, u32[]{:S(2)}, u32[]{:S(2)}) collective-permute-start(f32[4,128]{1,0:T(4,128)S(1)} %get-tuple-element.57), channel_id=1, source_target_pairs={{0,1},{2,3},{4,13},{14,15},{8,9},{10,11},{12,21},{22,23},{16,17},{... | collective-permute-start | bytes 6152 | tf_op jit(solution)/shard_map/ppermute | solution.py:409
  37.2 1.9 %collective-permute-start.3 = (f32[4,128]{1,0:T(4,128)S(1)}, f32[4,128]{1,0:T(4,128)S(1)}, u32[]{:S(2)}, u32[]{:S(2)}) collective-permute-start(f32[4,128]{1,0:T(4,128)S(1)} %get-tuple-element.58), channel_id=1, source_target_pairs={{1,2},{3,4},{13,14},{15,8},{9,10},{11,12},{21,22},{23,16},{17,18},... | collective-permute-start | bytes 6152 | tf_op jit(solution)/shard_map/ppermute | solution.py:409
  39.1 2.8 %density_inner.1 = (f32[8,128]{1,0:T(8,128)S(1)}, f32[8,768,128]{2,1,0:T(8,128)S(1)}) custom-call(s32[1,128]{1,0:T(1,128)S(1)} %get-tuple-element.48.table.refs_0_.refs_1_, f32[8,16,128]{2,1,0:T(8,128)S(1)} %get-tuple-element.49.arranged.refs_1_.refs_2_, f32[5,24,128,128]{3,2,1,0:T(8,128)S(1)} %get-tuple-element.53.refs_2_.cols), custom_call_target="tpu_custom_call" | custom-call | tf_op jit(solution)/shard_map/density_inner/pallas_call | solution.py:36
  41.9 1.9 %forces_edge.1.refs_4_ = bf16[8,2,768,128]{3,2,1,0:T(8,128)(2,1)S(1)} custom-call(s32[1,128]{1,0:T(1,128)S(1)} %get-tuple-element.48.table.refs_0_.refs_1_, f32[8,16,128]{2,1,0:T(8,128)S(1)} %get-tuple-element.49.arranged.refs_1_.refs_2_, f32[5,24,128,128]{3,2,1,0:T(8,128)S(1)} %get-tuple-element.53.refs_2_.cols, f32[8,768,128]{2,1,0:T(8,128)S(1)} %get-tuple-element.54.refs_3_), custom_call_target="tpu_custom_call" | custom-call | tf_op jit(solution)/shard_map/forces_edge/pallas_call | solution.py:36
  43.8 1.3 %limiter_first_edge.1 = (f32[8,128]{1,0:T(8,128)S(1)}, f32[4,128]{1,0:T(4,128)S(1)}, f32[4,128]{1,0:T(4,128)S(1)}, f32[2,8,128]{2,1,0:T(8,128)S(1)}, bf16[24,24,...) custom-call(s32[1]{0:T(128)} %bitcast.mem.refs_0_, ...), custom_call_target="tpu_custom_call" | custom-call | tf_op jit(solution)/shard_map/limiter_first_edge/pallas_call | solution.py:36
  45.5 3.3 %collective-permute-start.5 = (f32[4,128]{1,0:T(4,128)S(1)}, f32[4,128]{1,0:T(4,128)S(1)}, u32[]{:S(2)}, u32[]{:S(2)}) collective-permute-start(f32[4,128]{1,0:T(4,128)S(1)} %get-tuple-element.68), channel_id=1, source_target_pairs={{1,2},{3,4},{13,14},{15,8},{9,10},{11,12},{21,22},{23,16},{17,18},... | collective-permute-start | bytes 6152 | tf_op jit(solution)/shard_map/ppermute | solution.py:409
  48.8 1.9 %forces_inner.1.refs_3_.forces.refs_13_ = bf16[8,2,768,128]{3,2,1,0:T(8,128)(2,1)S(1)} custom-call(s32[1,128]{1,0:T(1,128)S(1)} %get-tuple-element.48.table.refs_0_.refs_1_, f32[8,16,128]{2,1,0:T(8,128)S(1)} %get-tuple-element.49.arranged.refs_1_.refs_2_, f32[5,24,128,128]{3,2,1,0:T(8,128)S(1)} %get-tuple-element.53.refs_2_.cols, ...), custom_call_target="tpu_custom_call" | custom-call | tf_op jit(solution)/shard_map/forces_inner/pallas_call | solution.py:36
  50.7 1.2 %limiter_first_inner.1 = (f32[8,128]{1,0:T(8,128)S(1)}, f32[2,8,128]{2,1,0:T(8,128)S(1)}, f32[4,8,128]{2,1,0:T(8,128)S(1)}) custom-call(s32[1,128]{1,0:T(1,128)S(1)} %get-tuple-element.48.table.refs_0_.refs_1_, f32[8,16,128]{2,1,0:T(8,128)S(1)} %get-tuple-element.49.arranged.refs_1_.refs_2_, ...), custom_call_target="tpu_custom_call" | custom-call | tf_op jit(solution)/shard_map/limiter_first_inner/pallas_call | solution.py:36
  52.0 1.1 %jacobi_edge.2 = (f32[8,128]{1,0:T(8,128)S(1)}, f32[4,128]{1,0:T(4,128)S(1)}, f32[4,128]{1,0:T(4,128)S(1)}, bf16[24,8,128]{2,1,0:T(8,128)(2,1)S(1)}) custom-call(s32[1]{0:T(128)} %bitcast.mem.refs_0_, s32[1,128]{1,0:T(1,128)S(1)} %get-tuple-element.48.table.refs_0_.refs_1_, f32[8,16,128]{2,1,0:T(8,128)S(1)} %get-tuple-element.49.arranged.refs_1_.refs_2_, ...), custom_call_target="tpu_custom_call" | custom-call | tf_op jit(solution)/shard_map/jacobi_edge/pallas_call | solution.py:36
  53.1 1.3 %collective-permute-start.6 = (f32[4,128]{1,0:T(4,128)S(1)}, f32[4,128]{1,0:T(4,128)S(1)}, u32[]{:S(2)}, u32[]{:S(2)}) collective-permute-start(f32[4,128]{1,0:T(4,128)S(1)} %get-tuple-element.71), channel_id=1, source_target_pairs={{0,1},{2,3},{4,13},{14,15},{8,9},{10,11},{12,21},{22,23},{16,17},{... | collective-permute-start | bytes 6152 | tf_op jit(solution)/shard_map/ppermute | solution.py:409
  54.4 3.6 %collective-permute-start.7 = (f32[4,128]{1,0:T(4,128)S(1)}, f32[4,128]{1,0:T(4,128)S(1)}, u32[]{:S(2)}, u32[]{:S(2)}) collective-permute-start(f32[4,128]{1,0:T(4,128)S(1)} %get-tuple-element.72), channel_id=1, source_target_pairs={{1,2},{3,4},{13,14},{15,8},{9,10},{11,12},{21,22},{23,16},{17,18},... | collective-permute-start | bytes 6152 | tf_op jit(solution)/shard_map/ppermute | solution.py:409
  58.0 1.1 %jacobi_inner.2.refs_7_ = f32[8,128]{1,0:T(8,128)S(1)} custom-call(s32[1,128]{1,0:T(1,128)S(1)} %get-tuple-element.48.table.refs_0_.refs_1_, f32[8,16,128]{2,1,0:T(8,128)S(1)} %get-tuple-element.49.arranged.refs_1_.refs_2_, bf16[8,2,768,128]{3,2,1,0:T(8,128)(2,1)S(1)} %forces_inner.1.refs_3_.forces.refs_13_, ...), custom_call_target="tpu_custom_call" | custom-call | tf_op jit(solution)/shard_map/jacobi_inner/pallas_call | solution.py:36
  59.3 1.1 %limiter_edge.2 = (f32[8,128]{1,0:T(8,128)S(1)}, f32[4,128]{1,0:T(4,128)S(1)}, f32[4,128]{1,0:T(4,128)S(1)}, f32[2,8,128]{2,1,0:T(8,128)S(1)}, bf16[24,16,128]{2,1,0:T(8,128)(2,1)S(1)}, /*index=5*/f32[24,128]{1,0:T(8,128)S(1)}) custom-call(s32[1]{0:T(128)} %bitcast.mem.refs_0_, s32[1,128]{1,0:T(1,128)S(1)} %get-tuple-element.48.table.refs_0_.refs_1_, ...), custom_call_target="tpu_custom_call" | custom-call | tf_op jit(solution)/shard_map/limiter_edge/pallas_call | solution.py:36
  60.4 1.8 %collective-permute-start.8 = (f32[4,128]{1,0:T(4,128)S(1)}, f32[4,128]{1,0:T(4,128)S(1)}, u32[]{:S(2)}, u32[]{:S(2)}) collective-permute-start(f32[4,128]{1,0:T(4,128)S(1)} %get-tuple-element.80), channel_id=1, source_target_pairs={{0,1},{2,3},{4,13},{14,15},{8,9},{10,11},{12,21},{22,23},{16,17},{... | collective-permute-start | bytes 6152 | tf_op jit(solution)/shard_map/ppermute | solution.py:409
  62.2 2.2 %collective-permute-start.9 = (f32[4,128]{1,0:T(4,128)S(1)}, f32[4,128]{1,0:T(4,128)S(1)}, u32[]{:S(2)}, u32[]{:S(2)}) collective-permute-start(f32[4,128]{1,0:T(4,128)S(1)} %get-tuple-element.81), channel_id=1, source_target_pairs={{1,2},{3,4},{13,14},{15,8},{9,10},{11,12},{21,22},{23,16},{17,18},... | collective-permute-start | bytes 6152 | tf_op jit(solution)/shard_map/ppermute | solution.py:409
  64.5 1.1 %limiter_inner.2 = (f32[8,128]{1,0:T(8,128)S(1)}, f32[2,8,128]{2,1,0:T(8,128)S(1)}) custom-call(s32[1,128]{1,0:T(1,128)S(1)} %get-tuple-element.48.table.refs_0_.refs_1_, f32[8,16,128]{2,1,0:T(8,128)S(1)} %get-tuple-element.49.arranged.refs_1_.refs_2_, f32[6,24,128]{2,1,0:T(8,128)S(1)} %get-tuple-element.52.refs_3_.refs_2_.refs_5_.refs_6_, ...), custom_call_target="tpu_custom_call" | custom-call | tf_op jit(solution)/shard_map/limiter_inner/pallas_call | solution.py:36
  65.6 1.5 %collective-permute-done.9.refs_12_ = f32[4,128]{1,0:T(4,128)S(1)} collective-permute-done((f32[4,128]{1,0:T(4,128)S(1)}, f32[4,128]{1,0:T(4,128)S(1)}, u32[]{:S(2)}, u32[]{:S(2)}) %collective-permute-start.9) | collective-permute-done | bytes 2080 | tf_op jit(solution)/shard_map/ppermute | solution.py:409
  68.2 1.3 %collective-permute-start.10 = (f32[4,128]{1,0:T(4,128)S(1)}, f32[4,128]{1,0:T(4,128)S(1)}, u32[]{:S(2)}, u32[]{:S(2)}) collective-permute-start(f32[4,128]{1,0:T(4,128)S(1)} %get-tuple-element.84), channel_id=1, source_target_pairs={{0,1},{2,3},{4,13},{14,15},{8,9},{10,11},{12,21},{22,23},{16,17},{... | collective-permute-start | bytes 6152 | tf_op jit(solution)/shard_map/ppermute | solution.py:409
  69.6 3.6 %collective-permute-start.11 = (f32[4,128]{1,0:T(4,128)S(1)}, f32[4,128]{1,0:T(4,128)S(1)}, u32[]{:S(2)}, u32[]{:S(2)}) collective-permute-start(f32[4,128]{1,0:T(4,128)S(1)} %get-tuple-element.85), channel_id=1, source_target_pairs={{1,2},{3,4},{13,14},{15,8},{9,10},{11,12},{21,22},{23,16},{17,18},... | collective-permute-start | bytes 6152 | tf_op jit(solution)/shard_map/ppermute | solution.py:409
  74.5 1.1 %limiter_edge.3 = (f32[8,128]{1,0:T(8,128)S(1)}, f32[4,128]{1,0:T(4,128)S(1)}, f32[4,128]{1,0:T(4,128)S(1)}, f32[2,8,128]{2,1,0:T(8,128)S(1)}, bf16[24,16,128]{2,1,0:T(8,128)(2,1)S(1)}, /*index=5*/f32[24,128]{1,0:T(8,128)S(1)}) custom-call(s32[1]{0:T(128)} %bitcast.mem.refs_0_, s32[1,128]{1,0:T(1,128)S(1)} %get-tuple-element.48.table.refs_0_.refs_1_, ...), custom_call_target="tpu_custom_call" | custom-call | tf_op jit(solution)/shard_map/limiter_edge/pallas_call | solution.py:36
  75.6 1.8 %collective-permute-start.12 = (f32[4,128]{1,0:T(4,128)S(1)}, f32[4,128]{1,0:T(4,128)S(1)}, u32[]{:S(2)}, u32[]{:S(2)}) collective-permute-start(f32[4,128]{1,0:T(4,128)S(1)} %get-tuple-element.92), channel_id=1, source_target_pairs={{0,1},{2,3},{4,13},{14,15},{8,9},{10,11},{12,21},{22,23},{16,17},{... | collective-permute-start | bytes 6152 | tf_op jit(solution)/shard_map/ppermute | solution.py:409
  77.4 2.2 %collective-permute-start.13 = (f32[4,128]{1,0:T(4,128)S(1)}, f32[4,128]{1,0:T(4,128)S(1)}, u32[]{:S(2)}, u32[]{:S(2)}) collective-permute-start(f32[4,128]{1,0:T(4,128)S(1)} %get-tuple-element.93), channel_id=1, source_target_pairs={{1,2},{3,4},{13,14},{15,8},{9,10},{11,12},{21,22},{23,16},{17,18},... | collective-permute-start | bytes 6152 | tf_op jit(solution)/shard_map/ppermute | solution.py:409
  79.6 1.1 %limiter_inner.3 = (f32[8,128]{1,0:T(8,128)S(1)}, f32[2,8,128]{2,1,0:T(8,128)S(1)}) custom-call(s32[1,128]{1,0:T(1,128)S(1)} %get-tuple-element.48.table.refs_0_.refs_1_, f32[8,16,128]{2,1,0:T(8,128)S(1)} %get-tuple-element.49.arranged.refs_1_.refs_2_, f32[6,24,128]{2,1,0:T(8,128)S(1)} %get-tuple-element.52.refs_3_.refs_2_.refs_5_.refs_6_, ...), custom_call_target="tpu_custom_call" | custom-call | tf_op jit(solution)/shard_map/limiter_inner/pallas_call | solution.py:36
  80.7 1.5 %collective-permute-done.13.refs_12_ = f32[4,128]{1,0:T(4,128)S(1)} collective-permute-done((f32[4,128]{1,0:T(4,128)S(1)}, f32[4,128]{1,0:T(4,128)S(1)}, u32[]{:S(2)}, u32[]{:S(2)}) %collective-permute-start.13) | collective-permute-done | bytes 2080 | tf_op jit(solution)/shard_map/ppermute | solution.py:409
  82.3 1.5 %jacobi_last.1 = f32[32,128]{1,0:T(8,128)S(1)} custom-call(s32[1]{0:T(128)} %bitcast.mem.refs_0_, s32[1,128]{1,0:T(1,128)S(1)} %get-tuple-element.48.table.refs_0_.refs_1_, f32[8,16,128]{2,1,0:T(8,128)S(1)} %get-tuple-element.49.arranged.refs_1_.refs_2_, f32[6,24,128]{2,1,0:T(8,128)S(1)} %get-tuple-element.52.refs_3_.refs_2_.refs_5_.refs_6_, ...), custom_call_target="tpu_custom_call" | custom-call | tf_op jit(solution)/shard_map/jacobi_last/pallas_call | solution.py:36
  83.8 1.9 %collective-permute-start.14 = (f32[32,128]{1,0:T(8,128)S(1)}, f32[32,128]{1,0:T(8,128)S(1)}, u32[]{:S(2)}, u32[]{:S(2)}) collective-permute-start(f32[32,128]{1,0:T(8,128)S(1)} %jacobi_last.1), channel_id=1, source_target_pairs={{0,0},{1,1},{2,2},{3,3},{4,4},{13,5},{14,6},{15,7},{8,8},{9,9},{10... | collective-permute-start | bytes 49160 | tf_op jit(solution)/shard_map/ppermute | solution.py:599
  85.7 3.7 %collective-permute-done.14 = f32[32,128]{1,0:T(8,128)S(1)} collective-permute-done((f32[32,128]{1,0:T(8,128)S(1)}, f32[32,128]{1,0:T(8,128)S(1)}, u32[]{:S(2)}, u32[]{:S(2)}) %collective-permute-start.14) | collective-permute-done | bytes 16416 | tf_op jit(solution)/shard_map/ppermute | solution.py:599
  (18 shorter events, 4.7 us)
Async XLA Ops:
  26.0 4.3 %collective-permute-start = (f32[6,4,128]{2,1,0:T(4,128)S(1)}, f32[6,4,128]{2,1,0:T(4,128)S(1)}, u32[]{:S(2)}, u32[]{:S(2)}) collective-permute-start(f32[6,4,128]{2,1,0:T(4,128)S(1)} %get-tuple-element.50), channel_id=1, source_target_pairs={{0,1},{2,3},{4,13},{14,15},{8,9},{10,11},{12,21},{22,23},{16,17},{... | collective-permute-start | bytes 36872 | tf_op jit(solution)/shard_map/ppermute | solution.py:409
  26.0 5.0 %collective-permute-start.1 = (f32[6,4,128]{2,1,0:T(4,128)S(1)}, f32[6,4,128]{2,1,0:T(4,128)S(1)}, u32[]{:S(2)}, u32[]{:S(2)}) collective-permute-start(f32[6,4,128]{2,1,0:T(4,128)S(1)} %get-tuple-element.51), channel_id=1, source_target_pairs={{1,2},{3,4},{13,14},{15,8},{9,10},{11,12},{21,22},{23,16},{17,18},... | collective-permute-start | bytes 36872 | tf_op jit(solution)/shard_map/ppermute | solution.py:409
  34.2 9.6 %collective-permute-start.2 = (f32[4,128]{1,0:T(4,128)S(1)}, f32[4,128]{1,0:T(4,128)S(1)}, u32[]{:S(2)}, u32[]{:S(2)}) collective-permute-start(f32[4,128]{1,0:T(4,128)S(1)} %get-tuple-element.57), channel_id=1, source_target_pairs={{0,1},{2,3},{4,13},{14,15},{8,9},{10,11},{12,21},{22,23},{16,17},{... | collective-permute-start | bytes 6152 | tf_op jit(solution)/shard_map/ppermute | solution.py:409
  37.2 6.6 %collective-permute-start.3 = (f32[4,128]{1,0:T(4,128)S(1)}, f32[4,128]{1,0:T(4,128)S(1)}, u32[]{:S(2)}, u32[]{:S(2)}) collective-permute-start(f32[4,128]{1,0:T(4,128)S(1)} %get-tuple-element.58), channel_id=1, source_target_pairs={{1,2},{3,4},{13,14},{15,8},{9,10},{11,12},{21,22},{23,16},{17,18},... | collective-permute-start | bytes 6152 | tf_op jit(solution)/shard_map/ppermute | solution.py:409
  45.1 6.9 %collective-permute-start.4 = (f32[4,128]{1,0:T(4,128)S(1)}, f32[4,128]{1,0:T(4,128)S(1)}, u32[]{:S(2)}, u32[]{:S(2)}) collective-permute-start(f32[4,128]{1,0:T(4,128)S(1)} %get-tuple-element.67), channel_id=1, source_target_pairs={{0,1},{2,3},{4,13},{14,15},{8,9},{10,11},{12,21},{22,23},{16,17},{... | collective-permute-start | bytes 6152 | tf_op jit(solution)/shard_map/ppermute | solution.py:409
  45.5 6.5 %collective-permute-start.5 = (f32[4,128]{1,0:T(4,128)S(1)}, f32[4,128]{1,0:T(4,128)S(1)}, u32[]{:S(2)}, u32[]{:S(2)}) collective-permute-start(f32[4,128]{1,0:T(4,128)S(1)} %get-tuple-element.68), channel_id=1, source_target_pairs={{1,2},{3,4},{13,14},{15,8},{9,10},{11,12},{21,22},{23,16},{17,18},... | collective-permute-start | bytes 6152 | tf_op jit(solution)/shard_map/ppermute | solution.py:409
  53.1 6.0 %collective-permute-start.6 = (f32[4,128]{1,0:T(4,128)S(1)}, f32[4,128]{1,0:T(4,128)S(1)}, u32[]{:S(2)}, u32[]{:S(2)}) collective-permute-start(f32[4,128]{1,0:T(4,128)S(1)} %get-tuple-element.71), channel_id=1, source_target_pairs={{0,1},{2,3},{4,13},{14,15},{8,9},{10,11},{12,21},{22,23},{16,17},{... | collective-permute-start | bytes 6152 | tf_op jit(solution)/shard_map/ppermute | solution.py:409
  54.4 4.9 %collective-permute-start.7 = (f32[4,128]{1,0:T(4,128)S(1)}, f32[4,128]{1,0:T(4,128)S(1)}, u32[]{:S(2)}, u32[]{:S(2)}) collective-permute-start(f32[4,128]{1,0:T(4,128)S(1)} %get-tuple-element.72), channel_id=1, source_target_pairs={{1,2},{3,4},{13,14},{15,8},{9,10},{11,12},{21,22},{23,16},{17,18},... | collective-permute-start | bytes 6152 | tf_op jit(solution)/shard_map/ppermute | solution.py:409
  60.4 5.2 %collective-permute-start.8 = (f32[4,128]{1,0:T(4,128)S(1)}, f32[4,128]{1,0:T(4,128)S(1)}, u32[]{:S(2)}, u32[]{:S(2)}) collective-permute-start(f32[4,128]{1,0:T(4,128)S(1)} %get-tuple-element.80), channel_id=1, source_target_pairs={{0,1},{2,3},{4,13},{14,15},{8,9},{10,11},{12,21},{22,23},{16,17},{... | collective-permute-start | bytes 6152 | tf_op jit(solution)/shard_map/ppermute | solution.py:409
  62.2 4.9 %collective-permute-start.9 = (f32[4,128]{1,0:T(4,128)S(1)}, f32[4,128]{1,0:T(4,128)S(1)}, u32[]{:S(2)}, u32[]{:S(2)}) collective-permute-start(f32[4,128]{1,0:T(4,128)S(1)} %get-tuple-element.81), channel_id=1, source_target_pairs={{1,2},{3,4},{13,14},{15,8},{9,10},{11,12},{21,22},{23,16},{17,18},... | collective-permute-start | bytes 6152 | tf_op jit(solution)/shard_map/ppermute | solution.py:409
  68.2 6.0 %collective-permute-start.10 = (f32[4,128]{1,0:T(4,128)S(1)}, f32[4,128]{1,0:T(4,128)S(1)}, u32[]{:S(2)}, u32[]{:S(2)}) collective-permute-start(f32[4,128]{1,0:T(4,128)S(1)} %get-tuple-element.84), channel_id=1, source_target_pairs={{0,1},{2,3},{4,13},{14,15},{8,9},{10,11},{12,21},{22,23},{16,17},{... | collective-permute-start | bytes 6152 | tf_op jit(solution)/shard_map/ppermute | solution.py:409
  69.6 4.9 %collective-permute-start.11 = (f32[4,128]{1,0:T(4,128)S(1)}, f32[4,128]{1,0:T(4,128)S(1)}, u32[]{:S(2)}, u32[]{:S(2)}) collective-permute-start(f32[4,128]{1,0:T(4,128)S(1)} %get-tuple-element.85), channel_id=1, source_target_pairs={{1,2},{3,4},{13,14},{15,8},{9,10},{11,12},{21,22},{23,16},{17,18},... | collective-permute-start | bytes 6152 | tf_op jit(solution)/shard_map/ppermute | solution.py:409
  75.6 5.2 %collective-permute-start.12 = (f32[4,128]{1,0:T(4,128)S(1)}, f32[4,128]{1,0:T(4,128)S(1)}, u32[]{:S(2)}, u32[]{:S(2)}) collective-permute-start(f32[4,128]{1,0:T(4,128)S(1)} %get-tuple-element.92), channel_id=1, source_target_pairs={{0,1},{2,3},{4,13},{14,15},{8,9},{10,11},{12,21},{22,23},{16,17},{... | collective-permute-start | bytes 6152 | tf_op jit(solution)/shard_map/ppermute | solution.py:409
  77.4 4.9 %collective-permute-start.13 = (f32[4,128]{1,0:T(4,128)S(1)}, f32[4,128]{1,0:T(4,128)S(1)}, u32[]{:S(2)}, u32[]{:S(2)}) collective-permute-start(f32[4,128]{1,0:T(4,128)S(1)} %get-tuple-element.93), channel_id=1, source_target_pairs={{1,2},{3,4},{13,14},{15,8},{9,10},{11,12},{21,22},{23,16},{17,18},... | collective-permute-start | bytes 6152 | tf_op jit(solution)/shard_map/ppermute | solution.py:409
  83.8 5.6 %collective-permute-start.14 = (f32[32,128]{1,0:T(8,128)S(1)}, f32[32,128]{1,0:T(8,128)S(1)}, u32[]{:S(2)}, u32[]{:S(2)}) collective-permute-start(f32[32,128]{1,0:T(8,128)S(1)} %jacobi_last.1), channel_id=1, source_target_pairs={{0,0},{1,1},{2,2},{3,3},{4,4},{13,5},{14,6},{15,7},{8,8},{9,9},{10... | collective-permute-start | bytes 49160 | tf_op jit(solution)/shard_map/ppermute | solution.py:599
